TPU v7x, 128 devices: a whole 4x4x4 slice. The times are simulated.
128 devices in a mesh: part: 1, loc: 2 (over core), grp: 64 (over z, y, x).
Axes of the slice: x: 4, y: 4, z: 4, core: 2. Of those that a mesh axis runs over, the one named last changes fastest.
Arguments:
- x_rows: bfloat16 [98304, 1024], P(('part', 'grp', 'loc'))
- dy_rows: bfloat16 [98304, 1024], P(('part', 'grp', 'loc'))
- expert_ids: int32 [98304, 8], P(('part', 'grp', 'loc'))
- gate_vals: float32 [98304, 8], P(('part', 'grp', 'loc'))
- w_gate: bfloat16 [128, 1024, 384], P(('part', 'grp', 'loc'))
- w_up: bfloat16 [128, 1024, 384], P(('part', 'grp', 'loc'))
- w_down: bfloat16 [128, 384, 1024], P(('part', 'grp', 'loc'))
Outputs:
- output 1: bfloat16 [98304, 1024], P(('part', 'grp', 'loc'))
- output 2: float32 [98304, 8], P(('part', 'grp', 'loc'))
- output 3: bfloat16 [128, 1024, 384], P(('part', 'grp', 'loc'))
- output 4: bfloat16 [128, 1024, 384], P(('part', 'grp', 'loc'))
- output 5: bfloat16 [128, 384, 1024], P(('part', 'grp', 'loc'))
All inputs are finite; a program needn't handle non-finite values.
Results may differ from a plain program's by a relative error of at most 0.001.
Values are sent between devices in bfloat16 or wider.
A program may use at most 1 GiB of HBM per device.

v0:
```python
import jax
import jax.numpy as jnp
from jax import lax
from jax.sharding import PartitionSpec as P


def slot_table(bin_ids, num_bins, capacity):
    n_items = bin_ids.shape[0]
    item_order = jnp.argsort(bin_ids, stable=True)
    sorted_bins = bin_ids[item_order]
    bin_sizes = jax.ops.segment_sum(jnp.ones_like(bin_ids), bin_ids, num_segments=num_bins + 1)
    bin_starts = jnp.cumsum(bin_sizes) - bin_sizes
    slot_rank = jnp.arange(n_items, dtype=jnp.int32) - bin_starts[sorted_bins]
    dest_slot = jnp.where(sorted_bins < num_bins, sorted_bins * capacity + slot_rank, num_bins * capacity)
    slot_grid = jnp.full((num_bins * capacity + 1,), n_items, jnp.int32).at[dest_slot].set(item_order.astype(jnp.int32))
    return slot_grid[:num_bins * capacity].reshape(num_bins, capacity)


def gather_rows(source, row_index, fill_val):
    return jnp.take(source, row_index, axis=0, mode='fill', fill_value=fill_val)


def first_in_group(dest_group):
    top_k = dest_group.shape[-1]
    same_group = dest_group[..., :, None] == dest_group[..., None, :]
    earlier = jnp.arange(top_k)[None, :] < jnp.arange(top_k)[:, None]
    return same_group, jnp.logical_not(jnp.any(same_group & earlier, axis=-1))


def expert_backward(x_own, dy_own, gate_own, w_gate, w_up, w_down, row_axes, wt_axes):
    up_form = row_axes + 'd,' + wt_axes + 'df->' + row_axes + 'f'
    down_form = row_axes + 'f,' + wt_axes + 'fd->' + row_axes + 'd'
    back_form = row_axes + 'd,' + wt_axes + 'fd->' + row_axes + 'f'
    tr_form = row_axes + 'f,' + wt_axes + 'df->' + row_axes + 'd'
    grad_down = row_axes + 'f,' + row_axes + 'd->' + wt_axes + 'fd'
    grad_up = row_axes + 'd,' + row_axes + 'f->' + wt_axes + 'df'
    pre_gate = jnp.einsum(up_form, x_own, w_gate, preferred_element_type=jnp.float32)
    pre_up = jnp.einsum(up_form, x_own, w_up, preferred_element_type=jnp.float32)
    sig_gate = jax.nn.sigmoid(pre_gate)
    silu_out = pre_gate * sig_gate
    hidden = (silu_out * pre_up).astype(jnp.bfloat16)
    expert_out = jnp.einsum(down_form, hidden, w_down, preferred_element_type=jnp.float32)
    d_gate = jnp.sum(dy_own * expert_out, axis=-1)
    d_out = (gate_own[..., None] * dy_own).astype(jnp.bfloat16)
    d_hidden = jnp.einsum(back_form, d_out, w_down, preferred_element_type=jnp.float32)
    dw_down = jnp.einsum(grad_down, hidden, d_out, preferred_element_type=jnp.float32).astype(jnp.bfloat16)
    d_pre_up = (d_hidden * silu_out).astype(jnp.bfloat16)
    d_pre_gate = (d_hidden * pre_up * sig_gate * (1.0 + pre_gate * (1.0 - sig_gate))).astype(jnp.bfloat16)
    dw_gate = jnp.einsum(grad_up, x_own, d_pre_gate, preferred_element_type=jnp.float32).astype(jnp.bfloat16)
    dw_up = jnp.einsum(grad_up, x_own, d_pre_up, preferred_element_type=jnp.float32).astype(jnp.bfloat16)
    d_x = (jnp.einsum(tr_form, d_pre_gate, w_gate, preferred_element_type=jnp.float32) + jnp.einsum(tr_form, d_pre_up, w_up, preferred_element_type=jnp.float32)).astype(jnp.bfloat16)
    return d_x, d_gate, dw_gate, dw_up, dw_down


def solution(mesh):
    grp_size = mesh.shape['grp']
    loc_size = mesh.shape['loc']
    spec = P(('part', 'grp', 'loc'))

    def device_step(x_rows, dy_rows, expert_ids, gate_vals, w_gate, w_up, w_down):
        n_tok, d_model = x_rows.shape
        top_k = expert_ids.shape[1]
        local_experts = w_gate.shape[0]
        group_experts = local_experts * loc_size
        num_experts = group_experts * grp_size
        group_limit = min(top_k // 2, grp_size)
        group_rows = group_limit * n_tok // grp_size
        src_cap = min(2 * (n_tok * top_k // num_experts), group_rows)
        relay_cap = grp_size * src_cap
        rows_in = grp_size * group_rows
        my_group = lax.axis_index('grp')

        dest_group = expert_ids // group_experts
        same_group, first_slot = first_in_group(dest_group)
        send_items = slot_table(jnp.where(first_slot, dest_group, grp_size).reshape(-1), grp_size, group_rows)
        send_tok = send_items // top_k
        x_recv = lax.all_to_all(gather_rows(x_rows, send_tok, 0), 'grp', 0, 0).reshape(rows_in, d_model)
        dy_recv = lax.all_to_all(gather_rows(dy_rows, send_tok, 0), 'grp', 0, 0).reshape(rows_in, d_model)
        ids_recv = lax.all_to_all(gather_rows(expert_ids, send_tok, -1), 'grp', 0, 0).reshape(rows_in, top_k)
        gate_recv = lax.all_to_all(gather_rows(gate_vals, send_tok, 0), 'grp', 0, 0).reshape(rows_in * top_k)

        local_ids = ids_recv - my_group * group_experts
        is_mine = (local_ids >= 0) & (local_ids < group_experts)
        fan_items = slot_table(jnp.where(is_mine, local_ids, group_experts).reshape(-1), group_experts, relay_cap)
        fan_rows = fan_items // top_k
        own_shape = (loc_size, local_experts, relay_cap)
        x_own = lax.all_to_all(gather_rows(x_recv, fan_rows, 0).reshape(own_shape + (d_model,)), 'loc', 0, 0)
        dy_own = lax.all_to_all(gather_rows(dy_recv, fan_rows, 0).reshape(own_shape + (d_model,)), 'loc', 0, 0)
        gate_own = lax.all_to_all(gather_rows(gate_recv, fan_items, 0).reshape(own_shape), 'loc', 0, 0)

        d_x, d_gate, dw_gate, dw_up, dw_down = expert_backward(x_own, dy_own, gate_own, w_gate, w_up, w_down, 'lec', 'e')

        contrib_back = lax.all_to_all(d_x, 'loc', 0, 0).reshape(group_experts * relay_cap, d_model)
        dgate_back = lax.all_to_all(d_gate, 'loc', 0, 0).reshape(-1)
        group_sum = jax.ops.segment_sum(contrib_back.astype(jnp.float32), fan_rows.reshape(-1), num_segments=rows_in + 1)
        group_part = group_sum[:rows_in].astype(jnp.bfloat16).reshape(grp_size, group_rows, d_model)
        dgate_rel = jax.ops.segment_sum(dgate_back, fan_items.reshape(-1), num_segments=rows_in * top_k + 1)
        dgate_rel = dgate_rel[:rows_in * top_k].reshape(grp_size, group_rows, top_k)
        part_home = lax.all_to_all(group_part, 'grp', 0, 0).reshape(rows_in, d_model)
        dgate_home = lax.all_to_all(dgate_rel, 'grp', 0, 0).reshape(rows_in, top_k)

        home_tok = send_tok.reshape(-1)
        dx_sum = jax.ops.segment_sum(part_home.astype(jnp.float32), home_tok, num_segments=n_tok + 1)
        d_gates = jax.ops.segment_sum(dgate_home, home_tok, num_segments=n_tok + 1)[:n_tok]
        return dx_sum[:n_tok].astype(jnp.bfloat16), d_gates, dw_gate, dw_up, dw_down

    return jax.shard_map(device_step, mesh=mesh, in_specs=(spec,) * 7, out_specs=(spec,) * 5, check_vma=False)
```

profile of v0, /device:TPU:0, one launch (start us, length us, event | category | flops | bytes accessed | tf_op | source)
XLA Modules:
  0.0 1362.4 jit_solution(2555030733698298018)
XLA Ops:
  9.6 34.3 %gather_fusion = s32[6144]{0:T(1024)S(1)} fusion(s32[6144]{0:T(1024)S(1)} %reshape.511, s32[6144]{0:T(1024)S(1)} %fusion.74), kind=kCustom, calls=%fused_computation.4 | custom fusion | bytes 73728 | tf_op jit(solution)/shard_map/gather | solution.py:10
  43.9 42.9 %scatter_custom_fusion = s32[65]{0:T(128)S(1)} fusion(s32[6144]{0:T(1024)S(1)} %reshape.511, s32[6144]{0:T(1024)S(1)} %broadcast.385, s32[]{:T(128)} %constant.80.clone.1), kind=kCustom, calls=%fused_computation.166 | custom fusion | flops 6144 | bytes 264 | tf_op jit(solution)/shard_map/scatter-add | solution.py:11
  87.1 36.8 %gather_fusion.1 = s32[6144]{0:T(1024)S(1)} fusion(s32[65]{0:T(128)S(1)} %sub.74, s32[6144]{0:T(1024)S(1)} %broadcast_clamp_fusion.2), kind=kCustom, calls=%fused_computation.5 | custom fusion | bytes 73728 | tf_op jit(solution)/shard_map/gather | solution.py:13
  124.0 23.0 %scatter_custom_fusion.1 = s32[3073]{0:T(1024)S(1)} fusion(s32[6144]{0:T(1024)S(1)} %bitcast.248, s32[6144]{0:T(1024)S(1)} %get-tuple-element.9, s32[]{:T(128)} %constant.72.clone.1), kind=kCustom, calls=%fused_computation.158 | custom fusion | bytes 12296 | tf_op jit(solution)/shard_map/scatter | solution.py:15
  158.9 11.8 all-to-all-start
  182.4 15.0 %gather_fusion.8 = bf16[3072,1024]{1,0:T(8,128)(2,1)} fusion(bf16[768,1024]{1,0:T(8,128)(2,1)S(1)} %copy-done, s32[3072]{0:T(1024)} %broadcast_clamp_fusion.3), kind=kCustom, calls=%fused_computation.2.clone | custom fusion | bytes 12595200 | tf_op jit(solution)/shard_map/jit(_take)/gather | solution.py:20
  197.4 13.9 %gather_fusion.6 = bf16[3072,1024]{1,0:T(8,128)(2,1)} fusion(bf16[768,1024]{1,0:T(8,128)(2,1)S(1)} %copy-done.2, s32[3072]{0:T(1024)S(1)} %copy-done.6), kind=kCustom, calls=%fused_computation.clone | custom fusion | bytes 12595200 | tf_op jit(solution)/shard_map/jit(_take)/gather | solution.py:20
  246.1 169.9 %scatter_custom_fusion.2 = s32[3]{0:T(128)S(1)} fusion(s32[24576]{0:T(1024)S(1)} %bitcast.238, s32[24576]{0:T(1024)S(1)} %broadcast.386, s32[]{:T(128)} %constant.80.clone.1), kind=kCustom, calls=%fused_computation.164 | custom fusion | flops 24576 | bytes 16 | tf_op jit(solution)/shard_map/scatter-add | solution.py:11
  428.1 135.7 %gather_fusion.3 = s32[24576]{0:T(1024)S(1)} fusion(s32[24576]{0:T(1024)S(1)} %and_select_fusion.2, s32[24576]{0:T(1024)S(1)} %fusion.65), kind=kCustom, calls=%fused_computation.7 | custom fusion | bytes 294912 | tf_op jit(solution)/shard_map/gather | solution.py:10
  566.1 90.2 %scatter_custom_fusion.3 = s32[6145]{0:T(1024)S(1)} fusion(s32[24576]{0:T(1024)S(1)} %bitcast.237, s32[24576]{0:T(1024)S(1)} %get-tuple-element.10, s32[]{:T(128)} %constant.99.clone.1), kind=kCustom, calls=%fused_computation.149 | custom fusion | bytes 24584 | tf_op jit(solution)/shard_map/scatter | solution.py:15
  657.1 34.3 %gather_fusion.5 = f32[6144]{0:T(1024)S(1)} fusion(f32[24576]{0:T(1024)S(1)} %reshape.519, s32[6144]{0:T(1024)S(1)} %broadcast_clamp_fusion.1), kind=kCustom, calls=%fused_computation.9 | custom fusion | bytes 73728 | tf_op jit(solution)/shard_map/jit(_take)/gather | solution.py:20
  695.2 90.1 %all_to_all.56 = bf16[64,48,1024]{2,1,0:T(8,128)(2,1)} all-to-all(bf16[64,48,1024]{2,1,0:T(8,128)(2,1)} %get-tuple-element.45), channel_id=1, replica_groups=mesh['part'=1,'loc'=2,'grp'=64] {'grp'}, dimensions={0} | all-to-all | bytes 12582912 | tf_op jit(solution)/shard_map/all_to_all | solution.py:77
  785.3 13.8 %all-to-all-start.3 = ((bf16[64,48,1024]{2,1,0:T(8,128)(2,1)}), bf16[64,48,1024]{2,1,0:T(8,128)(2,1)}, u32[]{:S(2)}, u32[]{:S(2)}) async-start(bf16[64,48,1024]{2,1,0:T(8,128)(2,1)} %get-tuple-element.44), calls=%async_computation.3 | async-start | bytes 12582912 | tf_op jit(solution)/shard_map/all_to_all | solution.py:78
  799.3 34.5 %gather_fusion.9 = bf16[6144,1024]{1,0:T(8,128)(2,1)} fusion(bf16[3072,1024]{1,0:T(8,128)(2,1)} %bitcast.217, s32[6144]{0:T(1024)S(1)} %broadcast_clamp_fusion), kind=kCustom, calls=%fused_computation.3.clone | custom fusion | bytes 25190400 | tf_op jit(solution)/shard_map/jit(_take)/gather | solution.py:20
  833.8 52.3 %all-to-all-done.3 = bf16[64,48,1024]{2,1,0:T(8,128)(2,1)} async-done(((bf16[64,48,1024]{2,1,0:T(8,128)(2,1)}), bf16[64,48,1024]{2,1,0:T(8,128)(2,1)}, u32[]{:S(2)}, u32[]{:S(2)}) %all-to-all-start.3) | async-done | bytes 6291488 | tf_op jit(solution)/shard_map/all_to_all | solution.py:78
  886.0 34.4 %gather_fusion.7 = bf16[6144,1024]{1,0:T(8,128)(2,1)} fusion(bf16[3072,1024]{1,0:T(8,128)(2,1)} %bitcast.18, s32[6144]{0:T(1024)S(1)} %broadcast_clamp_fusion), kind=kCustom, calls=%fused_computation.1.clone | custom fusion | bytes 25190400 | tf_op jit(solution)/shard_map/jit(_take)/gather | solution.py:20
  920.4 17.3 %select_bitcast_fusion.1 = (bf16[2,1,3072,1024]{3,2,0,1:T(8,128)(2,1)}, bf16[2,1,3072,1024]{3,2,1,0:T(8,128)(2,1)}) fusion(bf16[2,3072,1024]{2,1,0:T(8,128)(2,1)} %bitcast.220, pred[2,3072]{1,0:T(4,128)(4,1)S(1)} %get-tuple-element.31, bf16[2,3072,1024]{2,1,0:T(8,128)(2,1)} %bitcast.219), kind=kLoop, calls=%fused_computation.39 | loop fusion | flops 12582912 | bytes 50337792 | tf_op jit(solution)/shard_map/reshape | solution.py:88
  937.7 16.7 %copy.95 = bf16[2,1,3072,1024]{2,3,1,0:T(8,128)(2,1)} copy(bf16[2,1,3072,1024]{3,2,0,1:T(8,128)(2,1)} %get-tuple-element.42) | data formatting | bytes 25165824 | tf_op jit(solution)/shard_map/reshape | solution.py:88
  954.4 24.7 %all_to_all.57 = bf16[2,1,3072,1024]{3,2,1,0:T(8,128)(2,1)} all-to-all(bf16[2,1,3072,1024]{3,2,1,0:T(8,128)(2,1)} %get-tuple-element.43), channel_id=1, replica_groups=mesh['part'=1,'loc'=2,'grp'=64] {'loc'}, dimensions={0} | all-to-all | bytes 25165824 | tf_op jit(solution)/shard_map/all_to_all | solution.py:87
  987.6 12.2 fusion.12
  999.8 12.0 fusion.18
  1011.8 21.7 %fusion.31 = (bf16[2,3072,384]{2,1,0:T(8,128)(2,1)}, bf16[2,1,3072,384]{3,2,0,1:T(8,128)(2,1)}, bf16[2,3072,384]{2,1,0:T(8,128)(2,1)}) fusion(f32[2,3072,384]{2,1,0:T(8,128)} %fusion.12, f32[2,3072,384]{2,1,0:T(8,128)} %fusion.18, bf16[1,1024,384]{2,1,0:T(8,128)(2,1)S(1)} %copy-done.5, bf16[2,1,3072,1024]{3,2,1,0:T(8,128)(2,1)} %all_to_all.57), kind=kOutput, calls=%fused_computation.61 | convolution fusion | flops 4867227648 | bytes 46399488 | tf_op jit(solution)/shard_map/lecd,edf->lecf/dot_general | solution.py:38
  1048.8 43.0 %scatter_custom_fusion.6 = f32[24577]{0:T(1024)S(1)} fusion(s32[6144]{0:T(1024)} %copy-done.7, f32[6144]{0:T(1024)S(1)} %bitcast.247, f32[]{:T(128)} %constant.71.clone.1), kind=kCustom, calls=%fused_computation.106 | custom fusion | flops 6144 | bytes 98820 | tf_op jit(solution)/shard_map/scatter-add | solution.py:97
  1094.0 14.2 %fusion.33 = f32[2,3072,1024]{2,1,0:T(8,128)} fusion(bf16[2,1,3072,384]{3,2,0,1:T(8,128)(2,1)} %get-tuple-element.36, bf16[1,1024,384]{2,1,0:T(8,128)(2,1)S(1)} %copy-done.4), kind=kOutput, calls=%fused_computation.63 | convolution fusion | flops 4831838208 | bytes 30670848 | tf_op jit(solution)/shard_map/lecf,edf->lecd/dot_general | solution.py:51
  1108.3 15.7 %fusion.4 = bf16[2,1,3072,1024]{3,2,1,0:T(8,128)(2,1)} fusion(f32[2,3072,1024]{2,1,0:T(8,128)} %fusion.33, bf16[2,3072,384]{2,1,0:T(8,128)(2,1)} %get-tuple-element.37, bf16[1,1024,384]{2,1,0:T(8,128)(2,1)S(1)} %copy-done.5), kind=kOutput, calls=%fused_computation.25 | convolution fusion | flops 4844421120 | bytes 43253760 | tf_op jit(solution)/shard_map/lecf,edf->lecd/dot_general | solution.py:51
  1123.9 24.7 %all_to_all.59 = bf16[2,1,3072,1024]{3,2,1,0:T(8,128)(2,1)} all-to-all(bf16[2,1,3072,1024]{3,2,1,0:T(8,128)(2,1)} %fusion.4), channel_id=1, replica_groups=mesh['part'=1,'loc'=2,'grp'=64] {'loc'}, dimensions={0} | all-to-all | bytes 25165824 | tf_op jit(solution)/shard_map/all_to_all | solution.py:93
  1148.7 13.1 all-to-all-start.10
  1161.7 57.2 %scatter_custom_fusion.4 = f32[3073,1024]{1,0:T(8,128)} fusion(s32[6144]{0:T(1024)} %get-tuple-element.39, bf16[6144,1024]{1,0:T(8,128)(2,1)} %bitcast.218, f32[]{:T(128)} %constant.71.clone.1), kind=kCustom, calls=%fused_computation.22 | custom fusion | flops 12582912 | bytes 25170432 | tf_op jit(solution)/shard_map/scatter-add | solution.py:95
  1258.6 11.9 fusion.44
  1272.0 17.4 %scatter_custom_fusion.7 = f32[769,8]{1,0:T(8,128)S(1)} fusion(s32[3072]{0:T(1024)} %get-tuple-element.41, f32[3072,8]{1,0:T(8,128)S(1)} %bitcast.228, f32[]{:T(128)} %constant.71.clone.1), kind=kCustom, calls=%fused_computation.86 | custom fusion | flops 24576 | bytes 25120 | tf_op jit(solution)/shard_map/scatter-add | solution.py:104
  1290.2 40.2 %all-to-all-done.8 = bf16[64,48,1024]{2,1,0:T(8,128)(2,1)} async-done(((bf16[64,48,1024]{2,1,0:T(8,128)(2,1)}), bf16[64,48,1024]{2,1,0:T(8,128)(2,1)}, u32[]{:S(2)}, u32[]{:S(2)}) %all-to-all-start.8) | async-done | bytes 6291488 | tf_op jit(solution)/shard_map/all_to_all | solution.py:99
  1330.4 28.3 %scatter_custom_fusion.5 = f32[769,1024]{1,0:T(8,128)} fusion(s32[3072]{0:T(1024)} %get-tuple-element.41, bf16[3072,1024]{1,0:T(8,128)(2,1)} %bitcast.75, f32[]{:T(128)} %constant.71.clone.1), kind=kCustom, calls=%fused_computation.28 | custom fusion | flops 6291456 | bytes 9441792 | tf_op jit(solution)/shard_map/scatter-add | solution.py:103
  (122 shorter events, 157.6 us)
Async XLA Ops:
  0.6 181.7 %copy-start = (bf16[768,1024]{1,0:T(8,128)(2,1)S(1)}, bf16[768,1024]{1,0:T(8,128)(2,1)}, u32[]{:S(2)}) copy-start(bf16[768,1024]{1,0:T(8,128)(2,1)} %param.11) | copy-start | bytes 4718596
  87.1 60.6 %copy-start.8 = (s32[768,8]{0,1:T(8,128)S(1)}, s32[768,8]{0,1:T(8,128)}, u32[]{:S(2)}) copy-start(s32[768,8]{0,1:T(8,128)} %param.13) | copy-start | bytes 73732
  158.9 63.9 %all-to-all-start = ((s32[64,1,384]{2,1,0:T(1,128)}), s32[64,1,384]{2,1,0:T(1,128)}, u32[]{:S(2)}, u32[]{:S(2)}) async-start(s32[64,1,384]{2,1,0:T(1,128)} %reshape.766), calls=%async_computation | async-start | bytes 196608 | tf_op jit(solution)/shard_map/all_to_all | solution.py:79
  182.4 15.0 %copy-start.2 = (bf16[768,1024]{1,0:T(8,128)(2,1)S(1)}, bf16[768,1024]{1,0:T(8,128)(2,1)}, u32[]{:S(2)}) copy-start(bf16[768,1024]{1,0:T(8,128)(2,1)} %param.12) | copy-start | bytes 4718596
  182.4 15.0 %copy-start.6 = (s32[3072]{0:T(1024)S(1)}, s32[3072]{0:T(1024)}, u32[]{:S(2)}) copy-start(s32[3072]{0:T(1024)} %broadcast_clamp_fusion.3) | copy-start | bytes 36868
  197.4 14.0 %copy-start.9 = (pred[64,48]{1,0:T(8,128)(4,1)S(1)}, pred[64,48]{1,0:T(8,128)(4,1)}, u32[]{:S(2)}) copy-start(pred[64,48]{1,0:T(8,128)(4,1)} %get-tuple-element.33) | copy-start | bytes 9220
  211.4 10.5 copy-start.3
  222.8 20.2 %all-to-all-start.1 = ((f32[64,1,384]{2,1,0:T(1,128)}), f32[64,1,384]{2,1,0:T(1,128)S(1)}, u32[]{:S(2)}, u32[]{:S(2)}) async-start(f32[64,1,384]{2,1,0:T(1,128)} %reshape.768), calls=%async_computation.1 | async-start | bytes 196608 | tf_op jit(solution)/shard_map/all_to_all | solution.py:80
  657.0 142.1 %copy-start.7 = (s32[6144]{0:T(1024)}, s32[6144]{0:T(1024)S(1)}, u32[]{:S(2)}) copy-start(s32[6144]{0:T(1024)S(1)} %get-tuple-element.38) | copy-start | bytes 73732
  785.3 100.8 %all-to-all-start.3 = ((bf16[64,48,1024]{2,1,0:T(8,128)(2,1)}), bf16[64,48,1024]{2,1,0:T(8,128)(2,1)}, u32[]{:S(2)}, u32[]{:S(2)}) async-start(bf16[64,48,1024]{2,1,0:T(8,128)(2,1)} %get-tuple-element.44), calls=%async_computation.3 | async-start | bytes 12582912 | tf_op jit(solution)/shard_map/all_to_all | solution.py:78
  979.1 8.5 copy-start.4
  979.1 20.7 %all-to-all-start.4 = ((bf16[2,1,3072,1024]{2,3,1,0:T(8,128)(2,1)}), bf16[2,1,3072,1024]{2,3,1,0:T(8,128)(2,1)}, u32[]{:S(2)}, u32[]{:S(2)}) async-start(bf16[2,1,3072,1024]{2,3,1,0:T(8,128)(2,1)} %copy.95), calls=%async_computation.4 | async-start | bytes 25165824 | tf_op jit(solution)/shard_map/all_to_all | solution.py:88
  987.6 12.2 copy-start.10
  999.8 12.0 copy-start.5
  1148.7 78.6 %all-to-all-start.10 = ((f32[64,1,384]{2,1,0:T(1,128)}), f32[64,1,384]{2,1,0:T(1,128)S(1)}, u32[]{:S(2)}, u32[]{:S(2)}) async-start(f32[64,1,384]{2,1,0:T(1,128)} %reshape.770), calls=%async_computation.10 | async-start | bytes 196608 | tf_op jit(solution)/shard_map/all_to_all | solution.py:100
  1227.2 21.1 %slice-start = ((s8[4718592]{0:T(1024)(128)(4,1)}), s8[524288]{0:T(1024)(128)(4,1)S(1)}, s32[]{:S(2)}) async-start(s8[4718592]{0:T(1024)(128)(4,1)} %bitcast.224), calls=%async_computation.11 | async-start | bytes 1048576
  1227.2 103.1 %all-to-all-start.8 = ((bf16[64,48,1024]{2,1,0:T(8,128)(2,1)}), bf16[64,48,1024]{2,1,0:T(8,128)(2,1)}, u32[]{:S(2)}, u32[]{:S(2)}) async-start(bf16[64,48,1024]{2,1,0:T(8,128)(2,1)} %bitcast.221), calls=%async_computation.8 | async-start | bytes 12582912 | tf_op jit(solution)/shard_map/all_to_all | solution.py:99
  1237.9 10.4 slice-start.1
  1258.6 103.4 %copy-start.1 = (bf16[768,1024]{1,0:T(8,128)(2,1)S(1)}, bf16[768,1024]{1,0:T(8,128)(2,1)}, u32[]{:S(2)}) copy-start(bf16[768,1024]{1,0:T(8,128)(2,1)} %param.11) | copy-start | bytes 4718596
where the time goes:
time: 1380 us; the launch traced here: 1360 us
  local copies, waits for them, and re-layouts  512 us (37%)
  other arithmetic  416 us (30%)
  blocking collectives  147 us (11%)
  matrix products  120 us (9%)
  waiting for transfers between devices  97.1 us (7%)
  starting transfers between devices  68.5 us (5%)
    scatter-add x2, other arithmetic, slot_table(): jax.ops.segment_sum(jnp.ones_like(bin_ids), bin_ids, num_segments=num_bin...  213 us
    gather x2, local copies, waits for them, and re-layouts, slot_table(): sorted_bins = bin_ids[item_order]  170 us
    gather x9, local copies, waits for them, and re-layouts, gather_rows(): return jnp.take(source, row_index, axis=0, mode='fill', fill_value=fill_val)  150 us
    scatter x2, local copies, waits for them, and re-layouts, slot_table(): jnp.full((num_bins * capacity + 1,), n_items, jnp.int32).at[dest_slot]  113 us
    all_to_all x1, blocking collectives, device_step(): lax.all_to_all(gather_rows(x_rows, send_tok, 0), 'grp', 0, 0)  90.1 us
    scatter-add x1, other arithmetic, device_step(): jax.ops.segment_sum(contrib_back.astype(jnp.float32), fan_rows.reshape(-1...  57.2 us
    all_to_all x1, waiting for transfers between devices, device_step(): lax.all_to_all(gather_rows(dy_rows, send_tok, 0), 'grp', 0, 0)  52.3 us
    scatter-add x1, other arithmetic, device_step(): jax.ops.segment_sum(dgate_back, fan_items.reshape(-1), num_segments=rows_...  43 us
  transfers between devices with their start and end apart: 6, of which 3 were waited for; matrix products, arithmetic and copies ran while one was open for 16% of the time, Pallas kernels for 0%

commit v1 on v0

v1 whole, which is shorter than its diff:
```python
import jax
import jax.numpy as jnp
from jax import lax
from jax.experimental import pallas as pl
from jax.experimental.pallas import tpu as pltpu
from jax.sharding import PartitionSpec as P

MESH = pl.DeviceIdType.MESH
LANES = 128
WIDE = 256
F32 = jnp.float32
BF16 = jnp.bfloat16
SIDE = 4
PLANE = SIDE * SIDE
GROUPS = SIDE ** 3
TOK = 768
TOP_K = 8
D = 1024
F = 384
SLOTS = 48
ROUNDS = 3
RS = SLOTS // ROUNDS
NBLK = TOK // LANES
FWD = ((0, 640), (640, 640), (1280, 768))
BWD = ((0, 384), (384, 384), (768, 256))
OFFS = sorted(((a, b) for a in range(SIDE) for b in range(SIDE) if (a, b) != (0, 0)),
              key=lambda o: sum(min(v, SIDE - v) for v in o))


def dot(a, b, ca=1, cb=0):
    return lax.dot_general(a, b, (((ca,), (cb,)), ((), ())), preferred_element_type=F32)


def first(n):
    return pl.ds(0, n)


def over_lanes(v):
    return jnp.sum(v, axis=1, keepdims=True)


def over_rows(v):
    return jnp.sum(v, axis=0, keepdims=True)


def iota(shape, dim):
    return lax.broadcasted_iota(jnp.int32, shape, dim)


def kernel(x_hbm, dy_hbm, idst_hbm, gatt_hbm, ids_ref, wg_hbm, wu_hbm, wd_hbm,
           dx_hbm, dgate_ref, dwg_hbm, dwu_hbm, dwd_hbm, ia, ib, ic, rb,
           gat, snd, rx, wgu, wdn, acc, hd, ubuf, abuf, pbuf, slots, gws, slotn, idst, gatt,
           mg, mr, dgb, dgr, dgi, dgh, vbuf, dgacc,
           loc_sem, meta_s, meta_r, g1_s, g1_r, g2_s, g2_r, f2_s, f2_r, mg_s, mg_r, d2_s, d2_r, dm_s, dm_r,
           c_s, c_r, dg_s, dg_r, b1_s, b1_r, b1m_s, b1m_r, bl_s, b2_s, b2_r, b2m_s, b2m_r, out_s, credit):
    g = lax.axis_index('grp')
    l = lax.axis_index('loc')
    z, y, x = g // PLANE, (g // SIDE) % SIDE, g % SIDE
    coord = (x, y, z)
    other = 1 - l

    def gid(zz, yy, xx):
        return zz * PLANE + yy * SIDE + xx

    def along(c, k):
        return gid(*(k if a == c else coord[a] for a in (2, 1, 0)))

    def in_plane(c, a, b):
        if c == 0:
            return gid(a, b, x)
        if c == 1:
            return gid(a, y, b)
        return gid(z, a, b)

    my_plane = ((z, y), (z, x), (y, x))
    my_p = tuple(a * SIDE + b for a, b in my_plane)

    def rmod(v):
        return lax.rem(v, SIDE)

    def remote(src, dst, ss, rs, grp=None, loc=None):
        return pltpu.make_async_remote_copy(src, dst, ss, rs, device_id={'grp': g if grp is None else grp, 'loc': l if loc is None else loc},
                                            device_id_type=MESH)

    def local(src, dst, sem):
        return pltpu.make_async_copy(src, dst, sem)

    barrier = pltpu.get_barrier_semaphore()
    peers = []
    for dz in range(SIDE):
        for dyy in range(SIDE):
            for dxx in range(SIDE):
                if (dz, dyy, dxx) != (0, 0, 0) and 0 in (dz, dyy, dxx):
                    peers.append(gid(rmod(z + dz), rmod(y + dyy), rmod(x + dxx)))
    for p in peers:
        pl.semaphore_signal(barrier, inc=1, device_id={'grp': p, 'loc': l}, device_id_type=MESH)
    pl.semaphore_signal(barrier, inc=1, device_id={'grp': g, 'loc': other}, device_id_type=MESH)
    pl.semaphore_wait(barrier, len(peers) + 1)

    def slab_copies(c, make):
        c0, w = FWD[c]
        out = []
        if c0 < D:
            n = min(w, D - c0)
            out.append(make(x_hbm.at[:, pl.ds(c0, n)], pl.ds(c0, n)))
        if c0 + w > D:
            s = max(c0, D)
            out.append(make(dy_hbm.at[:, pl.ds(s - D, c0 + w - s)], pl.ds(s, c0 + w - s)))
        return out

    def cols(c):
        return pl.ds(*FWD[c])

    for c in range(3):
        for k in (1, 3, 2):
            t = along(c, rmod(coord[c] + k))
            remote(idst_hbm, idst.at[c, coord[c]], meta_s.at[c, 0], meta_r.at[c, 0], t).start()
            if c == 0:
                remote(gatt_hbm, gatt.at[x], meta_s.at[c, 1], meta_r.at[c, 1], t).start()
    for d, k in enumerate((1, 3)):
        for c in range(3):
            t = along(c, rmod(coord[c] + k))
            for cp in slab_copies(c, lambda src, cs: remote(src, gat.at[coord[c], :, cs], g1_s.at[c, d], g1_r.at[c, d], t)):
                cp.start()
    for c in range(3):
        local(idst_hbm, idst.at[c, coord[c]], loc_sem.at[0, c]).start()
    local(gatt_hbm, gatt.at[x], loc_sem.at[0, 3]).start()
    for c in range(3):
        for cp in slab_copies(c, lambda src, cs: local(src, gat.at[coord[c], :, cs], loc_sem.at[1, c])):
            cp.start()
    weights = [local(wg_hbm, wgu.at[:, first(F)], loc_sem.at[2, 0]), local(wu_hbm, wgu.at[:, pl.ds(F, F)], loc_sem.at[2, 1]),
               local(wd_hbm, wdn, loc_sem.at[2, 2])]
    for cp in weights:
        cp.start()
    for c in range(3):
        local(idst_hbm, idst.at[c, coord[c]], loc_sem.at[0, c]).wait()
    local(gatt_hbm, gatt.at[x], loc_sem.at[0, 3]).wait()

    tri = (iota((LANES, LANES), 0) < iota((LANES, LANES), 1)).astype(BF16)

    def plane_gid(c):
        p = iota((PLANE, 1), 0)
        a, b = p // SIDE, lax.rem(p, SIDE)
        return in_plane(c, a, b)

    def make_table(c, k):
        gids = plane_gid(c)
        carry = jnp.zeros((PLANE, 1), F32)
        for blk in range(NBLK):
            ls = pl.ds(blk * LANES, LANES)
            ids = idst[c, k, :, ls]
            member = jnp.zeros((PLANE, LANES), F32)
            w0 = jnp.zeros((PLANE, LANES), F32)
            w1 = jnp.zeros((PLANE, LANES), F32)
            for j in range(TOP_K):
                idj = ids[j:j + 1, :]
                e0 = idj == 2 * gids
                e1 = idj == 2 * gids + 1
                member = jnp.where(e0 | e1, 1.0, member)
                if c == 0:
                    gj = gatt[k, pl.ds(j, 1), ls]
                    w0 = jnp.where(e0, gj, w0)
                    w1 = jnp.where(e1, gj, w1)
            rank = dot(member.astype(BF16), tri) + carry
            carry = carry + over_lanes(member)
            slots[c, k, :, ls] = jnp.where(member > 0, rank, -1.0)
            if c == 0:
                gws[k, 0, :, ls] = w0
                gws[k, 1, :, ls] = w1

    for c in range(3):
        make_table(c, coord[c])

    rowtri = (iota((LANES, LANES), 1) < iota((LANES, LANES), 0)).astype(BF16)
    carry = jnp.zeros((1, GROUPS), F32)
    for blk in range(NBLK):
        ts = pl.ds(blk * LANES, LANES)
        ids = ids_ref[ts, :]
        member = jnp.zeros((LANES, GROUPS), F32)
        for j in range(TOP_K):
            member = jnp.where((ids[:, j:j + 1] // 2) == iota((1, GROUPS), 1), 1.0, member)
        rank = dot(rowtri, member.astype(BF16)) + carry
        carry = carry + over_rows(member)
        slotn[ts, :] = jnp.where(member > 0, rank, -1.0).astype(BF16)

    for r in range(ROUNDS):
        mg[r] = jnp.zeros((PLANE, 1, LANES), F32)

    def gather(c, k, r, s):
        base = (iota((RS, 1), 0) + r * RS).astype(F32)
        lane = iota((RS, LANES), 1)
        row = iota((RS, 1), 0)

        def one(p, carry_):
            mask = slots[c, k, pl.ds(p, 1), :] == base
            pbuf[pl.ds(p * RS, RS), :] = mask.astype(F32).astype(BF16)
            if c == 0:
                line = jnp.zeros((1, LANES), F32)
                for e in range(2):
                    col = over_lanes(jnp.where(mask, gws[k, e, pl.ds(p, 1), :], 0.0))
                    line = line + over_rows(jnp.where(lane == e * 64 + k * RS + row, col, 0.0))
                mg[r, p] = mg[r, p] + line
            return carry_

        lax.fori_loop(0, PLANE, one, 0)
        c0, w = FWD[c]
        rows = dot(pbuf[...], gat[k, :, pl.ds(c0, w)]).astype(BF16)
        snd[s, :, k, :, pl.ds(c0, w)] = rows.reshape(PLANE, RS, w)

    def slot_of(r):
        return lax.rem(r, 2)

    def gather_all(c, k, rounds):
        def one(r, carry_):
            gather(c, k, r, slot_of(r))
            return carry_
        lax.fori_loop(rounds[0], rounds[1], one, 0)

    for c in range(3):
        for cp in slab_copies(c, lambda src, cs: local(src, gat.at[coord[c], :, cs], loc_sem.at[1, c])):
            cp.wait()
        gather_all(c, coord[c], (0, 2))
    acc[...] = jnp.zeros_like(acc)

    for c in range(3):
        proxy = idst.at[c, first(3)]
        local(proxy, proxy, meta_r.at[c, 0]).wait()
        local(proxy, proxy, meta_s.at[c, 0]).wait()
        if c == 0:
            proxy = gatt.at[first(3)]
            local(proxy, proxy, meta_r.at[c, 1]).wait()
            local(proxy, proxy, meta_s.at[c, 1]).wait()
    for c in range(3):
        for k in (1, 3, 2):
            make_table(c, rmod(coord[c] + k))

    half = TOK // 2
    for d, k in enumerate((1, 3)):
        for c in range(3):
            src = rmod(coord[c] + SIDE - k)
            block = gat.at[src, :, cols(c)]
            local(block, block, g1_r.at[c, d]).wait()
            t = along(c, rmod(coord[c] + k))
            part = gat.at[src, pl.ds(d * half, half), cols(c)]
            remote(part, part, g2_s.at[c, d], g2_r.at[c, d], t).start()
    for d, k in enumerate((1, 3)):
        for c in range(3):
            gather_all(c, rmod(coord[c] + SIDE - k), (0, 2))

    def send_round(r):
        s = slot_of(r)
        for a, b in OFFS:
            for c in range(3):
                pa, pb = rmod(my_plane[c][0] + a), rmod(my_plane[c][1] + b)
                src = snd.at[s, pa * SIDE + pb, :, :, cols(c)]
                dst = (rx.at[l, r, z, y, :, :, cols(c)], rx.at[l, r, z, :, x, :, cols(c)], rx.at[l, r, :, y, x, :, cols(c)])[c]
                t = in_plane(c, pa, pb)
                remote(src, dst, f2_s.at[r, c], f2_r.at[r, c], t).start()
                if c == 0:
                    remote(mg.at[r, pa * SIDE + pb], mr.at[l, r, z * SIDE + y], mg_s.at[r], mg_r.at[r], t).start()
        for c in range(3):
            own = snd[s, my_p[c], :, :, cols(c)]
            if c == 0:
                rx[l, r, z, y, :, :, cols(c)] = own
            elif c == 1:
                rx[l, r, z, :, x, :, cols(c)] = own
            else:
                rx[l, r, :, y, x, :, cols(c)] = own
        mr[l, r, z * SIDE + y] = mg[r, my_p[0]]

    def proxy15(c, table):
        c0, w = table[c]
        return snd.at[0, first(PLANE - 1), :, :, first(w)]

    def wait_send(r):
        for c in range(3):
            local(proxy15(c, FWD), proxy15(c, FWD), f2_s.at[r, c]).wait()
        m = mg.at[r, first(PLANE - 1)]
        local(m, m, mg_s.at[r]).wait()

    for c in range(3):
        for d in range(2):
            src = rmod(coord[c] + 2)
            part = gat.at[src, pl.ds(d * half, half), cols(c)]
            local(part, part, g2_r.at[c, d]).wait()
    for r in range(2):
        for c in range(3):
            gather_all(c, rmod(coord[c] + 2), (r, r + 1))
        send_round(r)
    wait_send(0)
    for c in range(3):
        def one(k, carry_):
            gather(c, k, 2, 0)
            return carry_
        lax.fori_loop(0, SIDE, one, 0)
    send_round(2)
    for cp in weights:
        cp.wait()

    mine = (iota((64, LANES), 1) == l * 64 + iota((64, LANES), 0))

    def chunk(r, kk):
        lp = jnp.where(kk < 2, l, other)
        z0 = lax.rem(kk, 2) * 2
        zs = pl.ds(z0, 2)

        def col(c0, w):
            return rx[lp, r, zs, :, :, :, pl.ds(c0, w)].reshape(512, w)

        abuf[...] = dot(col(0, D), wgu[...])
        for m in range(8):
            line = mr[lp, r, z0 * SIDE + m]
            gcol = over_lanes(jnp.where(mine, line, 0.0))
            part = rx[lp, r, z0 + m // SIDE, m % SIDE, :, :, pl.ds(D, D)].reshape(64, D)
            ubuf[pl.ds(m * 64, 64), :] = (gcol * part.astype(F32)).astype(BF16)
        dh = dot(ubuf[...], wdn[...], 1, 1)
        a = abuf[:, :F]
        b = abuf[:, F:]
        sig = jax.nn.sigmoid(a)
        silu = a * sig
        hd[:, first(F)] = (silu * b).astype(BF16)
        hd[:, pl.ds(F, F)] = (dh * b * sig * (1.0 + a * (1.0 - sig))).astype(BF16)
        hd[:, pl.ds(2 * F, F)] = (dh * silu).astype(BF16)
        dg = jnp.zeros((512, 1), F32)
        for n in range(4):
            o = dot(hd[:, first(F)], wdn[:, pl.ds(n * WIDE, WIDE)])
            dg = dg + over_lanes(col(D + n * WIDE, WIDE).astype(F32) * o)
        for m in range(8):
            line = over_rows(jnp.where(mine, dg[m * 64:(m + 1) * 64, :], 0.0))
            dgb[kk // 2, r, z0 * SIDE + m] = line
        acc[first(F), :] += dot(hd[:, first(F)], ubuf[...], 0, 0)
        acc[pl.ds(F, 2 * F), :] += dot(hd[:, pl.ds(F, 2 * F)], col(0, D), 0, 0)
        for n in range(4):
            cval = dot(hd[:, pl.ds(F, 2 * F)], wgu[pl.ds(n * WIDE, WIDE), :], 1, 1)
            rx[lp, r, zs, :, :, :, pl.ds(n * WIDE, WIDE)] = cval.astype(BF16).reshape(2, SIDE, SIDE, RS, WIDE)

    def relay(r):
        for c, buf in enumerate((ia, ib, ic)):
            local(proxy15(c, BWD), proxy15(c, BWD), b1_r.at[r, c]).wait()
            own = buf.at[r, 0, 0]
            local(own, own, bl_s.at[r, c]).wait()
        m = dgi.at[r, first(PLANE - 1)]
        local(m, m, b1m_r.at[r]).wait()
        for k in (1, 3, 2):
            for c, buf in enumerate((ia, ib, ic)):
                to = rmod(coord[c] + k)
                cs = pl.ds(*BWD[c])
                dst = (rb.at[r, :, :, x, :, cs], rb.at[r, :, y, :, :, cs], rb.at[r, z, :, :, :, cs])[c]
                remote(buf.at[r, :, :, to], dst, b2_s.at[r, c], b2_r.at[r, c], along(c, to)).start()
                if c == 0:
                    remote(dgi.at[r], dgh.at[r, x], b2m_s.at[r], b2m_r.at[r], along(0, to)).start()
        dgh[r, x] = dgi[r]

    def round_body(r, carry_):
        for c in range(3):
            local(proxy15(c, FWD), proxy15(c, FWD), f2_r.at[r, c]).wait()
        m = mg.at[0, first(PLANE - 1)]
        local(m, m, mg_r.at[r]).wait()
        for h in range(2):
            blk = rx.at[l, r, pl.ds(2 * h, 2)]
            remote(blk, blk, d2_s.at[r, h], d2_r.at[r, h], loc=other).start()
        remote(mr.at[l, r], mr.at[l, r], dm_s.at[r], dm_r.at[r], loc=other).start()

        def step(kk, carry2):
            @pl.when(kk >= 2)
            def _():
                blk = rx.at[other, r, pl.ds((kk - 2) * 2, 2)]
                local(blk, blk, d2_r.at[r, kk - 2]).wait()

            @pl.when(kk == 2)
            def _():
                local(mr.at[other, r], mr.at[other, r], dm_r.at[r]).wait()

            @pl.when(kk < 2)
            def _():
                blk = rx.at[l, r, pl.ds(kk * 2, 2)]
                local(blk, blk, d2_s.at[r, kk]).wait()

            chunk(r, kk)

            @pl.when(kk == 1)
            def _():
                pl.semaphore_signal(credit.at[r], inc=1, device_id={'grp': g, 'loc': other}, device_id_type=MESH)

                @pl.when(r > 0)
                def _():
                    relay(r - 1)

            @pl.when(kk == 2)
            def _():
                pl.semaphore_wait(credit.at[r], 1)

            @pl.when(kk >= 2)
            def _():
                zs = pl.ds((kk - 2) * 2, 2)
                remote(rx.at[other, r, zs, :, :, :, first(D)], rx.at[other, r, zs, :, :, :, pl.ds(D, D)],
                       c_s.at[r, kk - 2], c_r.at[r, kk - 2], loc=other).start()
            return carry2

        lax.fori_loop(0, 4, step, 0)
        remote(dgb.at[1, r], dgr.at[r], dg_s.at[r], dg_r.at[r], loc=other).start()
        for h in range(2):
            blk = rx.at[l, r, pl.ds(2 * h, 2), :, :, :, pl.ds(D, D)]
            local(blk, blk, c_r.at[r, h]).wait()

            def add(zy, carry2):
                zz, yy = 2 * h + zy // SIDE, lax.rem(zy, SIDE)
                p0 = rx[l, r, zz, yy, :, :, first(D)].astype(F32)
                p1 = rx[l, r, zz, yy, :, :, pl.ds(D, D)].astype(F32)
                rx[l, r, zz, yy, :, :, first(D)] = (p0 + p1).astype(BF16)
                return carry2

            lax.fori_loop(0, 8, add, 0)
        local(dgr.at[r], dgr.at[r], dg_r.at[r]).wait()
        dgb[0, r] = dgb[0, r] + dgr[r]
        for c, buf in enumerate((ia, ib, ic)):
            cs = pl.ds(*BWD[c])
            src = (rx.at[l, r, z, y, :, :, cs], rx.at[l, r, z, :, x, :, cs], rx.at[l, r, :, y, x, :, cs])[c]
            local(src, buf.at[r, my_plane[c][0], my_plane[c][1]], bl_s.at[r, c]).start()
        for a, b in OFFS:
            for c, buf in enumerate((ia, ib, ic)):
                pa, pb = rmod(my_plane[c][0] + a), rmod(my_plane[c][1] + b)
                cs = pl.ds(*BWD[c])
                src = (rx.at[l, r, pa, pb, :, :, cs], rx.at[l, r, pa, :, pb, :, cs], rx.at[l, r, :, pa, pb, :, cs])[c]
                t = in_plane(c, pa, pb)
                remote(src, buf.at[r, my_plane[c][0], my_plane[c][1]], b1_s.at[r, c], b1_r.at[r, c], t).start()
                if c == 0:
                    remote(dgb.at[0, r, pa * SIDE + pb], dgi.at[r, my_p[0]], b1m_s.at[r], b1m_r.at[r], t).start()
        dgi[r, my_p[0]] = dgb[0, r, my_p[0]]
        return carry_

    lax.fori_loop(0, ROUNDS, round_body, 0)

    for c in range(3):
        for d in range(2):
            part = gat.at[0, first(half), cols(c)]
            local(part, part, g2_s.at[c, d]).wait()
    gat[1, first(F), first(D)] = acc[first(F), :].astype(BF16)
    gat[2, first(2 * F), first(D)] = acc[pl.ds(F, 2 * F), :].astype(BF16)
    outs = [local(gat.at[1, first(F), first(D)], dwd_hbm, out_s.at[0]),
            local(gat.at[2, first(F), first(D)], dwg_hbm, out_s.at[1]),
            local(gat.at[2, pl.ds(F, F), first(D)], dwu_hbm, out_s.at[2])]

    relay(ROUNDS - 1)
    for cp in outs:
        cp.start()
    wait_send(1)
    wait_send(2)

    dgacc[...] = jnp.zeros_like(dgacc)
    acc[first(TOK), :] = jnp.zeros((TOK, D), F32)
    for r in range(ROUNDS):
        half_cols = (r % 2) * D
        stage = snd.at[r // 2, :, :, :, pl.ds(half_cols, D)]
        for c, buf in enumerate((ia, ib, ic)):
            own = snd.at[0, first(12), :, :, first(BWD[c][1])]
            local(own, own, b2_r.at[r, c]).wait()
        m = dgh.at[r, first(3)]
        local(m, m, b2m_r.at[r]).wait()
        pieces = []
        for zy in range(PLANE):
            pieces.append(local(rb.at[r, zy // SIDE, zy % SIDE], snd.at[r // 2, zy, :, :, pl.ds(half_cols, D)], loc_sem.at[3, 0]))
        for cp in pieces:
            cp.start()
        spread = (iota((GROUPS, GROUPS * RS), 0) == iota((GROUPS, GROUPS * RS), 1) // RS).astype(F32).astype(BF16)
        want = (lax.rem(iota((1, GROUPS * RS), 1), RS) + r * RS).astype(F32)
        for n in range(4):
            ns = pl.ds(n * WIDE, WIDE)
            got = dot(slotn[...], spread[:, n * WIDE:(n + 1) * WIDE])
            gat[0, :, ns] = (got == want[:, n * WIDE:(n + 1) * WIDE]).astype(F32).astype(BF16)
        lane = iota((RS, LANES), 1)
        row = iota((RS, LANES), 0)

        def one(gg, carry_):
            line = dgh[r, lax.rem(gg, SIDE), gg // SIDE]
            out = jnp.zeros((RS, LANES), F32)
            for e in range(2):
                colv = over_lanes(jnp.where(lane == e * 64 + x * RS + row, line, 0.0))
                out = jnp.where(lane == 2 * gg + e, colv, out)
            vbuf[pl.ds(gg * RS, RS), :] = out
            return carry_

        lax.fori_loop(0, GROUPS, one, 0)
        rest = vbuf[...]
        for _ in range(3):
            part = rest.astype(BF16)
            dgacc[...] += dot(gat[0, :, first(D)], part)
            rest = rest - part.astype(F32)
        for cp in pieces:
            cp.wait()
        own_pieces = []
        for q in range(PLANE):
            a, b = q // SIDE, q % SIDE
            own_pieces.append(local(ia.at[r, a, b, x], snd.at[r // 2, q, x, :, pl.ds(half_cols + BWD[0][0], BWD[0][1])], loc_sem.at[3, 1]))
            own_pieces.append(local(ib.at[r, a, b, y], snd.at[r // 2, a * SIDE + y, b, :, pl.ds(half_cols + BWD[1][0], BWD[1][1])], loc_sem.at[3, 1]))
            own_pieces.append(local(ic.at[r, a, b, z], snd.at[r // 2, z * SIDE + a, b, :, pl.ds(half_cols + BWD[2][0], BWD[2][1])], loc_sem.at[3, 1]))
        for cp in own_pieces:
            cp.start()
        for cp in own_pieces:
            cp.wait()
        for n in range(4):
            got = snd[r // 2, :, :, :, pl.ds(half_cols + n * WIDE, WIDE)].reshape(GROUPS * RS, WIDE)
            acc[first(TOK), pl.ds(n * WIDE, WIDE)] += dot(gat[0, :, first(D)], got)
    gat[3, :, first(D)] = acc[first(TOK), :].astype(BF16)
    dx_out = local(gat.at[3, :, first(D)], dx_hbm, out_s.at[3])
    dx_out.start()
    lane = iota((TOK, LANES), 1)
    for j in range(TOP_K):
        hit = lane == ids_ref[:, j:j + 1]
        dgate_ref[:, j:j + 1] = over_lanes(jnp.where(hit, dgacc[...], 0.0))

    for c in range(3):
        for d in range(2):
            block = gat.at[0, :, cols(c)]
            local(block, block, g1_s.at[c, d]).wait()
    for r in range(ROUNDS):
        local(mr.at[0, r], mr.at[0, r], dm_s.at[r]).wait()
        local(dgr.at[r], dgr.at[r], dg_s.at[r]).wait()
        for h in range(2):
            blk = rx.at[0, r, pl.ds(2 * h, 2), :, :, :, first(D)]
            local(blk, blk, c_s.at[r, h]).wait()
        for c in range(3):
            local(proxy15(c, BWD), proxy15(c, BWD), b1_s.at[r, c]).wait()
            own = snd.at[0, first(12), :, :, first(BWD[c][1])]
            local(own, own, b2_s.at[r, c]).wait()
        m = dgi.at[r, first(PLANE - 1)]
        local(m, m, b1m_s.at[r]).wait()
        m = dgh.at[r, first(3)]
        local(m, m, b2m_s.at[r]).wait()
    for cp in outs:
        cp.wait()
    dx_out.wait()


def solution(mesh):
    spec = P(('part', 'grp', 'loc'))

    def device_step(x_rows, dy_rows, expert_ids, gate_vals, w_gate, w_up, w_down):
        any_ = pl.BlockSpec(memory_space=pl.ANY)
        vmem = pl.BlockSpec(memory_space=pltpu.VMEM)
        dma = pltpu.SemaphoreType.DMA
        sd = jax.ShapeDtypeStruct
        out = pl.pallas_call(
            kernel,
            name='moe_backward',
            in_specs=[any_] * 4 + [vmem] + [any_] * 3,
            out_specs=[any_, vmem] + [any_] * 7,
            out_shape=[sd((TOK, D), BF16), sd((TOK, TOP_K), F32), sd((F, D), BF16), sd((F, D), BF16), sd((F, D), BF16),
                       sd((ROUNDS, SIDE, SIDE, SIDE, RS, BWD[0][1]), BF16), sd((ROUNDS, SIDE, SIDE, SIDE, RS, BWD[1][1]), BF16),
                       sd((ROUNDS, SIDE, SIDE, SIDE, RS, BWD[2][1]), BF16), sd((ROUNDS, SIDE, SIDE, SIDE, RS, D), BF16)],
            scratch_shapes=[
                pltpu.VMEM((SIDE, TOK, 2 * D), BF16),
                pltpu.VMEM((2, PLANE, SIDE, RS, 2 * D), BF16),
                pltpu.VMEM((2, ROUNDS, SIDE, SIDE, SIDE, RS, 2 * D), BF16),
                pltpu.VMEM((D, 2 * F), BF16),
                pltpu.VMEM((F, D), BF16),
                pltpu.VMEM((3 * F, D), F32),
                pltpu.VMEM((512, 3 * F), BF16),
                pltpu.VMEM((512, D), BF16),
                pltpu.VMEM((512, 2 * F), F32),
                pltpu.VMEM((PLANE * RS, TOK), BF16),
                pltpu.VMEM((3, SIDE, PLANE, TOK), F32),
                pltpu.VMEM((SIDE, 2, PLANE, TOK), F32),
                pltpu.VMEM((TOK, GROUPS), BF16),
                pltpu.VMEM((3, SIDE, TOP_K, TOK), jnp.int32),
                pltpu.VMEM((SIDE, TOP_K, TOK), F32),
                pltpu.VMEM((ROUNDS, PLANE, 1, LANES), F32),
                pltpu.VMEM((2, ROUNDS, PLANE, 1, LANES), F32),
                pltpu.VMEM((2, ROUNDS, PLANE, 1, LANES), F32),
                pltpu.VMEM((ROUNDS, PLANE, 1, LANES), F32),
                pltpu.VMEM((ROUNDS, PLANE, 1, LANES), F32),
                pltpu.VMEM((ROUNDS, SIDE, PLANE, 1, LANES), F32),
                pltpu.VMEM((GROUPS * RS, LANES), F32),
                pltpu.VMEM((TOK, LANES), F32),
                dma((4, 4)), *[dma((3, 2))] * 6, *[dma((ROUNDS, 3))] * 2, *[dma((ROUNDS,))] * 2, *[dma((ROUNDS, 2))] * 2,
                *[dma((ROUNDS,))] * 2, *[dma((ROUNDS, 2))] * 2, *[dma((ROUNDS,))] * 2, *[dma((ROUNDS, 3))] * 2,
                *[dma((ROUNDS,))] * 2, *[dma((ROUNDS, 3))] * 3, *[dma((ROUNDS,))] * 2, dma((4,)),
                pltpu.SemaphoreType.REGULAR((ROUNDS,)),
            ],
            compiler_params=pltpu.CompilerParams(collective_id=0, has_side_effects=True, vmem_limit_bytes=67043328),
        )(x_rows, dy_rows, expert_ids.T, gate_vals.T, expert_ids, w_gate[0], w_up[0], w_down[0])
        dx, d_gates, dwg_t, dwu_t, dwd = out[:5]
        return dx, d_gates, dwg_t.T[None], dwu_t.T[None], dwd[None]

    return jax.shard_map(device_step, mesh=mesh, in_specs=(spec,) * 7, out_specs=(spec,) * 5, check_vma=False)
```

time: 1380 us -> 294 us (0.21); the launches traced: 1360 us -> 290 us
  local copies, waits for them, and re-layouts: 512 us -> 9.59 us
  other arithmetic: 416 us -> 0 us
  Pallas kernels: 0 us -> 280 us
  blocking collectives: 147 us -> 0 us
  matrix products: 120 us -> 0 us
  waiting for transfers between devices: 97.1 us -> 0 us
  starting transfers between devices: 68.5 us -> 0 us
    scatter-add x6 -> x0, other arithmetic: 359 us -> none  [the longest x2 213 us: slot_table(): jax.ops.segment_sum(jnp.ones_like(bin_ids), bin_ids, num_segments=num_bin...]
    gather x13 -> x0, local copies, waits for them, and re-layouts: 357 us -> none  [the longest x2 170 us: slot_table(): sorted_bins = bin_ids[item_order]]
    pallas_call x0 -> x1, Pallas kernels: none -> 280 us  [device_step(): pl.pallas_call(kernel, name='moe_backward', in_specs=[any_] * 4 + [vmem]...]
    all_to_all x5 -> x0, blocking collectives: 147 us -> none  [the longest x1 90.1 us: device_step(): lax.all_to_all(gather_rows(x_rows, send_tok, 0), 'grp', 0, 0)]
    dot_general x9 -> x0, matrix products: 120 us -> none  [the longest x1 21.7 us: expert_backward(): jnp.einsum(up_form, x_own, w_up, preferred_element_type=jnp.float32)]
    scatter x2 -> x0, local copies, waits for them, and re-layouts: 113 us -> none  [slot_table(): jnp.full((num_bins * capacity + 1,), n_items, jnp.int32).at[dest_slot]]
    all_to_all x6 -> x0, waiting for transfers between devices: 97.1 us -> none  [the longest x1 52.3 us: device_step(): lax.all_to_all(gather_rows(dy_rows, send_tok, 0), 'grp', 0, 0)]
    all_to_all x6 -> x0, starting transfers between devices: 68.5 us -> none  [the longest x1 13.8 us: device_step(): lax.all_to_all(gather_rows(dy_rows, send_tok, 0), 'grp', 0, 0)]
  transfers between devices with their start and end apart: 6 -> 0, of which waited for: 3 -> 0; matrix products, arithmetic and copies ran while one was open for 16% -> 0% of each run, Pallas kernels for 0% -> 0%
where the time goes in v1:
time: 294 us; the launch traced here: 290 us
  Pallas kernels  280 us (95%)
  local copies, waits for them, and re-layouts  9.59 us (3%)
    pallas_call x1, Pallas kernels, device_step(): pl.pallas_call(kernel, name='moe_backward', in_specs=[any_] * 4 + [vmem]...  280 us
    unnamed x12, local copies, waits for them, and re-layouts  9.59 us

profile of v1, /device:TPU:0, one launch (start us, length us, event | category | flops | bytes accessed | tf_op | source)
XLA Modules:
  0.0 290.5 jit_solution(17683602114187883043)
XLA Ops:
  0.6 1.7 copy.12.ids_ref
  2.3 280.2 %moe_backward.1 = (bf16[768,1024]{1,0:T(8,128)(2,1)}, f32[768,8]{1,0:T(8,128)}, bf16[384,1024]{1,0:T(8,128)(2,1)}, bf16[384,1024]{1,0:T(8,128)(2,1)}, bf16[384,1...) custom-call(bf16[768,1024]{1,0:T(8,128)(2,1)} %x_hbm.1, ...), custom_call_target="tpu_custom_call" | custom-call | tf_op jit(solution)/shard_map/moe_backward/pallas_call | solution.py:543
  282.5 0.0 copy-start.2
  282.5 1.8 copy.13
  284.4 0.0 copy-start
  284.4 2.4 copy.14
  286.8 0.0 copy-done.2
  286.8 1.2 copy.15
  287.9 0.0 copy-done
  287.9 0.0 copy-start.1
  287.9 1.1 copy.18
  289.1 0.5 copy-done.1
  289.6 0.9 copy.19
Async XLA Ops:
  282.5 4.2 %copy-start.2 = (bf16[384,1024]{1,0:T(8,128)(2,1)S(1)}, bf16[384,1024]{1,0:T(8,128)(2,1)}, u32[]{:S(2)}) copy-start(bf16[384,1024]{1,0:T(8,128)(2,1)} %get-tuple-element.13) | copy-start | bytes 2359300
  284.4 3.6 %copy-start = (bf16[768,1024]{1,0:T(8,128)(2,1)S(1)}, bf16[768,1024]{1,0:T(8,128)(2,1)}, u32[]{:S(2)}) copy-start(bf16[768,1024]{1,0:T(8,128)(2,1)} %get-tuple-element.25) | copy-start | bytes 4718596
  287.9 1.7 copy-start.1

commit v2 on v1

v2 whole, which is shorter than its diff:
```python
import jax
import jax.numpy as jnp
from jax import lax
from jax.experimental import pallas as pl
from jax.experimental.pallas import tpu as pltpu
from jax.sharding import PartitionSpec as P

MESH = pl.DeviceIdType.MESH
LANES = 128
WIDE = 256
F32 = jnp.float32
BF16 = jnp.bfloat16
SIDE = 4
PLANE = SIDE * SIDE
GROUPS = SIDE ** 3
TOK = 768
TOP_K = 8
D = 1024
F = 384
SLOTS = 48
ROUNDS = 3
RS = SLOTS // ROUNDS
NBLK = TOK // LANES
FWD = ((0, 640), (640, 640), (1280, 768))
BWD = ((0, 384), (384, 384), (768, 256))
OFFS = sorted(((a, b) for a in range(SIDE) for b in range(SIDE) if (a, b) != (0, 0)),
              key=lambda o: sum(min(v, SIDE - v) for v in o))


def dot(a, b, ca=1, cb=0):
    return lax.dot_general(a, b, (((ca,), (cb,)), ((), ())), preferred_element_type=F32)


def first(n):
    return pl.ds(0, n)


def over_lanes(v):
    return jnp.sum(v, axis=1, keepdims=True)


def over_rows(v):
    return jnp.sum(v, axis=0, keepdims=True)


scope = jax.named_scope


def iota(shape, dim):
    return lax.broadcasted_iota(jnp.int32, shape, dim)


def kernel(x_hbm, dy_hbm, idst_hbm, gatt_hbm, wg_hbm, wu_hbm, wd_hbm,
           dx_hbm, dgate_ref, dwg_hbm, dwu_hbm, dwd_hbm, ia, ib, ic, rb,
           gat, snd, rx, wgu, wdn, acc, pbuf, slots, gws, slott, idst, gatt,
           mg, mr, dgb, dgr, dgi, dgj, dgh, dgacc,
           loc_sem, meta_s, meta_r, g1_s, g1_r, g2_s, g2_r, f2_s, f2_r, mg_s, mg_r, d2_s, d2_r, dm_s, dm_r,
           c_s, c_r, dg_s, dg_r, b1_s, b1_r, b1m_s, b1m_r, bl_s, b2_s, b2_r, b2m_s, b2m_r, out_s, credit):
    g = lax.axis_index('grp')
    l = lax.axis_index('loc')
    z, y, x = g // PLANE, (g // SIDE) % SIDE, g % SIDE
    coord = (x, y, z)
    other = 1 - l

    def gid(zz, yy, xx):
        return zz * PLANE + yy * SIDE + xx

    def along(c, k):
        return gid(*(k if a == c else coord[a] for a in (2, 1, 0)))

    def in_plane(c, a, b):
        if c == 0:
            return gid(a, b, x)
        if c == 1:
            return gid(a, y, b)
        return gid(z, a, b)

    my_plane = ((z, y), (z, x), (y, x))
    my_p = tuple(a * SIDE + b for a, b in my_plane)

    def rmod(v):
        return lax.rem(v, SIDE)

    def remote(src, dst, ss, rs, grp=None, loc=None):
        return pltpu.make_async_remote_copy(src, dst, ss, rs, device_id={'grp': g if grp is None else grp, 'loc': l if loc is None else loc},
                                            device_id_type=MESH)

    def local(src, dst, sem):
        return pltpu.make_async_copy(src, dst, sem)

    barrier = pltpu.get_barrier_semaphore()
    peers = []
    for dz in range(SIDE):
        for dyy in range(SIDE):
            for dxx in range(SIDE):
                if (dz, dyy, dxx) != (0, 0, 0) and 0 in (dz, dyy, dxx):
                    peers.append(gid(rmod(z + dz), rmod(y + dyy), rmod(x + dxx)))
    for p in peers:
        pl.semaphore_signal(barrier, inc=1, device_id={'grp': p, 'loc': l}, device_id_type=MESH)
    pl.semaphore_signal(barrier, inc=1, device_id={'grp': g, 'loc': other}, device_id_type=MESH)

    def slab_copies(c, make):
        c0, w = FWD[c]
        out = []
        if c0 < D:
            n = min(w, D - c0)
            out.append(make(x_hbm.at[:, pl.ds(c0, n)], pl.ds(c0, n)))
        if c0 + w > D:
            s = max(c0, D)
            out.append(make(dy_hbm.at[:, pl.ds(s - D, c0 + w - s)], pl.ds(s, c0 + w - s)))
        return out

    def cols(c):
        return pl.ds(*FWD[c])

    for c in range(3):
        local(idst_hbm, idst.at[c, coord[c]], loc_sem.at[0, c]).start()
    local(gatt_hbm, gatt.at[x], loc_sem.at[0, 3]).start()
    for c in range(3):
        for cp in slab_copies(c, lambda src, cs: local(src, gat.at[coord[c], :, cs], loc_sem.at[1, c])):
            cp.start()
    weights = [local(wg_hbm, wgu.at[:, first(F)], loc_sem.at[2, 0]), local(wu_hbm, wgu.at[:, pl.ds(F, F)], loc_sem.at[2, 1]),
               local(wd_hbm, wdn, loc_sem.at[2, 2])]
    for cp in weights:
        cp.start()
    with scope('entry'):
        pl.semaphore_wait(barrier, len(peers) + 1)
    for c in range(3):
        for k in (1, 3, 2):
            t = along(c, rmod(coord[c] + k))
            remote(idst_hbm, idst.at[c, coord[c]], meta_s.at[c, 0], meta_r.at[c, 0], t).start()
            if c == 0:
                remote(gatt_hbm, gatt.at[x], meta_s.at[c, 1], meta_r.at[c, 1], t).start()
    for d, k in enumerate((1, 3)):
        for c in range(3):
            t = along(c, rmod(coord[c] + k))
            for cp in slab_copies(c, lambda src, cs: remote(src, gat.at[coord[c], :, cs], g1_s.at[c, d], g1_r.at[c, d], t)):
                cp.start()
    for c in range(3):
        local(idst_hbm, idst.at[c, coord[c]], loc_sem.at[0, c]).wait()
    local(gatt_hbm, gatt.at[x], loc_sem.at[0, 3]).wait()

    tri = (iota((LANES, LANES), 0) < iota((LANES, LANES), 1)).astype(BF16)

    def plane_gid(c):
        p = iota((PLANE, 1), 0)
        a, b = p // SIDE, lax.rem(p, SIDE)
        return in_plane(c, a, b)

    def make_table(c, k):
        gids = plane_gid(c)
        carry = jnp.zeros((PLANE, 1), F32)
        for blk in range(NBLK):
            ls = pl.ds(blk * LANES, LANES)
            ids = idst[c, k, :, ls]
            member = jnp.zeros((PLANE, LANES), F32)
            w0 = jnp.zeros((PLANE, LANES), F32)
            w1 = jnp.zeros((PLANE, LANES), F32)
            for j in range(TOP_K):
                idj = ids[j:j + 1, :]
                e0 = idj == 2 * gids
                e1 = idj == 2 * gids + 1
                member = jnp.where(e0 | e1, 1.0, member)
                if c == 0:
                    gj = gatt[k, pl.ds(j, 1), ls]
                    w0 = jnp.where(e0, gj, w0)
                    w1 = jnp.where(e1, gj, w1)
            rank = dot(member.astype(BF16), tri) + carry
            carry = carry + over_lanes(member)
            slots[c, k, :, ls] = jnp.where(member > 0, rank, -1.0)
            if c == 0:
                gws[k, 0, :, ls] = w0
                gws[k, 1, :, ls] = w1

    with scope('own_tables'):
        for c in range(3):
            make_table(c, coord[c])

    def home_gid():
        v = iota((GROUPS, 1), 0)
        return lax.rem(v, PLANE) * SIDE + v // PLANE

    with scope('home_table'):
        carry = jnp.zeros((GROUPS, 1), F32)
        for blk in range(NBLK):
            ls = pl.ds(blk * LANES, LANES)
            member = jnp.zeros((GROUPS, LANES), F32)
            for j in range(TOP_K):
                member = jnp.where(idst[0, x, pl.ds(j, 1), ls] // 2 == home_gid(), 1.0, member)
            rank = dot(member.astype(BF16), tri) + carry
            carry = carry + over_lanes(member)
            slott[:, ls] = jnp.where(member > 0, rank, -1.0)

    for r in range(ROUNDS):
        mg[r] = jnp.zeros((PLANE, 1, LANES), F32)

    def gather(c, k, r):
        base = (iota((RS, 1), 0) + r * RS).astype(F32)
        lane = iota((RS, LANES), 1)
        row = iota((RS, 1), 0)

        for p in range(PLANE):
            mask = slots[c, k, pl.ds(p, 1), :] == base
            pbuf[pl.ds(p * RS, RS), :] = mask.astype(F32).astype(BF16)
            if c == 0:
                line = jnp.zeros((1, LANES), F32)
                for e in range(2):
                    col = over_lanes(jnp.where(mask, gws[k, e, pl.ds(p, 1), :], 0.0))
                    line = line + over_rows(jnp.where(lane == e * 64 + k * RS + row, col, 0.0))
                mg[r, p] = mg[r, p] + line
        c0, w = FWD[c]
        rows = dot(pbuf[...], gat[k, :, pl.ds(c0, w)]).astype(BF16)
        snd[r, :, k, :, pl.ds(c0, w)] = rows.reshape(PLANE, RS, w)

    for c in range(3):
        for cp in slab_copies(c, lambda src, cs: local(src, gat.at[coord[c], :, cs], loc_sem.at[1, c])):
            cp.wait()

    def own_gather(r, carry_):
        for c in range(3):
            gather(c, coord[c], r)
        return carry_

    with scope('own_gather'):
        lax.fori_loop(0, ROUNDS, own_gather, 0)
    acc[...] = jnp.zeros_like(acc)

    for c in range(3):
        proxy = idst.at[c, first(3)]
        local(proxy, proxy, meta_r.at[c, 0]).wait()
        local(proxy, proxy, meta_s.at[c, 0]).wait()
        if c == 0:
            proxy = gatt.at[first(3)]
            local(proxy, proxy, meta_r.at[c, 1]).wait()
            local(proxy, proxy, meta_s.at[c, 1]).wait()
    for c in range(3):
        for k in (1, 3, 2):
            with scope('far_table'):
                make_table(c, rmod(coord[c] + k))

    half = TOK // 2
    for d, k in enumerate((1, 3)):
        for c in range(3):
            src = rmod(coord[c] + SIDE - k)
            block = gat.at[src, :, cols(c)]
            with scope('wait_g1'):
                local(block, block, g1_r.at[c, d]).wait()
            t = along(c, rmod(coord[c] + k))
            part = gat.at[src, pl.ds(d * half, half), cols(c)]
            remote(part, part, g2_s.at[c, d], g2_r.at[c, d], t).start()
    def next_gather(r, i):
        off = jnp.where(i == 2, 2, SIDE - 1 - 2 * i)
        for c in range(3):
            gather(c, rmod(coord[c] + off), r)

    def send_round(r):
        for a, b in OFFS:
            for c in range(3):
                pa, pb = rmod(my_plane[c][0] + a), rmod(my_plane[c][1] + b)
                src = snd.at[r, pa * SIDE + pb, :, :, cols(c)]
                dst = (rx.at[l, r, z, y, :, :, cols(c)], rx.at[l, r, z, :, x, :, cols(c)], rx.at[l, r, :, y, x, :, cols(c)])[c]
                t = in_plane(c, pa, pb)
                remote(src, dst, f2_s.at[r, c], f2_r.at[r, c], t).start()
                if c == 0:
                    remote(mg.at[r, pa * SIDE + pb], mr.at[l, r, z * SIDE + y], mg_s.at[r], mg_r.at[r], t).start()
        for c in range(3):
            own = snd[r, my_p[c], :, :, cols(c)]
            if c == 0:
                rx[l, r, z, y, :, :, cols(c)] = own
            elif c == 1:
                rx[l, r, z, :, x, :, cols(c)] = own
            else:
                rx[l, r, :, y, x, :, cols(c)] = own
        mr[l, r, z * SIDE + y] = mg[r, my_p[0]]

    def proxy15(c, table):
        c0, w = table[c]
        return snd.at[0, first(PLANE - 1), :, :, first(w)]

    def wait_send(r):
        for c in range(3):
            local(proxy15(c, FWD), proxy15(c, FWD), f2_s.at[r, c]).wait()
        m = mg.at[r, first(PLANE - 1)]
        local(m, m, mg_s.at[r]).wait()

    def early(i, carry_):
        next_gather(i // 2, lax.rem(i, 2))
        return carry_

    with scope('near_gather'):
        lax.fori_loop(0, SIDE, early, 0)
    for c in range(3):
        for d in range(2):
            src = rmod(coord[c] + 2)
            part = gat.at[src, pl.ds(d * half, half), cols(c)]
            with scope('wait_g2'):
                local(part, part, g2_r.at[c, d]).wait()

    def late(r, carry_):
        def one(i, carry2):
            next_gather(r, i)
            return carry2

        with scope('late_gather'):
            lax.fori_loop(jnp.where(r < 2, 2, 0), 3, one, 0)
        with scope('send_round'):
            send_round(r)
        return carry_

    lax.fori_loop(0, ROUNDS, late, 0)
    for c in range(3):
        for d in range(2):
            part = gat.at[0, pl.ds(d * half, half), cols(c)]
            local(part, part, g2_s.at[c, d]).wait()
    for cp in weights:
        cp.wait()

    mine = (iota((64, LANES), 1) == l * 64 + iota((64, LANES), 0))

    ubuf = gat.at[0, first(512), first(D)]
    hd = gat.at[1, first(512), first(3 * F)]

    def chunk(r, kk):
        lp = jnp.where(kk < 2, l, other)
        z0 = lax.rem(kk, 2) * 2
        zs = pl.ds(z0, 2)

        def col(c0, w):
            return rx[lp, r, zs, :, :, :, pl.ds(c0, w)].reshape(512, w)

        for h in range(2):
            hs = pl.ds(h * WIDE, WIDE)
            for m in range(4):
                line = mr[lp, r, z0 * SIDE + 4 * h + m]
                gcol = over_lanes(jnp.where(mine, line, 0.0))
                part = rx[lp, r, z0 + h, m, :, :, pl.ds(D, D)].reshape(64, D)
                gat[0, pl.ds(h * WIDE + m * 64, 64), first(D)] = (gcol * part.astype(F32)).astype(BF16)
            ab = dot(rx[lp, r, z0 + h, :, :, :, first(D)].reshape(WIDE, D), wgu[...])
            dh = dot(ubuf[hs, :], wdn[...], 1, 1)
            a = ab[:, :F]
            b = ab[:, F:]
            sig = jax.nn.sigmoid(a)
            silu = a * sig
            hd[hs, first(F)] = (silu * b).astype(BF16)
            hd[hs, pl.ds(F, F)] = (dh * b * sig * (1.0 + a * (1.0 - sig))).astype(BF16)
            hd[hs, pl.ds(2 * F, F)] = (dh * silu).astype(BF16)
        dg = jnp.zeros((512, 1), F32)
        for n in range(4):
            o = dot(hd[:, first(F)], wdn[:, pl.ds(n * WIDE, WIDE)])
            dg = dg + over_lanes(col(D + n * WIDE, WIDE).astype(F32) * o)
        for m in range(8):
            line = over_rows(jnp.where(mine, dg[m * 64:(m + 1) * 64, :], 0.0))
            dgb[kk // 2, r, z0 * SIDE + m] = line
        acc[first(F), :] += dot(hd[:, first(F)], ubuf[...], 0, 0)
        for i in (1, 2):
            acc[pl.ds(i * F, F), :] += dot(hd[:, pl.ds(i * F, F)], col(0, D), 0, 0)
        for n in range(4):
            ns = pl.ds(n * WIDE, WIDE)
            cval = dot(hd[:, pl.ds(F, 2 * F)], wgu[ns, :], 1, 1).astype(BF16)

            @pl.when(kk < 2)
            def _():
                gat[2 + kk, first(512), ns] = cval

            @pl.when(kk >= 2)
            def _():
                rx[lp, r, zs, :, :, :, ns] = cval.reshape(2, SIDE, SIDE, RS, WIDE)

    def relay(r):
        for c, buf in enumerate((ia, ib, ic)):
            local(proxy15(c, BWD), proxy15(c, BWD), b1_r.at[r, c]).wait()
            own = buf.at[r, 0, 0]
            local(own, own, bl_s.at[r, c]).wait()
        m = dgi.at[r, first(PLANE - 1)]
        local(m, m, b1m_r.at[r]).wait()
        for p in range(PLANE):
            dgj[r, pl.ds(p, 1), :] = dgi[r, p]
        for k in (1, 3, 2):
            for c, buf in enumerate((ia, ib, ic)):
                to = rmod(coord[c] + k)
                cs = pl.ds(*BWD[c])
                dst = (rb.at[r, :, :, x, :, cs], rb.at[r, :, y, :, :, cs], rb.at[r, z, :, :, :, cs])[c]
                remote(buf.at[r, :, :, to], dst, b2_s.at[r, c], b2_r.at[r, c], along(c, to)).start()
                if c == 0:
                    remote(dgj.at[r], dgh.at[r, x], b2m_s.at[r], b2m_r.at[r], along(0, to)).start()
        dgh[r, x] = dgj[r]

    def round_body(r, carry_):
        for c in range(3):
            with scope('wait_f2'):
                local(proxy15(c, FWD), proxy15(c, FWD), f2_r.at[r, c]).wait()
        m = mg.at[0, first(PLANE - 1)]
        local(m, m, mg_r.at[r]).wait()
        for h in range(2):
            blk = rx.at[l, r, pl.ds(2 * h, 2)]
            remote(blk, blk, d2_s.at[r, h], d2_r.at[r, h], loc=other).start()
        remote(mr.at[l, r], mr.at[l, r], dm_s.at[r], dm_r.at[r], loc=other).start()

        def step(kk, carry2):
            @pl.when(kk >= 2)
            def _():
                blk = rx.at[other, r, pl.ds((kk - 2) * 2, 2)]
                with scope('wait_d2'):
                    local(blk, blk, d2_r.at[r, kk - 2]).wait()

            @pl.when(kk == 2)
            def _():
                local(mr.at[other, r], mr.at[other, r], dm_r.at[r]).wait()

            with scope('chunk'):
                chunk(r, kk)

            @pl.when(kk == 1)
            def _():
                for h in range(2):
                    sent = rx.at[l, r, pl.ds(2 * h, 2)]
                    local(sent, sent, d2_s.at[r, h]).wait()
                pl.semaphore_signal(credit.at[r], inc=1, device_id={'grp': g, 'loc': other}, device_id_type=MESH)

            @pl.when(kk == 2)
            def _():
                with scope('credit'):
                    pl.semaphore_wait(credit.at[r], 1)

            @pl.when(kk >= 2)
            def _():
                zs = pl.ds((kk - 2) * 2, 2)
                remote(rx.at[other, r, zs, :, :, :, first(D)], rx.at[other, r, zs, :, :, :, pl.ds(D, D)],
                       c_s.at[r, kk - 2], c_r.at[r, kk - 2], loc=other).start()
            return carry2

        lax.fori_loop(0, 4, step, 0)
        remote(dgb.at[1, r], dgr.at[r], dg_s.at[r], dg_r.at[r], loc=other).start()
        for h in range(2):
            blk = rx.at[l, r, pl.ds(2 * h, 2), :, :, :, pl.ds(D, D)]
            with scope('wait_c'):
                local(blk, blk, c_r.at[r, h]).wait()

            def add(zy, carry2):
                zz, yy = 2 * h + zy // SIDE, lax.rem(zy, SIDE)
                p0 = gat[2 + h, pl.ds(zy * 64, 64), first(D)].astype(F32).reshape(SIDE, RS, D)
                p1 = rx[l, r, zz, yy, :, :, pl.ds(D, D)].astype(F32)
                rx[l, r, zz, yy, :, :, first(D)] = (p0 + p1).astype(BF16)
                return carry2

            with scope('add'):
                lax.fori_loop(0, 8, add, 0)
        local(dgr.at[r], dgr.at[r], dg_r.at[r]).wait()
        dgb[0, r] = dgb[0, r] + dgr[r]
        for c, buf in enumerate((ia, ib, ic)):
            cs = pl.ds(*BWD[c])
            src = (rx.at[l, r, z, y, :, :, cs], rx.at[l, r, z, :, x, :, cs], rx.at[l, r, :, y, x, :, cs])[c]
            local(src, buf.at[r, my_plane[c][0], my_plane[c][1]], bl_s.at[r, c]).start()
        for a, b in OFFS:
            for c, buf in enumerate((ia, ib, ic)):
                pa, pb = rmod(my_plane[c][0] + a), rmod(my_plane[c][1] + b)
                cs = pl.ds(*BWD[c])
                src = (rx.at[l, r, pa, pb, :, :, cs], rx.at[l, r, pa, :, pb, :, cs], rx.at[l, r, :, pa, pb, :, cs])[c]
                t = in_plane(c, pa, pb)
                remote(src, buf.at[r, my_plane[c][0], my_plane[c][1]], b1_s.at[r, c], b1_r.at[r, c], t).start()
                if c == 0:
                    remote(dgb.at[0, r, pa * SIDE + pb], dgi.at[r, my_p[0]], b1m_s.at[r], b1m_r.at[r], t).start()
        dgi[r, my_p[0]] = dgb[0, r, my_p[0]]
        return carry_

    lax.fori_loop(0, ROUNDS, round_body, 0)

    for r in range(2):
        with scope('relay'):
            relay(r)

    with scope('flush'):
        gat[1, first(F), first(D)] = acc[first(F), :].astype(BF16)
        gat[2, first(2 * F), first(D)] = acc[pl.ds(F, 2 * F), :].astype(BF16)
        outs = [local(gat.at[1, first(F), first(D)], dwd_hbm, out_s.at[0]),
                local(gat.at[2, first(F), first(D)], dwg_hbm, out_s.at[1]),
                local(gat.at[2, pl.ds(F, F), first(D)], dwu_hbm, out_s.at[2])]
        for cp in outs:
            cp.start()
        dgacc[...] = jnp.zeros_like(dgacc)
        acc[first(TOK), :] = jnp.zeros((TOK, D), F32)
        for r in range(ROUNDS):
            wait_send(r)
        slotn = slott[...].astype(BF16)
        glane = iota((GROUPS, GROUPS * RS), 1) // RS
        spread = (home_gid() == glane).astype(F32).astype(BF16)

    with scope('last_relay'):
        relay(ROUNDS - 1)

    for r in range(ROUNDS):
        with scope('pick'):
            want = (lax.rem(iota((1, GROUPS * RS), 1), RS) + r * RS).astype(F32)
            for n in range(4):
                ns = pl.ds(n * WIDE, WIDE)
                got = dot(slotn, spread[:, n * WIDE:(n + 1) * WIDE], 0, 0)
                gat[0, :, ns] = (got == want[:, n * WIDE:(n + 1) * WIDE]).astype(F32).astype(BF16)
        for c in range(3):
            own = snd.at[0, first(12), :, :, first(BWD[c][1])]
            with scope('wait_b2'):
                local(own, own, b2_r.at[r, c]).wait()
        m = dgh.at[r, first(3)]
        local(m, m, b2m_r.at[r]).wait()
        with scope('stage'):
            pieces = []
            for zy in range(PLANE):
                pieces.append(local(rb.at[r, zy // SIDE, zy % SIDE], snd.at[r, zy, :, :, first(D)], loc_sem.at[3, 0]))
            for cp in pieces:
                cp.start()
        with scope('dg'):
            for e in range(2):
                cur = dgacc[e]
                lines = jnp.zeros((GROUPS, RS), F32)
                for k in range(SIDE):
                    mine_k = dgh[r, :, :, pl.ds(e * 64 + k * RS, RS)].reshape(GROUPS, RS)
                    lines = jnp.where(x == k, mine_k, lines)
                for i in range(RS):
                    cur = jnp.where(slott[...] == float(r * RS + i), lines[:, i:i + 1], cur)
                dgacc[e] = cur
        with scope('own_pieces'):
            for cp in pieces:
                cp.wait()
            own_pieces = []
            for q in range(PLANE):
                a, b = q // SIDE, q % SIDE
                own_pieces.append(local(ia.at[r, a, b, x], snd.at[r, q, x, :, pl.ds(*BWD[0])], loc_sem.at[3, 1]))
                own_pieces.append(local(ib.at[r, a, b, y], snd.at[r, a * SIDE + y, b, :, pl.ds(*BWD[1])], loc_sem.at[3, 1]))
                own_pieces.append(local(ic.at[r, a, b, z], snd.at[r, z * SIDE + a, b, :, pl.ds(*BWD[2])], loc_sem.at[3, 1]))
            for cp in own_pieces:
                cp.start()
            for cp in own_pieces:
                cp.wait()
        with scope('combine'):
            for n in range(4):
                got = snd[r, :, :, :, pl.ds(n * WIDE, WIDE)].reshape(GROUPS * RS, WIDE)
                acc[first(TOK), pl.ds(n * WIDE, WIDE)] += dot(gat[0, :, first(D)], got)
    with scope('finish'):
        gat[3, :, first(D)] = acc[first(TOK), :].astype(BF16)
        dx_out = local(gat.at[3, :, first(D)], dx_hbm, out_s.at[3])
        dx_out.start()
        for j in range(TOP_K):
            idj = idst[0, x, pl.ds(j, 1), :]
            val = jnp.where(lax.rem(idj, 2) == 0, dgacc[0], dgacc[1])
            dgate_ref[pl.ds(j, 1), :] = over_rows(jnp.where(idj // 2 == home_gid(), val, 0.0))

    with scope('drain'):
        for c in range(3):
            for d in range(2):
                block = gat.at[0, :, cols(c)]
                local(block, block, g1_s.at[c, d]).wait()
        for r in range(ROUNDS):
            local(mr.at[0, r], mr.at[0, r], dm_s.at[r]).wait()
            local(dgr.at[r], dgr.at[r], dg_s.at[r]).wait()
            for h in range(2):
                blk = rx.at[0, r, pl.ds(2 * h, 2), :, :, :, first(D)]
                local(blk, blk, c_s.at[r, h]).wait()
            for c in range(3):
                local(proxy15(c, BWD), proxy15(c, BWD), b1_s.at[r, c]).wait()
                own = snd.at[0, first(12), :, :, first(BWD[c][1])]
                local(own, own, b2_s.at[r, c]).wait()
            m = dgi.at[r, first(PLANE - 1)]
            local(m, m, b1m_s.at[r]).wait()
            m = dgh.at[r, first(3)]
            local(m, m, b2m_s.at[r]).wait()
        for cp in outs:
            cp.wait()
        dx_out.wait()


def solution(mesh):
    spec = P(('part', 'grp', 'loc'))

    def device_step(x_rows, dy_rows, expert_ids, gate_vals, w_gate, w_up, w_down):
        any_ = pl.BlockSpec(memory_space=pl.ANY)
        vmem = pl.BlockSpec(memory_space=pltpu.VMEM)
        dma = pltpu.SemaphoreType.DMA
        sd = jax.ShapeDtypeStruct
        out = pl.pallas_call(
            kernel,
            name='moe_backward',
            in_specs=[any_] * 7,
            out_specs=[any_, vmem] + [any_] * 7,
            out_shape=[sd((TOK, D), BF16), sd((TOP_K, TOK), F32), sd((F, D), BF16), sd((F, D), BF16), sd((F, D), BF16),
                       sd((ROUNDS, SIDE, SIDE, SIDE, RS, BWD[0][1]), BF16), sd((ROUNDS, SIDE, SIDE, SIDE, RS, BWD[1][1]), BF16),
                       sd((ROUNDS, SIDE, SIDE, SIDE, RS, BWD[2][1]), BF16), sd((ROUNDS, SIDE, SIDE, SIDE, RS, D), BF16)],
            scratch_shapes=[
                pltpu.VMEM((SIDE, TOK, 2 * D), BF16),
                pltpu.VMEM((ROUNDS, PLANE, SIDE, RS, 2 * D), BF16),
                pltpu.VMEM((2, ROUNDS, SIDE, SIDE, SIDE, RS, 2 * D), BF16),
                pltpu.VMEM((D, 2 * F), BF16),
                pltpu.VMEM((F, D), BF16),
                pltpu.VMEM((3 * F, D), F32),
                pltpu.VMEM((PLANE * RS, TOK), BF16),
                pltpu.VMEM((3, SIDE, PLANE, TOK), F32),
                pltpu.VMEM((SIDE, 2, PLANE, TOK), F32),
                pltpu.VMEM((GROUPS, TOK), F32),
                pltpu.VMEM((3, SIDE, TOP_K, TOK), jnp.int32),
                pltpu.VMEM((SIDE, TOP_K, TOK), F32),
                pltpu.VMEM((ROUNDS, PLANE, 1, LANES), F32),
                pltpu.VMEM((2, ROUNDS, PLANE, 1, LANES), F32),
                pltpu.VMEM((2, ROUNDS, PLANE, 1, LANES), F32),
                pltpu.VMEM((ROUNDS, PLANE, 1, LANES), F32),
                pltpu.VMEM((ROUNDS, PLANE, 1, LANES), F32),
                pltpu.VMEM((ROUNDS, PLANE, LANES), F32),
                pltpu.VMEM((ROUNDS, SIDE, PLANE, LANES), F32),
                pltpu.VMEM((2, GROUPS, TOK), F32),
                dma((4, 4)), *[dma((3, 2))] * 6, *[dma((ROUNDS, 3))] * 2, *[dma((ROUNDS,))] * 2, *[dma((ROUNDS, 2))] * 2,
                *[dma((ROUNDS,))] * 2, *[dma((ROUNDS, 2))] * 2, *[dma((ROUNDS,))] * 2, *[dma((ROUNDS, 3))] * 2,
                *[dma((ROUNDS,))] * 2, *[dma((ROUNDS, 3))] * 3, *[dma((ROUNDS,))] * 2, dma((4,)),
                pltpu.SemaphoreType.REGULAR((ROUNDS,)),
            ],
            compiler_params=pltpu.CompilerParams(collective_id=0, has_side_effects=True, vmem_limit_bytes=67043328),
        )(x_rows, dy_rows, expert_ids.T, gate_vals.T, w_gate[0], w_up[0], w_down[0])
        dx, d_gates, dwg_t, dwu_t, dwd = out[:5]
        return dx, d_gates.T, dwg_t.T[None], dwu_t.T[None], dwd[None]

    return jax.shard_map(device_step, mesh=mesh, in_specs=(spec,) * 7, out_specs=(spec,) * 5, check_vma=False)
```

time: 294 us -> 254 us (0.86)
  the two profiles are of different devices: /device:TPU:0 before, /device:TPU:92 now
where the time goes in v2:
time: 254 us; the launch traced here: 253 us
  Pallas kernels  246 us (97%)
  local copies, waits for them, and re-layouts  6.24 us (2%)
    pallas_call x1, Pallas kernels, device_step(): pl.pallas_call(kernel, name='moe_backward', in_specs=[any_] * 7, out_spec...  246 us
    unnamed x13, local copies, waits for them, and re-layouts  6.24 us

profile of v2, /device:TPU:92, one launch (start us, length us, event | category | flops | bytes accessed | tf_op | source)
XLA Modules:
  0.0 253.4 jit_solution(9256616461024600698)
XLA Ops:
  0.6 246.5 %moe_backward.1 = (bf16[768,1024]{1,0:T(8,128)(2,1)}, f32[8,768]{1,0:T(8,128)}, bf16[384,1024]{1,0:T(8,128)(2,1)}, bf16[384,1024]{1,0:T(8,128)(2,1)}, bf16[384,1...) custom-call(bf16[768,1024]{1,0:T(8,128)(2,1)} %x_hbm.1, ...), custom_call_target="tpu_custom_call" | custom-call | tf_op jit(solution)/shard_map/moe_backward/pallas_call | solution.py:578
  247.1 0.0 copy-start.2
  247.1 0.0 copy-start
  247.1 2.4 copy.12
  249.6 0.0 copy-done.2
  249.6 1.2 copy.13
  250.7 0.0 copy-done
  250.7 0.0 copy-start.3
  250.7 0.0 copy-start.1
  250.7 1.1 copy.17
  251.9 0.0 copy-done.3
  251.9 0.6 copy.18
  252.5 0.0 copy-done.1
  252.5 0.9 copy.19
Async XLA Ops:
  247.1 2.5 copy-start.2
  247.1 3.6 %copy-start = (bf16[768,1024]{1,0:T(8,128)(2,1)S(1)}, bf16[768,1024]{1,0:T(8,128)(2,1)}, u32[]{:S(2)}) copy-start(bf16[768,1024]{1,0:T(8,128)(2,1)} %get-tuple-element.25) | copy-start | bytes 4718596
  250.7 1.1 copy-start.3
  250.7 1.8 copy-start.1

commit v3 on v2

v3 whole, which is shorter than its diff:
```python
import jax
import jax.numpy as jnp
from jax import lax
from jax.experimental import pallas as pl
from jax.experimental.pallas import tpu as pltpu
from jax.sharding import PartitionSpec as P

MESH = pl.DeviceIdType.MESH
F32 = jnp.float32
BF16 = jnp.bfloat16
LANES = 128
WIDE = 256
SIDE = 4
PLANE = SIDE * SIDE
GROUPS = SIDE ** 3
TOK = 768
HALF = TOK // 2
TOP_K = 8
D = 1024
F = 384
SLOTS = 48
ROUNDS = 3
RS = SLOTS // ROUNDS
LINE = SIDE * RS
CH = 2 * PLANE * RS
NBLK = TOK // LANES
FWD = ((0, 640), (640, 640), (1280, 768))
BWD = ((0, 384), (384, 384), (768, 256))
AXES = ((1, 2), (2, 0), (0, 1))
NEAR = (1, 3, 2)
scope = jax.named_scope


def dot(a, b, ca=1, cb=0):
    return lax.dot_general(a, b, (((ca,), (cb,)), ((), ())), preferred_element_type=F32)


def first(n):
    return pl.ds(0, n)


def over_lanes(v):
    return jnp.sum(v, axis=1, keepdims=True)


def over_rows(v):
    return jnp.sum(v, axis=0, keepdims=True)


def iota(shape, dim):
    return lax.broadcasted_iota(jnp.int32, shape, dim)


def onehot(mask):
    return mask.astype(F32).astype(BF16)


def kernel(x_hbm, dy_hbm, idst_hbm, gatt_hbm, wg_hbm, wu_hbm, wd_hbm,
           dx_hbm, dgate_ref, dwg_hbm, dwu_hbm, dwd_hbm, ja, jb, jc, ia, ib, ic,
           gat, snd, rx, wgu, wdn, acc, hd, pbuf, slott, idst, gatt, mg, jm, mr, dgb, dgr, km, dgi, dgj, dgh, dgacc,
           loc_sem, out_sem, meta_s, meta_r, g1_s, g1_r, g2_s, g2_r, fa_s, fa_r, fb_s, fb_r, fl, fm_s, fm_r,
           d2_s, d2_r, c_s, c_r, dm_s, dm_r, ba_s, ba_r, bb_s, bb_r, bc_s, bc_r, bl, bm_s, bm_r, credit, free):
    g = lax.axis_index('grp')
    l = lax.axis_index('loc')
    z, y, x = g // PLANE, (g // SIDE) % SIDE, g % SIDE
    coord = (x, y, z)
    other = 1 - l

    def rmod(v):
        return lax.rem(v, SIDE)

    def gid(zz, yy, xx):
        return zz * PLANE + yy * SIDE + xx

    def along(axis, k):
        return gid(*(k if a == axis else coord[a] for a in (2, 1, 0)))

    def in_plane(c, a, b):
        at = {c: coord[c], AXES[c][0]: a, AXES[c][1]: b}
        return gid(at[2], at[1], at[0])

    def remote(src, dst, ss, rs, grp=g, loc=l):
        return pltpu.make_async_remote_copy(src, dst, ss, rs, device_id={'grp': grp, 'loc': loc}, device_id_type=MESH)

    def local(src, dst, sem):
        return pltpu.make_async_copy(src, dst, sem)

    def wait(ref, sem):
        local(ref, ref, sem).wait()

    neighbours = [along(axis, rmod(coord[axis] + k)) for axis in range(3) for k in NEAR]

    barrier = pltpu.get_barrier_semaphore()
    for p in neighbours:
        pl.semaphore_signal(barrier, inc=1, device_id={'grp': p, 'loc': l}, device_id_type=MESH)
    pl.semaphore_signal(barrier, inc=1, device_id={'grp': g, 'loc': other}, device_id_type=MESH)

    def slab_copies(c, rows, make):
        c0, w = FWD[c]
        out = []
        if c0 < D:
            n = min(w, D - c0)
            out.append(make(x_hbm.at[rows, pl.ds(c0, n)], pl.ds(c0, n)))
        if c0 + w > D:
            s = max(c0, D)
            out.append(make(dy_hbm.at[rows, pl.ds(s - D, c0 + w - s)], pl.ds(s, c0 + w - s)))
        return out

    def cols(c):
        return pl.ds(*FWD[c])

    def own_slab(c):
        return slab_copies(c, first(TOK), lambda src, cs: local(src, gat.at[coord[c], :, cs], loc_sem.at[1, c]))

    routing = [local(idst_hbm, idst.at[c, coord[c]], loc_sem.at[0, c]) for c in range(3)]
    routing.append(local(gatt_hbm, gatt.at[x], loc_sem.at[0, 3]))
    weights = [local(wg_hbm, wgu.at[:, first(F)], loc_sem.at[2, 0]), local(wu_hbm, wgu.at[:, pl.ds(F, F)], loc_sem.at[2, 1]),
               local(wd_hbm, wdn, loc_sem.at[2, 2])]
    for cp in routing + own_slab(0) + own_slab(1) + own_slab(2) + weights:
        cp.start()
    with scope('entry'):
        pl.semaphore_wait(barrier, len(neighbours) + 1)

    for c in range(3):
        for k in NEAR:
            t = along(c, rmod(coord[c] + k))
            remote(idst_hbm, idst.at[c, coord[c]], meta_s.at[c, 0], meta_r.at[c, 0], t).start()
            if c == 0:
                remote(gatt_hbm, gatt.at[x], meta_s.at[c, 1], meta_r.at[c, 1], t).start()
    for i in range(2):
        for d, k in enumerate((1, 3)):
            h = (d + i) % 2
            rows = pl.ds(h * HALF, HALF)
            for c in range(3):
                t = along(c, rmod(coord[c] + k))
                for cp in slab_copies(c, rows, lambda src, cs: remote(src, gat.at[coord[c], rows, cs], g1_s.at[c, d, h],
                                                                      g1_r.at[c, d, h], t)):
                    cp.start()
    for cp in routing:
        cp.wait()

    tri = onehot(iota((LANES, LANES), 0) < iota((LANES, LANES), 1))
    tables = 3 * SIDE * PLANE

    def table(c, k, p):
        return acc.at[pl.ds((c * SIDE + k) * PLANE + p, 1), first(TOK)]

    def gates(k, e, p):
        return acc.at[pl.ds(tables + (k * 2 + e) * PLANE + p, 1), first(TOK)]

    def make_table(c, k):
        p = iota((PLANE, 1), 0)
        gids = in_plane(c, p // SIDE, rmod(p))
        carry = jnp.zeros((PLANE, 1), F32)
        for blk in range(NBLK):
            ls = pl.ds(blk * LANES, LANES)
            ids = idst[c, k, :, ls]
            member = jnp.zeros((PLANE, LANES), F32)
            w0 = jnp.zeros((PLANE, LANES), F32)
            w1 = jnp.zeros((PLANE, LANES), F32)
            for j in range(TOP_K):
                idj = ids[j:j + 1, :]
                e0 = idj == 2 * gids
                e1 = idj == 2 * gids + 1
                member = jnp.where(e0 | e1, 1.0, member)
                if c == 0:
                    gj = gatt[k, pl.ds(j, 1), ls]
                    w0 = jnp.where(e0, gj, w0)
                    w1 = jnp.where(e1, gj, w1)
            rank = dot(member.astype(BF16), tri) + carry
            carry = carry + over_lanes(member)
            acc[pl.ds((c * SIDE + k) * PLANE, PLANE), ls] = jnp.where(member > 0, rank, -1.0)
            if c == 0:
                acc[pl.ds(tables + k * 2 * PLANE, PLANE), ls] = w0
                acc[pl.ds(tables + (k * 2 + 1) * PLANE, PLANE), ls] = w1

    with scope('own_tables'):
        for c in range(3):
            make_table(c, coord[c])

    def home_gid():
        v = iota((GROUPS, 1), 0)
        return lax.rem(v, PLANE) * SIDE + v // PLANE

    with scope('home_table'):
        carry = jnp.zeros((GROUPS, 1), F32)
        for blk in range(NBLK):
            ls = pl.ds(blk * LANES, LANES)
            member = jnp.zeros((GROUPS, LANES), F32)
            for j in range(TOP_K):
                member = jnp.where(idst[0, x, pl.ds(j, 1), ls] // 2 == home_gid(), 1.0, member)
            rank = dot(member.astype(BF16), tri) + carry
            carry = carry + over_lanes(member)
            slott[:, ls] = jnp.where(member > 0, rank, -1.0)

    for r in range(ROUNDS):
        mg[r] = jnp.zeros((SIDE, SIDE, 1, LANES), F32)

    def gather(c, k, r):
        base = (iota((RS, 1), 0) + r * RS).astype(F32)
        lane = iota((RS, LANES), 1)
        row = iota((RS, 1), 0)
        for p in range(PLANE):
            mask = table(c, k, p)[...] == base
            pbuf[pl.ds(p * RS, RS), :] = onehot(mask)
            if c == 0:
                line = jnp.zeros((1, LANES), F32)
                for e in range(2):
                    col = over_lanes(jnp.where(mask, gates(k, e, p)[...], 0.0))
                    line = line + over_rows(jnp.where(lane == e * LINE + k * RS + row, col, 0.0))
                mg[r, p // SIDE, p % SIDE] = mg[r, p // SIDE, p % SIDE] + line
        rows = dot(pbuf[...], gat[k, :, cols(c)]).astype(BF16).reshape(SIDE, SIDE, RS, FWD[c][1])
        if c == 2:
            snd[r, :, k, :, :, cols(c)] = rows
        else:
            snd[r, :, :, k, :, cols(c)] = rows

    for c in range(3):
        for cp in own_slab(c):
            cp.wait()

    def own_gather(r, carry_):
        for c in range(3):
            gather(c, coord[c], r)
        return carry_

    with scope('own_gather'):
        lax.fori_loop(0, ROUNDS, own_gather, 0)

    for c in range(3):
        wait(idst.at[c, first(3)], meta_r.at[c, 0])
        wait(idst.at[c, first(3)], meta_s.at[c, 0])
    wait(gatt.at[first(3)], meta_r.at[0, 1])
    wait(gatt.at[first(3)], meta_s.at[0, 1])
    with scope('far_table'):
        for c in range(3):
            for k in NEAR:
                make_table(c, rmod(coord[c] + k))

    def part(c, k, h):
        return gat.at[k, pl.ds(h * HALF, HALF), cols(c)]

    for d, k in enumerate((1, 3)):
        for c in range(3):
            src = rmod(coord[c] + SIDE - k)
            with scope('wait_g1'):
                wait(part(c, src, d), g1_r.at[c, d, d])
            remote(part(c, src, d), part(c, src, d), g2_s.at[c, d], g2_r.at[c, d], along(c, rmod(coord[c] + k))).start()
    for d, k in enumerate((1, 3)):
        for c in range(3):
            with scope('wait_g1b'):
                wait(part(c, rmod(coord[c] + SIDE - k), 1 - d), g1_r.at[c, d, 1 - d])

    def next_gather(r, i):
        off = jnp.where(i == 2, 2, SIDE - 1 - 2 * i)
        for c in range(3):
            gather(c, rmod(coord[c] + off), r)

    def early(i, carry_):
        next_gather(i // 2, lax.rem(i, 2))
        return carry_

    with scope('near_gather'):
        lax.fori_loop(0, SIDE, early, 0)
    for c in range(3):
        for d in range(2):
            with scope('wait_g2'):
                wait(part(c, rmod(coord[c] + 2), d), g2_r.at[c, d])

    def plane_hop(r):
        for c, buf in enumerate((ja, jb, jc)):
            axis = AXES[c][0]
            dst = buf.at[r, :, coord[axis], :, :, :] if c == 2 else buf.at[r, coord[axis]]
            for k in NEAR:
                to = rmod(coord[axis] + k)
                remote(snd.at[r, to, :, :, :, cols(c)], dst, fa_s.at[r, c], fa_r.at[r, c], along(axis, to)).start()
                if c == 0:
                    remote(mg.at[r, to], jm.at[r, y], fm_s.at[0, r], fm_r.at[0, r], along(axis, to)).start()
            local(snd.at[r, coord[axis], :, :, :, cols(c)], dst, fl.at[0, r, c]).start()
        jm[r, y] = mg[r, y]

    def blocks(n, w):
        return snd.at[0, first(n), :, :, :, first(w)]

    def pass_on(r):
        for c, buf in enumerate((ja, jb, jc)):
            axis = AXES[c][1]
            w = FWD[c][1]
            with scope('wait_fa'):
                wait(blocks(3, w), fa_r.at[r, c])
            wait(blocks(1, w), fl.at[0, r, c])
            dst = (rx.at[l, r, z, :, :, :, cols(c)], rx.at[l, r, :, :, x, :, cols(c)], rx.at[l, r, :, y, :, :, cols(c)])[c]
            if c == 0:
                wait(mg.at[0, first(3)], fm_r.at[0, r])
            for k in (*NEAR, 0):
                to = rmod(coord[axis] + k)
                src = buf.at[r, :, :, to] if c == 2 else buf.at[r, :, to]
                if k:
                    remote(src, dst, fb_s.at[r, c], fb_r.at[r, c], along(axis, to)).start()
                    if c == 0:
                        remote(jm.at[r, :, to], mr.at[l, r, z], fm_s.at[1, r], fm_r.at[1, r], along(axis, to)).start()
                else:
                    local(src, dst, fl.at[1, r, c]).start()
        mr[l, r, z] = jm[r, :, z]
        for c in range(3):
            wait(blocks(3, FWD[c][1]), fa_s.at[r, c])
        wait(mg.at[0, first(3)], fm_s.at[0, r])
        for p in neighbours:
            pl.semaphore_signal(free.at[r], inc=1, device_id={'grp': p, 'loc': l}, device_id_type=MESH)

    def late(r, carry_):
        def one(i, carry2):
            next_gather(r, i)
            return carry2

        with scope('late_gather'):
            lax.fori_loop(jnp.where(r < 2, 2, 0), 3, one, 0)

        @pl.when(r < 2)
        def _():
            plane_hop(r)
        return carry_

    lax.fori_loop(0, ROUNDS, late, 0)
    with scope('pass_on'):
        pass_on(0)
    plane_hop(2)
    with scope('pass_on'):
        pass_on(1)
    for c in range(3):
        for d in range(2):
            wait(part(c, 0, d), g2_s.at[c, d])
            for h in range(2):
                wait(part(c, 0, d), g1_s.at[c, d, h])
    acc[...] = jnp.zeros_like(acc)
    for cp in weights:
        cp.wait()

    mine = (iota((LINE, LANES), 1) == l * LINE + iota((LINE, LANES), 0))
    ubuf = gat.at[0, first(CH), pl.ds(D, D)]

    def result(kk, n=first(D)):
        return gat.at[kk, first(CH), n]

    def chunk(r, kk):
        who, half = kk // 2, lax.rem(kk, 2)
        lp = jnp.where(who == 0, l, other)
        z0 = half * 2
        zs = pl.ds(z0, 2)

        def col(c0, w):
            return rx[lp, r, zs, :, :, :, pl.ds(c0, w)].reshape(CH, w)

        for m in range(2 * SIDE):
            zz, yy = z0 + m // SIDE, m % SIDE
            gcol = over_lanes(jnp.where(mine, mr[lp, r, zz, yy], 0.0))
            rows = rx[lp, r, zz, yy, :, :, pl.ds(D, D)].reshape(LINE, D)
            ubuf[pl.ds(m * LINE, LINE), :] = (gcol * rows.astype(F32)).astype(BF16)
        for h in range(2):
            hs = pl.ds(h * WIDE, WIDE)
            ab = dot(rx[lp, r, z0 + h, :, :, :, first(D)].reshape(WIDE, D), wgu[...])
            dh = dot(ubuf[hs, :], wdn[...], 1, 1)
            a = ab[:, :F]
            b = ab[:, F:]
            sig = jax.nn.sigmoid(a)
            silu = a * sig
            hd[hs, first(F)] = (silu * b).astype(BF16)
            hd[hs, pl.ds(F, F)] = (dh * b * sig * (1.0 + a * (1.0 - sig))).astype(BF16)
            hd[hs, pl.ds(2 * F, F)] = (dh * silu).astype(BF16)
        dg = jnp.zeros((CH, 1), F32)
        for n in range(4):
            o = dot(hd[:, first(F)], wdn[:, pl.ds(n * WIDE, WIDE)])
            dg = dg + over_lanes(col(D + n * WIDE, WIDE).astype(F32) * o)
        for m in range(2 * SIDE):
            line = over_rows(jnp.where(mine, dg[m * LINE:(m + 1) * LINE, :], 0.0))
            dgb[who, r, z0 + m // SIDE, m % SIDE] = line
        acc[first(F), :] += dot(hd[:, first(F)], ubuf[...], 0, 0)
        for i in (1, 2):
            acc[pl.ds(i * F, F), :] += dot(hd[:, pl.ds(i * F, F)], col(0, D), 0, 0)
        for n in range(4):
            cval = dot(hd[:, pl.ds(F, 2 * F)], wgu[pl.ds(n * WIDE, WIDE), :], 1, 1)
            result(kk, pl.ds(n * WIDE, WIDE))[...] = cval.astype(BF16)

    def home_first(r):
        pl.semaphore_wait(free.at[r], len(neighbours))
        for c in range(3):
            axis = AXES[c][1]
            cs = pl.ds(*BWD[c])
            dst = snd.at[r, coord[axis], :, :, :, pl.ds(D + BWD[c][0], BWD[c][1])]
            for k in (*NEAR, 0):
                to = rmod(coord[axis] + k)
                src = (rx.at[l, r, to, :, :, :, cs], rx.at[l, r, :, :, to, :, cs], rx.at[l, r, :, to, :, :, cs])[c]
                if k:
                    remote(src, dst, ba_s.at[r, c], ba_r.at[r, c], along(axis, to)).start()
                    if c == 0:
                        remote(dgb.at[0, r, to], km.at[r, z], bm_s.at[0, r], bm_r.at[0, r], along(axis, to)).start()
                else:
                    dst[...] = src[...]
        km[r, z] = dgb[0, r, z]

    def home_second(r):
        for c, buf in enumerate((ia, ib, ic)):
            axis = AXES[c][0]
            with scope('wait_ba'):
                wait(blocks(3, BWD[c][1]), ba_r.at[r, c])
            if c == 0:
                wait(mg.at[0, first(3)], bm_r.at[0, r])
            dst = buf.at[r, coord[axis]] if c == 1 else buf.at[r, :, coord[axis]]
            cs = pl.ds(D + BWD[c][0], BWD[c][1])
            for k in (*NEAR, 0):
                to = rmod(coord[axis] + k)
                src = snd.at[r, :, :, to, :, cs] if c == 2 else snd.at[r, :, to, :, :, cs]
                if k:
                    remote(src, dst, bb_s.at[r, c], bb_r.at[r, c], along(axis, to)).start()
                    if c == 0:
                        remote(km.at[r, :, to], dgi.at[r, :, y], bm_s.at[1, r], bm_r.at[1, r], along(axis, to)).start()
                else:
                    local(src, dst, bl.at[0, r, c]).start()
        dgi[r, :, y] = km[r, :, y]

    def home_third(r):
        for c, buf in enumerate((ia, ib, ic)):
            with scope('wait_bb'):
                wait(blocks(3, BWD[c][1]), bb_r.at[r, c])
            wait(blocks(1, BWD[c][1]), bl.at[0, r, c])
            if c == 0:
                wait(mg.at[0, first(3)], bm_r.at[1, r])
                for p in range(PLANE):
                    dgj[r, pl.ds(p, 1), :] = dgi[r, p // SIDE, p % SIDE]
            cs = pl.ds(*BWD[c])
            dst = (snd.at[r, :, :, x, :, cs], snd.at[r, :, y, :, :, cs], snd.at[r, z, :, :, :, cs])[c]
            for k in (*NEAR, 0):
                to = rmod(coord[c] + k)
                src = buf.at[r, :, :, to]
                if k:
                    remote(src, dst, bc_s.at[r, c], bc_r.at[r, c], along(c, to)).start()
                    if c == 0:
                        remote(dgj.at[r], dgh.at[r, x], bm_s.at[2, r], bm_r.at[2, r], along(c, to)).start()
                else:
                    local(src, dst, bl.at[1, r, c]).start()
        dgh[r, x] = dgj[r]

    hooks = (((0, 3), 'pass_on2', lambda: pass_on(2)), ((2, 0), 'home_second0', lambda: home_second(0)),
             ((2, 2), 'home_second1', lambda: home_second(1)), ((2, 3), 'home_third0', lambda: home_third(0)))

    def round_body(r, carry_):
        for c in range(3):
            with scope('wait_fb'):
                wait(blocks(3, FWD[c][1]), fb_r.at[r, c])
            wait(blocks(1, FWD[c][1]), fl.at[1, r, c])
        wait(mg.at[0, first(3)], fm_r.at[1, r])
        for h in range(2):
            blk = rx.at[l, r, pl.ds(2 * h, 2)]
            remote(blk, blk, d2_s.at[r, h], d2_r.at[r, h], loc=other).start()
        remote(mr.at[l, r], mr.at[l, r], dm_s.at[0, r], dm_r.at[0, r], loc=other).start()

        def step(kk, carry2):
            half = lax.rem(kk, 2)
            zs = pl.ds(half * 2, 2)

            @pl.when(kk >= 2)
            def _():
                with scope('wait_d2'):
                    wait(rx.at[other, r, zs], d2_r.at[r, half])

            @pl.when(kk == 2)
            def _():
                wait(mr.at[other, r], dm_r.at[0, r])

            with scope('chunk'):
                chunk(r, kk)

            @pl.when(kk == 1)
            def _():
                for h in range(2):
                    wait(rx.at[l, r, pl.ds(2 * h, 2)], d2_s.at[r, h])
                pl.semaphore_signal(credit.at[r], inc=1, device_id={'grp': g, 'loc': other}, device_id_type=MESH)

            for (rr, at), name, hook in hooks:
                @pl.when((r == rr) & (kk == at))
                def _():
                    with scope(name):
                        hook()

            @pl.when(kk == 2)
            def _():
                with scope('credit'):
                    pl.semaphore_wait(credit.at[r], 1)

            @pl.when(kk >= 2)
            def _():
                rx[other, r, zs, :, :, :, first(D)] = result(kk)[...].reshape(2, SIDE, SIDE, RS, D)
                remote(rx.at[other, r, zs, :, :, :, first(D)], rx.at[other, r, zs, :, :, :, pl.ds(D, D)],
                       c_s.at[r, half], c_r.at[r, half], loc=other).start()
            return carry2

        lax.fori_loop(0, 4, step, 0)
        remote(dgb.at[1, r], dgr.at[r], dm_s.at[1, r], dm_r.at[1, r], loc=other).start()
        for h in range(2):
            with scope('wait_c'):
                wait(rx.at[l, r, pl.ds(2 * h, 2), :, :, :, pl.ds(D, D)], c_r.at[r, h])

            def add(zy, carry2):
                zz, yy = 2 * h + zy // SIDE, lax.rem(zy, SIDE)
                p0 = gat[h, pl.ds(zy * LINE, LINE), first(D)].astype(F32).reshape(SIDE, RS, D)
                p1 = rx[l, r, zz, yy, :, :, pl.ds(D, D)].astype(F32)
                rx[l, r, zz, yy, :, :, first(D)] = (p0 + p1).astype(BF16)
                return carry2

            with scope('add'):
                lax.fori_loop(0, 2 * SIDE, add, 0)
        wait(dgr.at[r], dm_r.at[1, r])
        dgb[0, r] = dgb[0, r] + dgr[r]
        with scope('home_first'):
            home_first(r)
        return carry_

    lax.fori_loop(0, ROUNDS, round_body, 0)

    with scope('flush'):
        gat[1, first(F), first(D)] = acc[first(F), :].astype(BF16)
        gat[2, first(2 * F), first(D)] = acc[pl.ds(F, 2 * F), :].astype(BF16)
        outs = [local(gat.at[1, first(F), first(D)], dwd_hbm, out_sem.at[0]),
                local(gat.at[2, first(F), first(D)], dwg_hbm, out_sem.at[1]),
                local(gat.at[2, pl.ds(F, F), first(D)], dwu_hbm, out_sem.at[2])]
        for cp in outs:
            cp.start()
        dgacc[...] = jnp.zeros_like(dgacc)
        acc[first(TOK), :] = jnp.zeros((TOK, D), F32)
        slotn = slott[...].astype(BF16)
        glane = iota((GROUPS, GROUPS * RS), 1) // RS
        spread = onehot(home_gid() == glane)
    with scope('home_third1'):
        home_third(1)
    with scope('home_second'):
        home_second(2)

    def combine(r):
        with scope('pick'):
            want = (lax.rem(iota((1, GROUPS * RS), 1), RS) + r * RS).astype(F32)
            for n in range(4):
                ns = pl.ds(n * WIDE, WIDE)
                got = dot(slotn, spread[:, n * WIDE:(n + 1) * WIDE], 0, 0)
                gat[0, :, ns] = onehot(got == want[:, n * WIDE:(n + 1) * WIDE])
        wait(dgh.at[r, first(3)], bm_r.at[2, r])
        with scope('dg'):
            for e in range(2):
                cur = dgacc[e]
                lines = jnp.zeros((GROUPS, RS), F32)
                for k in range(SIDE):
                    mine_k = dgh[r, :, :, pl.ds(e * LINE + k * RS, RS)].reshape(GROUPS, RS)
                    lines = jnp.where(x == k, mine_k, lines)
                for i in range(RS):
                    cur = jnp.where(slott[...] == float(r * RS + i), lines[:, i:i + 1], cur)
                dgacc[e] = cur
        for c in range(3):
            with scope('wait_bc'):
                wait(blocks(3, BWD[c][1]), bc_r.at[r, c])
            wait(blocks(1, BWD[c][1]), bl.at[1, r, c])
        with scope('combine'):
            for n in range(4):
                ns = pl.ds(n * WIDE, WIDE)
                acc[first(TOK), ns] += dot(gat[0, :, first(D)], snd[r, :, :, :, :, ns].reshape(GROUPS * RS, WIDE))

    combine(0)
    with scope('home_third2'):
        home_third(2)
    combine(1)
    combine(2)
    with scope('finish'):
        gat[3, :, first(D)] = acc[first(TOK), :].astype(BF16)
        dx_out = local(gat.at[3, :, first(D)], dx_hbm, out_sem.at[3])
        dx_out.start()
        for j in range(TOP_K):
            idj = idst[0, x, pl.ds(j, 1), :]
            val = jnp.where(lax.rem(idj, 2) == 0, dgacc[0], dgacc[1])
            dgate_ref[pl.ds(j, 1), :] = over_rows(jnp.where(idj // 2 == home_gid(), val, 0.0))

    with scope('drain'):
        for r in range(ROUNDS):
            for i in range(3):
                wait(dgh.at[0, first(3)] if i == 2 else mg.at[0, first(3)], bm_s.at[i, r])
            wait(mg.at[0, first(3)], fm_s.at[1, r])
            for i in range(2):
                wait(dgr.at[r], dm_s.at[i, r])
                wait(rx.at[0, r, first(2), :, :, :, first(D)], c_s.at[r, i])
            for c in range(3):
                wait(blocks(3, FWD[c][1]), fb_s.at[r, c])
                for sem in (ba_s, bb_s, bc_s):
                    wait(blocks(3, BWD[c][1]), sem.at[r, c])
        for cp in outs:
            cp.wait()
        dx_out.wait()


def solution(mesh):
    spec = P(('part', 'grp', 'loc'))

    def device_step(x_rows, dy_rows, expert_ids, gate_vals, w_gate, w_up, w_down):
        any_ = pl.BlockSpec(memory_space=pl.ANY)
        vmem = pl.BlockSpec(memory_space=pltpu.VMEM)
        dma = pltpu.SemaphoreType.DMA
        sd = jax.ShapeDtypeStruct
        cube = (ROUNDS, SIDE, SIDE, SIDE, RS)
        lines = (ROUNDS, SIDE, SIDE, 1, LANES)
        weight = sd((F, D), BF16)
        out = pl.pallas_call(
            kernel,
            name='moe_backward',
            in_specs=[any_] * 7,
            out_specs=[any_, vmem] + [any_] * 9,
            out_shape=[sd((TOK, D), BF16), sd((TOP_K, TOK), F32), weight, weight, weight,
                       *[sd((*cube, w), BF16) for _, w in FWD + BWD]],
            scratch_shapes=[
                pltpu.VMEM((SIDE, TOK, 2 * D), BF16),
                pltpu.VMEM((*cube, 2 * D), BF16),
                pltpu.VMEM((2, *cube, 2 * D), BF16),
                pltpu.VMEM((D, 2 * F), BF16),
                pltpu.VMEM((F, D), BF16),
                pltpu.VMEM((3 * F, D), F32),
                pltpu.VMEM((CH, 3 * F), BF16),
                pltpu.VMEM((PLANE * RS, TOK), BF16),
                pltpu.VMEM((GROUPS, TOK), F32),
                pltpu.VMEM((3, SIDE, TOP_K, TOK), jnp.int32),
                pltpu.VMEM((SIDE, TOP_K, TOK), F32),
                pltpu.VMEM(lines, F32),
                pltpu.VMEM(lines, F32),
                pltpu.VMEM((2, *lines), F32),
                pltpu.VMEM((2, *lines), F32),
                pltpu.VMEM(lines, F32),
                pltpu.VMEM(lines, F32),
                pltpu.VMEM(lines, F32),
                pltpu.VMEM((ROUNDS, PLANE, LANES), F32),
                pltpu.VMEM((ROUNDS, SIDE, PLANE, LANES), F32),
                pltpu.VMEM((2, GROUPS, TOK), F32),
                dma((3, 4)), dma((4,)), *[dma((3, 2))] * 2, *[dma((3, 2, 2))] * 2, *[dma((3, 2))] * 2,
                *[dma((ROUNDS, 3))] * 4, dma((2, ROUNDS, 3)), *[dma((2, ROUNDS))] * 2,
                *[dma((ROUNDS, 2))] * 4, *[dma((2, ROUNDS))] * 2, *[dma((ROUNDS, 3))] * 6, dma((2, ROUNDS, 3)),
                *[dma((3, ROUNDS))] * 2, *[pltpu.SemaphoreType.REGULAR((ROUNDS,))] * 2,
            ],
            compiler_params=pltpu.CompilerParams(collective_id=0, has_side_effects=True, vmem_limit_bytes=67043328),
        )(x_rows, dy_rows, expert_ids.T, gate_vals.T, w_gate[0], w_up[0], w_down[0])
        dx, d_gates, dwg_t, dwu_t, dwd = out[:5]
        return dx, d_gates.T, dwg_t.T[None], dwu_t.T[None], dwd[None]

    return jax.shard_map(device_step, mesh=mesh, in_specs=(spec,) * 7, out_specs=(spec,) * 5, check_vma=False)
```

time: 254 us -> 234 us (0.921)
  the two profiles are of different devices: /device:TPU:92 before, /device:TPU:0 now
where the time goes in v3:
time: 234 us; the launch traced here: 233 us
  Pallas kernels  225 us (96%)
  local copies, waits for them, and re-layouts  7.41 us (3%)
    pallas_call x1, Pallas kernels, device_step(): pl.pallas_call(kernel, name='moe_backward', in_specs=[any_] * 7, out_spec...  225 us
    unnamed x11, local copies, waits for them, and re-layouts  7.41 us

profile of v3, /device:TPU:0, one launch (start us, length us, event | category | flops | bytes accessed | tf_op | source)
XLA Modules:
  0.0 232.6 jit_solution(9220062680741664660)
XLA Ops:
  0.6 224.6 %moe_backward.1 = (bf16[768,1024]{1,0:T(8,128)(2,1)}, f32[8,768]{1,0:T(8,128)}, bf16[384,1024]{1,0:T(8,128)(2,1)}, bf16[384,1024]{1,0:T(8,128)(2,1)}, bf16[384,1...) custom-call(bf16[768,1024]{1,0:T(8,128)(2,1)} %x_hbm.1, ...), custom_call_target="tpu_custom_call" | custom-call | tf_op jit(solution)/shard_map/moe_backward/pallas_call | solution.py:607
  225.2 0.0 copy-start
  225.2 2.4 %copy.12 = bf16[1,1024,384]{2,1,0:T(8,128)(2,1)} copy(bf16[1,1024,384]{1,2,0:T(8,128)(2,1)} %bitcast.15) | data formatting | bytes 1572864
  227.6 0.0 copy-start.2
  227.6 0.0 copy-start.1
  227.6 2.4 %copy.13 = bf16[1,1024,384]{2,1,0:T(8,128)(2,1)} copy(bf16[1,1024,384]{1,2,0:T(8,128)(2,1)} %bitcast.14) | data formatting | bytes 1572864
  230.0 0.0 copy-done
  230.0 1.1 copy.17
  231.1 0.0 copy-done.2
  231.1 0.6 copy.18
  231.8 0.0 copy-done.1
  231.8 0.9 copy.19
Async XLA Ops:
  225.2 4.8 %copy-start = (bf16[768,1024]{1,0:T(8,128)(2,1)S(1)}, bf16[768,1024]{1,0:T(8,128)(2,1)}, u32[]{:S(2)}) copy-start(bf16[768,1024]{1,0:T(8,128)(2,1)} %get-tuple-element.25) | copy-start | bytes 4718596
  227.6 3.5 %copy-start.2 = (f32[8,768]{1,0:T(8,128)S(1)}, f32[8,768]{1,0:T(8,128)}, u32[]{:S(2)}) copy-start(f32[8,768]{1,0:T(8,128)} %get-tuple-element.11) | copy-start | bytes 73732
  227.6 4.1 %copy-start.1 = (bf16[384,1024]{1,0:T(8,128)(2,1)S(1)}, bf16[384,1024]{1,0:T(8,128)(2,1)}, u32[]{:S(2)}) copy-start(bf16[384,1024]{1,0:T(8,128)(2,1)} %get-tuple-element.14) | copy-start | bytes 2359300

commit v4 on v3

--- a/solution.py
+++ b/solution.py
@@ -19,10 +19,12 @@
 D = 1024
 F = 384
 SLOTS = 48
-ROUNDS = 3
+ROUNDS = 6
+PAIRS = ROUNDS // 2
 RS = SLOTS // ROUNDS
+GS = 2 * RS
 LINE = SIDE * RS
-CH = 2 * PLANE * RS
+CH = GROUPS * RS
 NBLK = TOK // LANES
 FWD = ((0, 640), (640, 640), (1280, 768))
 BWD = ((0, 384), (384, 384), (768, 256))
@@ -121,13 +123,7 @@
     with scope('entry'):
         pl.semaphore_wait(barrier, len(neighbours) + 1)
 
-    for c in range(3):
-        for k in NEAR:
-            t = along(c, rmod(coord[c] + k))
-            remote(idst_hbm, idst.at[c, coord[c]], meta_s.at[c, 0], meta_r.at[c, 0], t).start()
-            if c == 0:
-                remote(gatt_hbm, gatt.at[x], meta_s.at[c, 1], meta_r.at[c, 1], t).start()
-    for i in range(2):
+    def slab_send(i):
         for d, k in enumerate((1, 3)):
             h = (d + i) % 2
             rows = pl.ds(h * HALF, HALF)
@@ -136,6 +132,15 @@
                 for cp in slab_copies(c, rows, lambda src, cs: remote(src, gat.at[coord[c], rows, cs], g1_s.at[c, d, h],
                                                                       g1_r.at[c, d, h], t)):
                     cp.start()
+
+    slab_send(0)
+    for c in range(3):
+        for k in NEAR:
+            t = along(c, rmod(coord[c] + k))
+            remote(idst_hbm, idst.at[c, coord[c]], meta_s.at[c, 0], meta_r.at[c, 0], t).start()
+            if c == 0:
+                remote(gatt_hbm, gatt.at[x], meta_s.at[c, 1], meta_r.at[c, 1], t).start()
+    slab_send(1)
     for cp in routing:
         cp.wait()
 
@@ -196,94 +201,73 @@
     for r in range(ROUNDS):
         mg[r] = jnp.zeros((SIDE, SIDE, 1, LANES), F32)
 
-    def gather(c, k, r):
-        base = (iota((RS, 1), 0) + r * RS).astype(F32)
-        lane = iota((RS, LANES), 1)
-        row = iota((RS, 1), 0)
+    def gather(c, k, pair):
+        base = (iota((GS, 1), 0) + pair * GS).astype(F32)
+        row = iota((GS, LANES), 0)
+        at = iota((GS, LANES), 1) - k * RS - lax.rem(row, RS)
         for p in range(PLANE):
             mask = table(c, k, p)[...] == base
-            pbuf[pl.ds(p * RS, RS), :] = onehot(mask)
+            pbuf[pl.ds(p * GS, GS), :] = onehot(mask)
             if c == 0:
-                line = jnp.zeros((1, LANES), F32)
+                both = jnp.zeros((GS, LANES), F32)
                 for e in range(2):
                     col = over_lanes(jnp.where(mask, gates(k, e, p)[...], 0.0))
-                    line = line + over_rows(jnp.where(lane == e * LINE + k * RS + row, col, 0.0))
-                mg[r, p // SIDE, p % SIDE] = mg[r, p // SIDE, p % SIDE] + line
-        rows = dot(pbuf[...], gat[k, :, cols(c)]).astype(BF16).reshape(SIDE, SIDE, RS, FWD[c][1])
-        if c == 2:
-            snd[r, :, k, :, :, cols(c)] = rows
-        else:
-            snd[r, :, :, k, :, cols(c)] = rows
+                    both = jnp.where(at == e * LINE, col, both)
+                for i in range(2):
+                    line = over_rows(jnp.where(row // RS == i, both, 0.0))
+                    mg[2 * pair + i, p // SIDE, p % SIDE] = mg[2 * pair + i, p // SIDE, p % SIDE] + line
+        w = FWD[c][1]
+        rows = dot(pbuf[...], gat[k, :, cols(c)]).astype(BF16).reshape(SIDE, SIDE, 2, RS, w)
+        for i in range(2):
+            if c == 2:
+                snd[2 * pair + i, :, k, :, :, cols(c)] = rows[:, :, i]
+            else:
+                snd[2 * pair + i, :, :, k, :, cols(c)] = rows[:, :, i]
 
     for c in range(3):
         for cp in own_slab(c):
             cp.wait()
 
-    def own_gather(r, carry_):
-        for c in range(3):
-            gather(c, coord[c], r)
-        return carry_
-
-    with scope('own_gather'):
-        lax.fori_loop(0, ROUNDS, own_gather, 0)
-
-    for c in range(3):
-        wait(idst.at[c, first(3)], meta_r.at[c, 0])
-        wait(idst.at[c, first(3)], meta_s.at[c, 0])
-    wait(gatt.at[first(3)], meta_r.at[0, 1])
-    wait(gatt.at[first(3)], meta_s.at[0, 1])
-    with scope('far_table'):
-        for c in range(3):
-            for k in NEAR:
-                make_table(c, rmod(coord[c] + k))
+    hop_bufs = (ja, jb, jc)
+
+    def hop_part(r, c, k):
+        axis = AXES[c][0]
+        for off in NEAR:
+            to = rmod(coord[axis] + off)
+            if c == 2:
+                src, dst = snd.at[r, to, k, :, :, cols(c)], jc.at[r, k, coord[axis]]
+            else:
+                src, dst = snd.at[r, to, :, k, :, cols(c)], hop_bufs[c].at[r, coord[axis], :, k]
+            remote(src, dst, fa_s.at[r, c], fa_r.at[r, c], along(axis, to)).start()
+
+    def hop_dst(r, c):
+        axis = AXES[c][0]
+        return jc.at[r, :, coord[axis], :, :, :] if c == 2 else hop_bufs[c].at[r, coord[axis]]
+
+    def hop_rest(r):
+        for c in range(3):
+            local(snd.at[r, coord[AXES[c][0]], :, :, :, cols(c)], hop_dst(r, c), fl.at[0, r, c]).start()
+        for off in NEAR:
+            to = rmod(y + off)
+            remote(mg.at[r, to], jm.at[r, y], fm_s.at[0, r], fm_r.at[0, r], along(AXES[0][0], to)).start()
+        jm[r, y] = mg[r, y]
+
+    def plane_hop(r):
+        for c in range(3):
+            axis = AXES[c][0]
+            for off in NEAR:
+                to = rmod(coord[axis] + off)
+                remote(snd.at[r, to, :, :, :, cols(c)], hop_dst(r, c), fa_s.at[r, c], fa_r.at[r, c], along(axis, to)).start()
+        hop_rest(r)
 
     def part(c, k, h):
         return gat.at[k, pl.ds(h * HALF, HALF), cols(c)]
 
-    for d, k in enumerate((1, 3)):
-        for c in range(3):
-            src = rmod(coord[c] + SIDE - k)
-            with scope('wait_g1'):
-                wait(part(c, src, d), g1_r.at[c, d, d])
-            remote(part(c, src, d), part(c, src, d), g2_s.at[c, d], g2_r.at[c, d], along(c, rmod(coord[c] + k))).start()
-    for d, k in enumerate((1, 3)):
-        for c in range(3):
-            with scope('wait_g1b'):
-                wait(part(c, rmod(coord[c] + SIDE - k), 1 - d), g1_r.at[c, d, 1 - d])
-
-    def next_gather(r, i):
-        off = jnp.where(i == 2, 2, SIDE - 1 - 2 * i)
-        for c in range(3):
-            gather(c, rmod(coord[c] + off), r)
-
-    def early(i, carry_):
-        next_gather(i // 2, lax.rem(i, 2))
-        return carry_
-
-    with scope('near_gather'):
-        lax.fori_loop(0, SIDE, early, 0)
-    for c in range(3):
-        for d in range(2):
-            with scope('wait_g2'):
-                wait(part(c, rmod(coord[c] + 2), d), g2_r.at[c, d])
-
-    def plane_hop(r):
-        for c, buf in enumerate((ja, jb, jc)):
-            axis = AXES[c][0]
-            dst = buf.at[r, :, coord[axis], :, :, :] if c == 2 else buf.at[r, coord[axis]]
-            for k in NEAR:
-                to = rmod(coord[axis] + k)
-                remote(snd.at[r, to, :, :, :, cols(c)], dst, fa_s.at[r, c], fa_r.at[r, c], along(axis, to)).start()
-                if c == 0:
-                    remote(mg.at[r, to], jm.at[r, y], fm_s.at[0, r], fm_r.at[0, r], along(axis, to)).start()
-            local(snd.at[r, coord[axis], :, :, :, cols(c)], dst, fl.at[0, r, c]).start()
-        jm[r, y] = mg[r, y]
-
     def blocks(n, w):
         return snd.at[0, first(n), :, :, :, first(w)]
 
     def pass_on(r):
-        for c, buf in enumerate((ja, jb, jc)):
+        for c, buf in enumerate(hop_bufs):
             axis = AXES[c][1]
             w = FWD[c][1]
             with scope('wait_fa'):
@@ -308,25 +292,78 @@
         for p in neighbours:
             pl.semaphore_signal(free.at[r], inc=1, device_id={'grp': p, 'loc': l}, device_id_type=MESH)
 
-    def late(r, carry_):
-        def one(i, carry2):
-            next_gather(r, i)
-            return carry2
-
-        with scope('late_gather'):
-            lax.fori_loop(jnp.where(r < 2, 2, 0), 3, one, 0)
-
-        @pl.when(r < 2)
-        def _():
-            plane_hop(r)
+    def before_near():
+        for r in range(2):
+            for c in (0, 2):
+                hop_part(r, c, coord[c])
+
+        for c in range(3):
+            wait(idst.at[c, first(3)], meta_r.at[c, 0])
+            wait(idst.at[c, first(3)], meta_s.at[c, 0])
+        wait(gatt.at[first(3)], meta_r.at[0, 1])
+        wait(gatt.at[first(3)], meta_s.at[0, 1])
+        with scope('far_table'):
+            def far_table(k, carry_):
+                for c in range(3):
+                    make_table(c, rmod(coord[c] + k))
+                return carry_
+
+            lax.fori_loop(1, SIDE, far_table, 0)
+
+        for d, k in enumerate((1, 3)):
+            for c in range(3):
+                src = rmod(coord[c] + SIDE - k)
+                with scope('wait_g1'):
+                    wait(part(c, src, d), g1_r.at[c, d, d])
+                remote(part(c, src, d), part(c, src, d), g2_s.at[c, d], g2_r.at[c, d], along(c, rmod(coord[c] + k))).start()
+        for d, k in enumerate((1, 3)):
+            for c in range(3):
+                with scope('wait_g1b'):
+                    wait(part(c, rmod(coord[c] + SIDE - k), 1 - d), g1_r.at[c, d, 1 - d])
+
+
+    def before_second_near():
+        hop_part(0, 1, y)
+        for c in range(3):
+            for k in (1, 3):
+                hop_part(0, c, rmod(coord[c] + k))
+
+    def before_far():
+        for c in range(3):
+            for d in range(2):
+                with scope('wait_g2'):
+                    wait(part(c, rmod(coord[c] + 2), d), g2_r.at[c, d])
+
+    def after_far():
+        for c in range(3):
+            hop_part(0, c, rmod(coord[c] + 2))
+        hop_rest(0)
+        hop_part(1, 1, y)
+        for k in NEAR:
+            for c in range(3):
+                hop_part(1, c, rmod(coord[c] + k))
+        hop_rest(1)
+
+    events = ((3, before_near), (5, before_second_near), (7, before_far), (8, after_far))
+
+    def gather_step(i, carry_):
+        for at, event in events:
+            @pl.when(i == at)
+            def _():
+                event()
+        far = (i == 7) | (i == 8) | (i == 11)
+        off = jnp.where(i < 3, 0, jnp.where(far, 2, jnp.where(lax.rem(i, 2) == 1, 3, 1)))
+        pair = jnp.where(i < 3, i, jnp.where(i > 8, 2, jnp.where((i == 5) | (i == 6) | (i == 8), 1, 0)))
+        with scope('gather'):
+            for c in range(3):
+                gather(c, rmod(coord[c] + off), pair)
         return carry_
 
-    lax.fori_loop(0, ROUNDS, late, 0)
-    with scope('pass_on'):
-        pass_on(0)
-    plane_hop(2)
-    with scope('pass_on'):
-        pass_on(1)
+    lax.fori_loop(0, SIDE * PAIRS, gather_step, 0)
+    for r in range(2):
+        with scope('pass_on'):
+            pass_on(r)
+        plane_hop(r + 2)
     for c in range(3):
         for d in range(2):
             wait(part(c, 0, d), g2_s.at[c, d])
@@ -343,22 +380,19 @@
         return gat.at[kk, first(CH), n]
 
     def chunk(r, kk):
-        who, half = kk // 2, lax.rem(kk, 2)
-        lp = jnp.where(who == 0, l, other)
-        z0 = half * 2
-        zs = pl.ds(z0, 2)
+        lp = jnp.where(kk == 0, l, other)
 
         def col(c0, w):
-            return rx[lp, r, zs, :, :, :, pl.ds(c0, w)].reshape(CH, w)
-
-        for m in range(2 * SIDE):
-            zz, yy = z0 + m // SIDE, m % SIDE
+            return rx[lp, r, :, :, :, :, pl.ds(c0, w)].reshape(CH, w)
+
+        for m in range(PLANE):
+            zz, yy = m // SIDE, m % SIDE
             gcol = over_lanes(jnp.where(mine, mr[lp, r, zz, yy], 0.0))
             rows = rx[lp, r, zz, yy, :, :, pl.ds(D, D)].reshape(LINE, D)
             ubuf[pl.ds(m * LINE, LINE), :] = (gcol * rows.astype(F32)).astype(BF16)
         for h in range(2):
             hs = pl.ds(h * WIDE, WIDE)
-            ab = dot(rx[lp, r, z0 + h, :, :, :, first(D)].reshape(WIDE, D), wgu[...])
+            ab = dot(rx[lp, r, pl.ds(2 * h, 2), :, :, :, first(D)].reshape(WIDE, D), wgu[...])
             dh = dot(ubuf[hs, :], wdn[...], 1, 1)
             a = ab[:, :F]
             b = ab[:, F:]
@@ -371,9 +405,9 @@
         for n in range(4):
             o = dot(hd[:, first(F)], wdn[:, pl.ds(n * WIDE, WIDE)])
             dg = dg + over_lanes(col(D + n * WIDE, WIDE).astype(F32) * o)
-        for m in range(2 * SIDE):
+        for m in range(PLANE):
             line = over_rows(jnp.where(mine, dg[m * LINE:(m + 1) * LINE, :], 0.0))
-            dgb[who, r, z0 + m // SIDE, m % SIDE] = line
+            dgb[kk, r, m // SIDE, m % SIDE] = line
         acc[first(F), :] += dot(hd[:, first(F)], ubuf[...], 0, 0)
         for i in (1, 2):
             acc[pl.ds(i * F, F), :] += dot(hd[:, pl.ds(i * F, F)], col(0, D), 0, 0)
@@ -440,89 +474,86 @@
                     local(src, dst, bl.at[1, r, c]).start()
         dgh[r, x] = dgj[r]
 
-    hooks = (((0, 3), 'pass_on2', lambda: pass_on(2)), ((2, 0), 'home_second0', lambda: home_second(0)),
-             ((2, 2), 'home_second1', lambda: home_second(1)), ((2, 3), 'home_third0', lambda: home_third(0)))
-
     def round_body(r, carry_):
         for c in range(3):
             with scope('wait_fb'):
                 wait(blocks(3, FWD[c][1]), fb_r.at[r, c])
             wait(blocks(1, FWD[c][1]), fl.at[1, r, c])
         wait(mg.at[0, first(3)], fm_r.at[1, r])
-        for h in range(2):
-            blk = rx.at[l, r, pl.ds(2 * h, 2)]
-            remote(blk, blk, d2_s.at[r, h], d2_r.at[r, h], loc=other).start()
+        remote(rx.at[l, r], rx.at[l, r], d2_s.at[r], d2_r.at[r], loc=other).start()
         remote(mr.at[l, r], mr.at[l, r], dm_s.at[0, r], dm_r.at[0, r], loc=other).start()
 
         def step(kk, carry2):
-            half = lax.rem(kk, 2)
-            zs = pl.ds(half * 2, 2)
-
-            @pl.when(kk >= 2)
+            @pl.when(kk == 1)
             def _():
+                wait(rx.at[l, r], d2_s.at[r])
+                pl.semaphore_signal(credit.at[r], inc=1, device_id={'grp': g, 'loc': other}, device_id_type=MESH)
                 with scope('wait_d2'):
-                    wait(rx.at[other, r, zs], d2_r.at[r, half])
-
-            @pl.when(kk == 2)
-            def _():
+                    wait(rx.at[other, r], d2_r.at[r])
                 wait(mr.at[other, r], dm_r.at[0, r])
 
             with scope('chunk'):
                 chunk(r, kk)
-
-            @pl.when(kk == 1)
-            def _():
-                for h in range(2):
-                    wait(rx.at[l, r, pl.ds(2 * h, 2)], d2_s.at[r, h])
-                pl.semaphore_signal(credit.at[r], inc=1, device_id={'grp': g, 'loc': other}, device_id_type=MESH)
-
-            for (rr, at), name, hook in hooks:
-                @pl.when((r == rr) & (kk == at))
-                def _():
-                    with scope(name):
-                        hook()
-
-            @pl.when(kk == 2)
-            def _():
-                with scope('credit'):
-                    pl.semaphore_wait(credit.at[r], 1)
-
-            @pl.when(kk >= 2)
-            def _():
-                rx[other, r, zs, :, :, :, first(D)] = result(kk)[...].reshape(2, SIDE, SIDE, RS, D)
-                remote(rx.at[other, r, zs, :, :, :, first(D)], rx.at[other, r, zs, :, :, :, pl.ds(D, D)],
-                       c_s.at[r, half], c_r.at[r, half], loc=other).start()
             return carry2
 
-        lax.fori_loop(0, 4, step, 0)
+        lax.fori_loop(0, 2, step, 0)
+        with scope('credit'):
+            pl.semaphore_wait(credit.at[r], 1)
+        rx[other, r, :, :, :, :, first(D)] = result(1)[...].reshape(SIDE, SIDE, SIDE, RS, D)
+        remote(rx.at[other, r, :, :, :, :, first(D)], rx.at[other, r, :, :, :, :, pl.ds(D, D)], c_s.at[r], c_r.at[r], loc=other).start()
         remote(dgb.at[1, r], dgr.at[r], dm_s.at[1, r], dm_r.at[1, r], loc=other).start()
-        for h in range(2):
-            with scope('wait_c'):
-                wait(rx.at[l, r, pl.ds(2 * h, 2), :, :, :, pl.ds(D, D)], c_r.at[r, h])
-
-            def add(zy, carry2):
-                zz, yy = 2 * h + zy // SIDE, lax.rem(zy, SIDE)
-                p0 = gat[h, pl.ds(zy * LINE, LINE), first(D)].astype(F32).reshape(SIDE, RS, D)
-                p1 = rx[l, r, zz, yy, :, :, pl.ds(D, D)].astype(F32)
-                rx[l, r, zz, yy, :, :, first(D)] = (p0 + p1).astype(BF16)
-                return carry2
-
-            with scope('add'):
-                lax.fori_loop(0, 2 * SIDE, add, 0)
+
+        @pl.when(r < ROUNDS - 2)
+        def _():
+            with scope('pass_on'):
+                pass_on(r + 2)
+
+        @pl.when(r < ROUNDS - 4)
+        def _():
+            plane_hop(r + 4)
+
+        with scope('wait_c'):
+            wait(rx.at[l, r, :, :, :, :, pl.ds(D, D)], c_r.at[r])
+
+        def add(zy, carry2):
+            zz, yy = zy // SIDE, rmod(zy)
+            p0 = gat[0, pl.ds(zy * LINE, LINE), first(D)].astype(F32).reshape(SIDE, RS, D)
+            p1 = rx[l, r, zz, yy, :, :, pl.ds(D, D)].astype(F32)
+            rx[l, r, zz, yy, :, :, first(D)] = (p0 + p1).astype(BF16)
+            return carry2
+
+        with scope('add'):
+            lax.fori_loop(0, PLANE, add, 0)
         wait(dgr.at[r], dm_r.at[1, r])
         dgb[0, r] = dgb[0, r] + dgr[r]
         with scope('home_first'):
             home_first(r)
+
+        @pl.when(r >= 2)
+        def _():
+            with scope('home_second'):
+                home_second(r - 2)
+
+        @pl.when(r >= 4)
+        def _():
+            with scope('home_third'):
+                home_third(r - 4)
         return carry_
 
     lax.fori_loop(0, ROUNDS, round_body, 0)
 
+    with scope('home_third'):
+        home_third(2)
     with scope('flush'):
-        gat[1, first(F), first(D)] = acc[first(F), :].astype(BF16)
-        gat[2, first(2 * F), first(D)] = acc[pl.ds(F, 2 * F), :].astype(BF16)
-        outs = [local(gat.at[1, first(F), first(D)], dwd_hbm, out_sem.at[0]),
-                local(gat.at[2, first(F), first(D)], dwg_hbm, out_sem.at[1]),
-                local(gat.at[2, pl.ds(F, F), first(D)], dwu_hbm, out_sem.at[2])]
+        outs = [local(gat.at[3, first(F), pl.ds(D, D)], dwd_hbm, out_sem.at[0])]
+        gat[3, first(F), pl.ds(D, D)] = acc[first(F), :].astype(BF16)
+        eye = onehot(iota((F, F), 0) == iota((F, F), 1))
+        for i, out in enumerate((dwg_hbm, dwu_hbm)):
+            for n in range(4):
+                block = acc[pl.ds((i + 1) * F, F), pl.ds(n * WIDE, WIDE)].astype(BF16)
+                stage = gat.at[1 + n // 3, pl.ds(n % 3 * WIDE, WIDE), pl.ds(i * F, F)]
+                stage[...] = dot(block, eye, 0, 0).astype(BF16)
+                outs.append(local(stage, out.at[pl.ds(n * WIDE, WIDE), :], out_sem.at[1 + 4 * i + n]))
         for cp in outs:
             cp.start()
         dgacc[...] = jnp.zeros_like(dgacc)
@@ -530,15 +561,13 @@
         slotn = slott[...].astype(BF16)
         glane = iota((GROUPS, GROUPS * RS), 1) // RS
         spread = onehot(home_gid() == glane)
-    with scope('home_third1'):
-        home_third(1)
     with scope('home_second'):
-        home_second(2)
+        home_second(4)
 
     def combine(r):
         with scope('pick'):
             want = (lax.rem(iota((1, GROUPS * RS), 1), RS) + r * RS).astype(F32)
-            for n in range(4):
+            for n in range(2):
                 ns = pl.ds(n * WIDE, WIDE)
                 got = dot(slotn, spread[:, n * WIDE:(n + 1) * WIDE], 0, 0)
                 gat[0, :, ns] = onehot(got == want[:, n * WIDE:(n + 1) * WIDE])
@@ -551,7 +580,7 @@
                     mine_k = dgh[r, :, :, pl.ds(e * LINE + k * RS, RS)].reshape(GROUPS, RS)
                     lines = jnp.where(x == k, mine_k, lines)
                 for i in range(RS):
-                    cur = jnp.where(slott[...] == float(r * RS + i), lines[:, i:i + 1], cur)
+                    cur = jnp.where(slott[...] == (r * RS + i).astype(F32), lines[:, i:i + 1], cur)
                 dgacc[e] = cur
         for c in range(3):
             with scope('wait_bc'):
@@ -560,16 +589,23 @@
         with scope('combine'):
             for n in range(4):
                 ns = pl.ds(n * WIDE, WIDE)
-                acc[first(TOK), ns] += dot(gat[0, :, first(D)], snd[r, :, :, :, :, ns].reshape(GROUPS * RS, WIDE))
-
-    combine(0)
-    with scope('home_third2'):
-        home_third(2)
-    combine(1)
-    combine(2)
+                acc[first(TOK), ns] += dot(gat[0, :, first(GROUPS * RS)], snd[r, :, :, :, :, ns].reshape(GROUPS * RS, WIDE))
+
+    tail = ((0, lambda: home_third(3)), (1, lambda: home_second(5)), (2, lambda: home_third(4)), (3, lambda: home_third(5)))
+
+    def last(r, carry_):
+        for at, hook in tail:
+            @pl.when(r == at)
+            def _():
+                with scope('tail_hook'):
+                    hook()
+        combine(r)
+        return carry_
+
+    lax.fori_loop(0, ROUNDS, last, 0)
     with scope('finish'):
         gat[3, :, first(D)] = acc[first(TOK), :].astype(BF16)
-        dx_out = local(gat.at[3, :, first(D)], dx_hbm, out_sem.at[3])
+        dx_out = local(gat.at[3, :, first(D)], dx_hbm, out_sem.at[9])
         dx_out.start()
         for j in range(TOP_K):
             idj = idst[0, x, pl.ds(j, 1), :]
@@ -583,7 +619,7 @@
             wait(mg.at[0, first(3)], fm_s.at[1, r])
             for i in range(2):
                 wait(dgr.at[r], dm_s.at[i, r])
-                wait(rx.at[0, r, first(2), :, :, :, first(D)], c_s.at[r, i])
+            wait(rx.at[0, r, :, :, :, :, first(D)], c_s.at[r])
             for c in range(3):
                 wait(blocks(3, FWD[c][1]), fb_s.at[r, c])
                 for sem in (ba_s, bb_s, bc_s):
@@ -603,13 +639,12 @@
         sd = jax.ShapeDtypeStruct
         cube = (ROUNDS, SIDE, SIDE, SIDE, RS)
         lines = (ROUNDS, SIDE, SIDE, 1, LANES)
-        weight = sd((F, D), BF16)
         out = pl.pallas_call(
             kernel,
             name='moe_backward',
             in_specs=[any_] * 7,
             out_specs=[any_, vmem] + [any_] * 9,
-            out_shape=[sd((TOK, D), BF16), sd((TOP_K, TOK), F32), weight, weight, weight,
+            out_shape=[sd((TOK, D), BF16), sd((TOP_K, TOK), F32), *[sd((D, F), BF16)] * 2, sd((F, D), BF16),
                        *[sd((*cube, w), BF16) for _, w in FWD + BWD]],
             scratch_shapes=[
                 pltpu.VMEM((SIDE, TOK, 2 * D), BF16),
@@ -619,7 +654,7 @@
                 pltpu.VMEM((F, D), BF16),
                 pltpu.VMEM((3 * F, D), F32),
                 pltpu.VMEM((CH, 3 * F), BF16),
-                pltpu.VMEM((PLANE * RS, TOK), BF16),
+                pltpu.VMEM((PLANE * GS, TOK), BF16),
                 pltpu.VMEM((GROUPS, TOK), F32),
                 pltpu.VMEM((3, SIDE, TOP_K, TOK), jnp.int32),
                 pltpu.VMEM((SIDE, TOP_K, TOK), F32),
@@ -633,14 +668,14 @@
                 pltpu.VMEM((ROUNDS, PLANE, LANES), F32),
                 pltpu.VMEM((ROUNDS, SIDE, PLANE, LANES), F32),
                 pltpu.VMEM((2, GROUPS, TOK), F32),
-                dma((3, 4)), dma((4,)), *[dma((3, 2))] * 2, *[dma((3, 2, 2))] * 2, *[dma((3, 2))] * 2,
+                dma((3, 4)), dma((10,)), *[dma((3, 2))] * 2, *[dma((3, 2, 2))] * 2, *[dma((3, 2))] * 2,
                 *[dma((ROUNDS, 3))] * 4, dma((2, ROUNDS, 3)), *[dma((2, ROUNDS))] * 2,
-                *[dma((ROUNDS, 2))] * 4, *[dma((2, ROUNDS))] * 2, *[dma((ROUNDS, 3))] * 6, dma((2, ROUNDS, 3)),
+                *[dma((ROUNDS,))] * 4, *[dma((2, ROUNDS))] * 2, *[dma((ROUNDS, 3))] * 6, dma((2, ROUNDS, 3)),
                 *[dma((3, ROUNDS))] * 2, *[pltpu.SemaphoreType.REGULAR((ROUNDS,))] * 2,
             ],
             compiler_params=pltpu.CompilerParams(collective_id=0, has_side_effects=True, vmem_limit_bytes=67043328),
         )(x_rows, dy_rows, expert_ids.T, gate_vals.T, w_gate[0], w_up[0], w_down[0])
-        dx, d_gates, dwg_t, dwu_t, dwd = out[:5]
-        return dx, d_gates.T, dwg_t.T[None], dwu_t.T[None], dwd[None]
+        dx, d_gates, dwg, dwu, dwd = out[:5]
+        return dx, d_gates.T, dwg[None], dwu[None], dwd[None]
 
     return jax.shard_map(device_step, mesh=mesh, in_specs=(spec,) * 7, out_specs=(spec,) * 5, check_vma=False)

time: 234 us -> 220 us (0.940)
  Pallas kernels: 225 us -> 213 us
    pallas_call x1, Pallas kernels: 225 us -> 213 us  [device_step(): pl.pallas_call(kernel, name='moe_backward', in_specs=[any_] * 7, out_spec...]
    unnamed x11 -> x13, local copies, waits for them, and re-layouts: 7.41 us -> 6.05 us
where the time goes in v4:
time: 220 us
  Pallas kernels  213 us (97%)
  local copies, waits for them, and re-layouts  6.05 us (3%)
    pallas_call x1, Pallas kernels, device_step(): pl.pallas_call(kernel, name='moe_backward', in_specs=[any_] * 7, out_spec...  213 us
    unnamed x13, local copies, waits for them, and re-layouts  6.05 us

profile of v4, /device:TPU:0, one launch (start us, length us, event | category | flops | bytes accessed | tf_op | source)
XLA Modules:
  0.0 219.9 jit_solution(3961204438387371110)
XLA Ops:
  0.6 213.1 %moe_backward.1 = (bf16[768,1024]{1,0:T(8,128)(2,1)}, f32[8,768]{1,0:T(8,128)}, bf16[1024,384]{1,0:T(8,128)(2,1)}, bf16[1024,384]{1,0:T(8,128)(2,1)}, bf16[384,1...) custom-call(bf16[768,1024]{1,0:T(8,128)(2,1)} %x_hbm.1, ...), custom_call_target="tpu_custom_call" | custom-call | tf_op jit(solution)/shard_map/moe_backward/pallas_call | solution.py:642
  213.8 0.0 copy-start.3
  213.8 0.0 copy-start.2
  213.8 0.0 copy-start.1
  213.8 2.8 %copy.17 = bf16[768,1024]{1,0:T(8,128)(2,1)} copy(bf16[768,1024]{1,0:T(8,128)(2,1)} %get-tuple-element.20) | data formatting | bytes 3145728
  216.6 0.0 copy-done.3
  216.6 0.0 copy-start
  216.6 0.6 copy.18
  217.2 0.0 copy-done.2
  217.2 0.9 copy.19
  218.1 0.0 copy-done.1
  218.1 0.9 copy.20
  219.0 0.0 copy-done
  219.0 0.9 copy.21
Async XLA Ops:
  213.8 2.8 %copy-start.3 = (f32[8,768]{1,0:T(8,128)S(1)}, f32[8,768]{1,0:T(8,128)}, u32[]{:S(2)}) copy-start(f32[8,768]{1,0:T(8,128)} %get-tuple-element.11) | copy-start | bytes 73732
  213.8 3.4 %copy-start.2 = (bf16[1024,384]{1,0:T(8,128)(2,1)S(1)}, bf16[1024,384]{1,0:T(8,128)(2,1)}, u32[]{:S(2)}) copy-start(bf16[1024,384]{1,0:T(8,128)(2,1)} %get-tuple-element.12) | copy-start | bytes 2359300
  213.8 4.3 %copy-start.1 = (bf16[1024,384]{1,0:T(8,128)(2,1)S(1)}, bf16[1024,384]{1,0:T(8,128)(2,1)}, u32[]{:S(2)}) copy-start(bf16[1024,384]{1,0:T(8,128)(2,1)} %get-tuple-element.13) | copy-start | bytes 2359300
  216.6 2.4 %copy-start = (bf16[384,1024]{1,0:T(8,128)(2,1)S(1)}, bf16[384,1024]{1,0:T(8,128)(2,1)}, u32[]{:S(2)}) copy-start(bf16[384,1024]{1,0:T(8,128)(2,1)} %get-tuple-element.14) | copy-start | bytes 2359300

commit v5 on v4

--- a/solution.py
+++ b/solution.py
@@ -30,6 +30,7 @@
 BWD = ((0, 384), (384, 384), (768, 256))
 AXES = ((1, 2), (2, 0), (0, 1))
 NEAR = (1, 3, 2)
+BOTH = (1, 3)
 scope = jax.named_scope
 
 
@@ -90,6 +91,7 @@
     def wait(ref, sem):
         local(ref, ref, sem).wait()
 
+    three_lines, three_planes, three_gates = mg.at[0, first(3)], dgh.at[0, first(3)], gatt.at[first(3)]
     neighbours = [along(axis, rmod(coord[axis] + k)) for axis in range(3) for k in NEAR]
 
     barrier = pltpu.get_barrier_semaphore()
@@ -124,7 +126,7 @@
         pl.semaphore_wait(barrier, len(neighbours) + 1)
 
     def slab_send(i):
-        for d, k in enumerate((1, 3)):
+        for d, k in enumerate(BOTH):
             h = (d + i) % 2
             rows = pl.ds(h * HALF, HALF)
             for c in range(3):
@@ -275,7 +277,7 @@
             wait(blocks(1, w), fl.at[0, r, c])
             dst = (rx.at[l, r, z, :, :, :, cols(c)], rx.at[l, r, :, :, x, :, cols(c)], rx.at[l, r, :, y, :, :, cols(c)])[c]
             if c == 0:
-                wait(mg.at[0, first(3)], fm_r.at[0, r])
+                wait(three_lines, fm_r.at[0, r])
             for k in (*NEAR, 0):
                 to = rmod(coord[axis] + k)
                 src = buf.at[r, :, :, to] if c == 2 else buf.at[r, :, to]
@@ -288,7 +290,7 @@
         mr[l, r, z] = jm[r, :, z]
         for c in range(3):
             wait(blocks(3, FWD[c][1]), fa_s.at[r, c])
-        wait(mg.at[0, first(3)], fm_s.at[0, r])
+        wait(three_lines, fm_s.at[0, r])
         for p in neighbours:
             pl.semaphore_signal(free.at[r], inc=1, device_id={'grp': p, 'loc': l}, device_id_type=MESH)
 
@@ -300,8 +302,8 @@
         for c in range(3):
             wait(idst.at[c, first(3)], meta_r.at[c, 0])
             wait(idst.at[c, first(3)], meta_s.at[c, 0])
-        wait(gatt.at[first(3)], meta_r.at[0, 1])
-        wait(gatt.at[first(3)], meta_s.at[0, 1])
+        wait(three_gates, meta_r.at[0, 1])
+        wait(three_gates, meta_s.at[0, 1])
         with scope('far_table'):
             def far_table(k, carry_):
                 for c in range(3):
@@ -310,13 +312,13 @@
 
             lax.fori_loop(1, SIDE, far_table, 0)
 
-        for d, k in enumerate((1, 3)):
+        for d, k in enumerate(BOTH):
             for c in range(3):
                 src = rmod(coord[c] + SIDE - k)
                 with scope('wait_g1'):
                     wait(part(c, src, d), g1_r.at[c, d, d])
                 remote(part(c, src, d), part(c, src, d), g2_s.at[c, d], g2_r.at[c, d], along(c, rmod(coord[c] + k))).start()
-        for d, k in enumerate((1, 3)):
+        for d, k in enumerate(BOTH):
             for c in range(3):
                 with scope('wait_g1b'):
                     wait(part(c, rmod(coord[c] + SIDE - k), 1 - d), g1_r.at[c, d, 1 - d])
@@ -325,7 +327,7 @@
     def before_second_near():
         hop_part(0, 1, y)
         for c in range(3):
-            for k in (1, 3):
+            for k in BOTH:
                 hop_part(0, c, rmod(coord[c] + k))
 
     def before_far():
@@ -438,7 +440,7 @@
             with scope('wait_ba'):
                 wait(blocks(3, BWD[c][1]), ba_r.at[r, c])
             if c == 0:
-                wait(mg.at[0, first(3)], bm_r.at[0, r])
+                wait(three_lines, bm_r.at[0, r])
             dst = buf.at[r, coord[axis]] if c == 1 else buf.at[r, :, coord[axis]]
             cs = pl.ds(D + BWD[c][0], BWD[c][1])
             for k in (*NEAR, 0):
@@ -458,7 +460,7 @@
                 wait(blocks(3, BWD[c][1]), bb_r.at[r, c])
             wait(blocks(1, BWD[c][1]), bl.at[0, r, c])
             if c == 0:
-                wait(mg.at[0, first(3)], bm_r.at[1, r])
+                wait(three_lines, bm_r.at[1, r])
                 for p in range(PLANE):
                     dgj[r, pl.ds(p, 1), :] = dgi[r, p // SIDE, p % SIDE]
             cs = pl.ds(*BWD[c])
@@ -467,21 +469,34 @@
                 to = rmod(coord[c] + k)
                 src = buf.at[r, :, :, to]
                 if k:
-                    remote(src, dst, bc_s.at[r, c], bc_r.at[r, c], along(c, to)).start()
                     if c == 0:
                         remote(dgj.at[r], dgh.at[r, x], bm_s.at[2, r], bm_r.at[2, r], along(c, to)).start()
+                    remote(src, dst, bc_s.at[r, c], bc_r.at[r, c], along(c, to)).start()
                 else:
                     local(src, dst, bl.at[1, r, c]).start()
         dgh[r, x] = dgj[r]
 
+    start, mid, end = range(3)
+    moves = ((2, end, home_second, 0), (3, end, home_second, 1), (4, mid, home_second, 2), (4, end, home_third, 0),
+             (5, start, home_second, 3), (5, mid, home_third, 1), (5, end, home_second, 4), (5, end, home_third, 2))
+
+    def move(r, place):
+        for rr, at, hop, which in moves:
+            if at == place:
+                @pl.when(r == rr)
+                def _():
+                    with scope(f'{hop.__name__}{which}'):
+                        hop(which)
+
     def round_body(r, carry_):
         for c in range(3):
             with scope('wait_fb'):
                 wait(blocks(3, FWD[c][1]), fb_r.at[r, c])
             wait(blocks(1, FWD[c][1]), fl.at[1, r, c])
-        wait(mg.at[0, first(3)], fm_r.at[1, r])
+        wait(three_lines, fm_r.at[1, r])
         remote(rx.at[l, r], rx.at[l, r], d2_s.at[r], d2_r.at[r], loc=other).start()
         remote(mr.at[l, r], mr.at[l, r], dm_s.at[0, r], dm_r.at[0, r], loc=other).start()
+        move(r, start)
 
         def step(kk, carry2):
             @pl.when(kk == 1)
@@ -491,6 +506,7 @@
                 with scope('wait_d2'):
                     wait(rx.at[other, r], d2_r.at[r])
                 wait(mr.at[other, r], dm_r.at[0, r])
+                move(r, mid)
 
             with scope('chunk'):
                 chunk(r, kk)
@@ -528,22 +544,11 @@
         dgb[0, r] = dgb[0, r] + dgr[r]
         with scope('home_first'):
             home_first(r)
-
-        @pl.when(r >= 2)
-        def _():
-            with scope('home_second'):
-                home_second(r - 2)
-
-        @pl.when(r >= 4)
-        def _():
-            with scope('home_third'):
-                home_third(r - 4)
+        move(r, end)
         return carry_
 
     lax.fori_loop(0, ROUNDS, round_body, 0)
 
-    with scope('home_third'):
-        home_third(2)
     with scope('flush'):
         outs = [local(gat.at[3, first(F), pl.ds(D, D)], dwd_hbm, out_sem.at[0])]
         gat[3, first(F), pl.ds(D, D)] = acc[first(F), :].astype(BF16)
@@ -561,72 +566,103 @@
         slotn = slott[...].astype(BF16)
         glane = iota((GROUPS, GROUPS * RS), 1) // RS
         spread = onehot(home_gid() == glane)
-    with scope('home_second'):
-        home_second(4)
-
-    def combine(r):
-        with scope('pick'):
-            want = (lax.rem(iota((1, GROUPS * RS), 1), RS) + r * RS).astype(F32)
-            for n in range(2):
-                ns = pl.ds(n * WIDE, WIDE)
-                got = dot(slotn, spread[:, n * WIDE:(n + 1) * WIDE], 0, 0)
-                gat[0, :, ns] = onehot(got == want[:, n * WIDE:(n + 1) * WIDE])
-        wait(dgh.at[r, first(3)], bm_r.at[2, r])
-        with scope('dg'):
-            for e in range(2):
-                cur = dgacc[e]
-                lines = jnp.zeros((GROUPS, RS), F32)
-                for k in range(SIDE):
-                    mine_k = dgh[r, :, :, pl.ds(e * LINE + k * RS, RS)].reshape(GROUPS, RS)
-                    lines = jnp.where(x == k, mine_k, lines)
-                for i in range(RS):
-                    cur = jnp.where(slott[...] == (r * RS + i).astype(F32), lines[:, i:i + 1], cur)
-                dgacc[e] = cur
+    def pick(r):
+        want = (lax.rem(iota((1, GROUPS * RS), 1), RS) + r * RS).astype(F32)
+        for n in range(2):
+            ns = pl.ds(n * WIDE, WIDE)
+            got = dot(slotn, spread[:, n * WIDE:(n + 1) * WIDE], 0, 0)
+            gat[0, :, ns] = onehot(got == want[:, n * WIDE:(n + 1) * WIDE])
+
+    def gate_gradients(r):
+        wait(three_planes, bm_r.at[2, r])
+        for e in range(2):
+            cur = dgacc[e]
+            lines = jnp.zeros((GROUPS, RS), F32)
+            for k in range(SIDE):
+                mine_k = dgh[r, :, :, pl.ds(e * LINE + k * RS, RS)].reshape(GROUPS, RS)
+                lines = jnp.where(x == k, mine_k, lines)
+            for i in range(RS):
+                cur = jnp.where(slott[...] == jnp.float32(r * RS + i), lines[:, i:i + 1], cur)
+            dgacc[e] = cur
+
+    def arrived(r):
         for c in range(3):
             with scope('wait_bc'):
                 wait(blocks(3, BWD[c][1]), bc_r.at[r, c])
             wait(blocks(1, BWD[c][1]), bl.at[1, r, c])
+
+    def summed(r, ns):
+        return acc[first(TOK), ns] + dot(gat[0, :, first(GROUPS * RS)], snd[r, :, :, :, :, ns].reshape(GROUPS * RS, WIDE))
+
+    tail = ((1, home_second, 5), (1, home_third, 3), (2, home_third, 4), (3, home_third, 5))
+
+    def last(r, carry_):
+        for at, hop, which in tail:
+            @pl.when(r == at)
+            def _():
+                with scope(f'{hop.__name__}{which}'):
+                    hop(which)
+        with scope('pick'):
+            pick(r)
+        with scope('dg'):
+            gate_gradients(r)
+        arrived(r)
         with scope('combine'):
             for n in range(4):
                 ns = pl.ds(n * WIDE, WIDE)
-                acc[first(TOK), ns] += dot(gat[0, :, first(GROUPS * RS)], snd[r, :, :, :, :, ns].reshape(GROUPS * RS, WIDE))
-
-    tail = ((0, lambda: home_third(3)), (1, lambda: home_second(5)), (2, lambda: home_third(4)), (3, lambda: home_third(5)))
-
-    def last(r, carry_):
-        for at, hook in tail:
-            @pl.when(r == at)
-            def _():
-                with scope('tail_hook'):
-                    hook()
-        combine(r)
+                acc[first(TOK), ns] = summed(r, ns)
         return carry_
 
-    lax.fori_loop(0, ROUNDS, last, 0)
-    with scope('finish'):
-        gat[3, :, first(D)] = acc[first(TOK), :].astype(BF16)
-        dx_out = local(gat.at[3, :, first(D)], dx_hbm, out_sem.at[9])
-        dx_out.start()
+    lax.fori_loop(0, ROUNDS - 1, last, 0)
+    with scope('pick'):
+        pick(ROUNDS - 1)
+    with scope('drain'):
+        for r in range(ROUNDS):
+            for i in range(2):
+                wait(three_lines, bm_s.at[i, r])
+                wait(dgr.at[r], dm_s.at[i, r])
+            wait(three_lines, fm_s.at[1, r])
+            wait(rx.at[0, r, :, :, :, :, first(D)], c_s.at[r])
+            for c in range(3):
+                wait(blocks(3, FWD[c][1]), fb_s.at[r, c])
+                for sem in (ba_s, bb_s):
+                    wait(blocks(3, BWD[c][1]), sem.at[r, c])
+        for cp in outs:
+            cp.wait()
+    with scope('dg'):
+        gate_gradients(ROUNDS - 1)
         for j in range(TOP_K):
             idj = idst[0, x, pl.ds(j, 1), :]
             val = jnp.where(lax.rem(idj, 2) == 0, dgacc[0], dgacc[1])
             dgate_ref[pl.ds(j, 1), :] = over_rows(jnp.where(idj // 2 == home_gid(), val, 0.0))
-
-    with scope('drain'):
+    arrived(ROUNDS - 1)
+    with scope('finish'):
+        outs = []
+        for n in range(4):
+            ns = pl.ds(n * WIDE, WIDE)
+            gat[3, :, ns] = summed(ROUNDS - 1, ns).astype(BF16)
+            outs.append(local(gat.at[3, :, ns], dx_hbm.at[:, ns], out_sem.at[9 + n]))
+            outs[-1].start()
         for r in range(ROUNDS):
-            for i in range(3):
-                wait(dgh.at[0, first(3)] if i == 2 else mg.at[0, first(3)], bm_s.at[i, r])
-            wait(mg.at[0, first(3)], fm_s.at[1, r])
-            for i in range(2):
-                wait(dgr.at[r], dm_s.at[i, r])
-            wait(rx.at[0, r, :, :, :, :, first(D)], c_s.at[r])
+            wait(three_planes, bm_s.at[2, r])
             for c in range(3):
-                wait(blocks(3, FWD[c][1]), fb_s.at[r, c])
-                for sem in (ba_s, bb_s, bc_s):
-                    wait(blocks(3, BWD[c][1]), sem.at[r, c])
+                wait(blocks(3, BWD[c][1]), bc_s.at[r, c])
         for cp in outs:
             cp.wait()
-        dx_out.wait()
+
+
+def hand_over(*refs):
+    n = len(refs) // 4
+    ins, outs, bufs, sems = refs[:n], refs[n:2 * n], refs[2 * n:3 * n], refs[3 * n:]
+    loads = [pltpu.make_async_copy(a, b, sem.at[0]) for a, b, sem in zip(ins, bufs, sems)]
+    stores = [pltpu.make_async_copy(b, o, sem.at[1]) for b, o, sem in zip(bufs, outs, sems)]
+    for cp in loads:
+        cp.start()
+    for load, store in zip(loads, stores):
+        load.wait()
+        store.start()
+    for cp in stores:
+        cp.wait()
 
 
 def solution(mesh):
@@ -668,14 +704,21 @@
                 pltpu.VMEM((ROUNDS, PLANE, LANES), F32),
                 pltpu.VMEM((ROUNDS, SIDE, PLANE, LANES), F32),
                 pltpu.VMEM((2, GROUPS, TOK), F32),
-                dma((3, 4)), dma((10,)), *[dma((3, 2))] * 2, *[dma((3, 2, 2))] * 2, *[dma((3, 2))] * 2,
+                dma((3, 4)), dma((13,)), *[dma((3, 2))] * 2, *[dma((3, 2, 2))] * 2, *[dma((3, 2))] * 2,
                 *[dma((ROUNDS, 3))] * 4, dma((2, ROUNDS, 3)), *[dma((2, ROUNDS))] * 2,
                 *[dma((ROUNDS,))] * 4, *[dma((2, ROUNDS))] * 2, *[dma((ROUNDS, 3))] * 6, dma((2, ROUNDS, 3)),
                 *[dma((3, ROUNDS))] * 2, *[pltpu.SemaphoreType.REGULAR((ROUNDS,))] * 2,
             ],
             compiler_params=pltpu.CompilerParams(collective_id=0, has_side_effects=True, vmem_limit_bytes=67043328),
         )(x_rows, dy_rows, expert_ids.T, gate_vals.T, w_gate[0], w_up[0], w_down[0])
-        dx, d_gates, dwg, dwu, dwd = out[:5]
+        dx, d_gates, dwg, dwu, dwd = pl.pallas_call(
+            hand_over,
+            name='hand_over',
+            in_specs=[any_] * 5,
+            out_specs=[any_] * 5,
+            out_shape=[sd(o.shape, o.dtype) for o in out[:5]],
+            scratch_shapes=[pltpu.VMEM(o.shape, o.dtype) for o in out[:5]] + [dma((2,))] * 5,
+        )(*out[:5])
         return dx, d_gates.T, dwg[None], dwu[None], dwd[None]
 
     return jax.shard_map(device_step, mesh=mesh, in_specs=(spec,) * 7, out_specs=(spec,) * 5, check_vma=False)

time: 220 us -> 217 us (0.986)
  local copies, waits for them, and re-layouts: 6.05 us -> 0 us
  Pallas kernels: 213 us -> 216 us
    unnamed x13 -> x0, local copies, waits for them, and re-layouts: 6.05 us -> none
    pallas_call x0 -> x1, Pallas kernels: none -> 3.42 us  [device_step(): pl.pallas_call(hand_over, name='hand_over', in_specs=[any_] * 5, out_spec...]
where the time goes in v5:
time: 217 us
  Pallas kernels  216 us (100%)
    pallas_call x1, Pallas kernels, device_step(): pl.pallas_call(kernel, name='moe_backward', in_specs=[any_] * 7, out_spec...  213 us

profile of v5, /device:TPU:0, one launch (start us, length us, event | category | flops | bytes accessed | tf_op | source)
XLA Modules:
  0.0 216.8 jit_solution(11218904932777319164)
XLA Ops:
  0.6 212.6 %moe_backward.1 = (bf16[768,1024]{1,0:T(8,128)(2,1)}, f32[8,768]{1,0:T(8,128)}, bf16[1024,384]{1,0:T(8,128)(2,1)}, bf16[1024,384]{1,0:T(8,128)(2,1)}, bf16[384,1...) custom-call(bf16[768,1024]{1,0:T(8,128)(2,1)} %x_hbm.1, ...), custom_call_target="tpu_custom_call" | custom-call | tf_op jit(solution)/shard_map/moe_backward/pallas_call | solution.py:678
  213.2 3.4 %hand_over.1 = (bf16[768,1024]{1,0:T(8,128)(2,1)}, f32[8,768]{1,0:T(8,128)}, bf16[1024,384]{1,0:T(8,128)(2,1)}, bf16[1024,384]{1,0:T(8,128)(2,1)}, bf16[384,1024]{1,0:T(8,128)(2,1)}) custom-call(bf16[768,1024]{1,0:T(8,128)(2,1)} %get-tuple-element.15.refs_0_, f32[8,768]{1,0:T(8,128)} %get-tuple-element.16.refs_1_, ...), custom_call_target="tpu_custom_call" | custom-call | tf_op jit(solution)/shard_map/hand_over/pallas_call | solution.py:714

commit v6 on v5

--- a/solution.py
+++ b/solution.py
@@ -62,7 +62,7 @@
            dx_hbm, dgate_ref, dwg_hbm, dwu_hbm, dwd_hbm, ja, jb, jc, ia, ib, ic,
            gat, snd, rx, wgu, wdn, acc, hd, pbuf, slott, idst, gatt, mg, jm, mr, dgb, dgr, km, dgi, dgj, dgh, dgacc,
            loc_sem, out_sem, meta_s, meta_r, g1_s, g1_r, g2_s, g2_r, fa_s, fa_r, fb_s, fb_r, fl, fm_s, fm_r,
-           d2_s, d2_r, c_s, c_r, dm_s, dm_r, ba_s, ba_r, bb_s, bb_r, bc_s, bc_r, bl, bm_s, bm_r, credit, free):
+           d2, c_sem, dm_s, dm_r, b_s, b_r, bl, bm_s, bm_r, credit, free):
     g = lax.axis_index('grp')
     l = lax.axis_index('loc')
     z, y, x = g // PLANE, (g // SIDE) % SIDE, g % SIDE
@@ -92,6 +92,11 @@
         local(ref, ref, sem).wait()
 
     three_lines, three_planes, three_gates = mg.at[0, first(3)], dgh.at[0, first(3)], gatt.at[first(3)]
+    half_slab = gat.at[0, first(HALF)]
+
+    def blocks(n, w=2 * D):
+        return snd.at[0, first(n), :, :, :, first(w)]
+
     neighbours = [along(axis, rmod(coord[axis] + k)) for axis in range(3) for k in NEAR]
 
     barrier = pltpu.get_barrier_semaphore()
@@ -114,12 +119,12 @@
         return pl.ds(*FWD[c])
 
     def own_slab(c):
-        return slab_copies(c, first(TOK), lambda src, cs: local(src, gat.at[coord[c], :, cs], loc_sem.at[1, c]))
-
-    routing = [local(idst_hbm, idst.at[c, coord[c]], loc_sem.at[0, c]) for c in range(3)]
-    routing.append(local(gatt_hbm, gatt.at[x], loc_sem.at[0, 3]))
-    weights = [local(wg_hbm, wgu.at[:, first(F)], loc_sem.at[2, 0]), local(wu_hbm, wgu.at[:, pl.ds(F, F)], loc_sem.at[2, 1]),
-               local(wd_hbm, wdn, loc_sem.at[2, 2])]
+        return slab_copies(c, first(TOK), lambda src, cs: local(src, gat.at[coord[c], :, cs], loc_sem.at[1]))
+
+    routing = [local(idst_hbm, idst.at[c, coord[c]], loc_sem.at[0]) for c in range(3)]
+    routing.append(local(gatt_hbm, gatt.at[x], loc_sem.at[2]))
+    weights = [local(wg_hbm, wgu.at[:, first(F)], loc_sem.at[3]), local(wu_hbm, wgu.at[:, pl.ds(F, F)], loc_sem.at[3]),
+               local(wd_hbm, wdn, loc_sem.at[4])]
     for cp in routing + own_slab(0) + own_slab(1) + own_slab(2) + weights:
         cp.start()
     with scope('entry'):
@@ -131,20 +136,20 @@
             rows = pl.ds(h * HALF, HALF)
             for c in range(3):
                 t = along(c, rmod(coord[c] + k))
-                for cp in slab_copies(c, rows, lambda src, cs: remote(src, gat.at[coord[c], rows, cs], g1_s.at[c, d, h],
-                                                                      g1_r.at[c, d, h], t)):
+                for cp in slab_copies(c, rows, lambda src, cs: remote(src, gat.at[coord[c], rows, cs], g1_s.at[0],
+                                                                      g1_r.at[d, h], t)):
                     cp.start()
 
     slab_send(0)
     for c in range(3):
         for k in NEAR:
             t = along(c, rmod(coord[c] + k))
-            remote(idst_hbm, idst.at[c, coord[c]], meta_s.at[c, 0], meta_r.at[c, 0], t).start()
+            remote(idst_hbm, idst.at[c, coord[c]], meta_s.at[0], meta_r.at[0], t).start()
             if c == 0:
-                remote(gatt_hbm, gatt.at[x], meta_s.at[c, 1], meta_r.at[c, 1], t).start()
+                remote(gatt_hbm, gatt.at[x], meta_s.at[1], meta_r.at[1], t).start()
     slab_send(1)
-    for cp in routing:
-        cp.wait()
+    wait(idst.at[:, 0], loc_sem.at[0])
+    wait(gatt.at[0], loc_sem.at[2])
 
     tri = onehot(iota((LANES, LANES), 0) < iota((LANES, LANES), 1))
     tables = 3 * SIDE * PLANE
@@ -226,9 +231,7 @@
             else:
                 snd[2 * pair + i, :, :, k, :, cols(c)] = rows[:, :, i]
 
-    for c in range(3):
-        for cp in own_slab(c):
-            cp.wait()
+    wait(gat.at[0], loc_sem.at[1])
 
     hop_bufs = (ja, jb, jc)
 
@@ -240,7 +243,7 @@
                 src, dst = snd.at[r, to, k, :, :, cols(c)], jc.at[r, k, coord[axis]]
             else:
                 src, dst = snd.at[r, to, :, k, :, cols(c)], hop_bufs[c].at[r, coord[axis], :, k]
-            remote(src, dst, fa_s.at[r, c], fa_r.at[r, c], along(axis, to)).start()
+            remote(src, dst, fa_s.at[lax.rem(r, 2)], fa_r.at[r], along(axis, to)).start()
 
     def hop_dst(r, c):
         axis = AXES[c][0]
@@ -248,10 +251,10 @@
 
     def hop_rest(r):
         for c in range(3):
-            local(snd.at[r, coord[AXES[c][0]], :, :, :, cols(c)], hop_dst(r, c), fl.at[0, r, c]).start()
+            local(snd.at[r, coord[AXES[c][0]], :, :, :, cols(c)], hop_dst(r, c), fl.at[0, lax.rem(r, 2)]).start()
         for off in NEAR:
             to = rmod(y + off)
-            remote(mg.at[r, to], jm.at[r, y], fm_s.at[0, r], fm_r.at[0, r], along(AXES[0][0], to)).start()
+            remote(mg.at[r, to], jm.at[r, y], fm_s.at[lax.rem(r, 2)], fm_r.at[0, r], along(AXES[0][0], to)).start()
         jm[r, y] = mg[r, y]
 
     def plane_hop(r):
@@ -259,38 +262,33 @@
             axis = AXES[c][0]
             for off in NEAR:
                 to = rmod(coord[axis] + off)
-                remote(snd.at[r, to, :, :, :, cols(c)], hop_dst(r, c), fa_s.at[r, c], fa_r.at[r, c], along(axis, to)).start()
+                remote(snd.at[r, to, :, :, :, cols(c)], hop_dst(r, c), fa_s.at[lax.rem(r, 2)], fa_r.at[r], along(axis, to)).start()
         hop_rest(r)
 
     def part(c, k, h):
         return gat.at[k, pl.ds(h * HALF, HALF), cols(c)]
 
-    def blocks(n, w):
-        return snd.at[0, first(n), :, :, :, first(w)]
-
     def pass_on(r):
+        odd = lax.rem(r, 2)
+        with scope('wait_fa'):
+            wait(blocks(3), fa_r.at[r])
+        wait(blocks(1), fl.at[0, odd])
+        wait(three_lines, fm_r.at[0, r])
         for c, buf in enumerate(hop_bufs):
             axis = AXES[c][1]
-            w = FWD[c][1]
-            with scope('wait_fa'):
-                wait(blocks(3, w), fa_r.at[r, c])
-            wait(blocks(1, w), fl.at[0, r, c])
             dst = (rx.at[l, r, z, :, :, :, cols(c)], rx.at[l, r, :, :, x, :, cols(c)], rx.at[l, r, :, y, :, :, cols(c)])[c]
-            if c == 0:
-                wait(three_lines, fm_r.at[0, r])
             for k in (*NEAR, 0):
                 to = rmod(coord[axis] + k)
                 src = buf.at[r, :, :, to] if c == 2 else buf.at[r, :, to]
                 if k:
-                    remote(src, dst, fb_s.at[r, c], fb_r.at[r, c], along(axis, to)).start()
+                    remote(src, dst, fb_s.at[0], fb_r.at[r], along(axis, to)).start()
                     if c == 0:
-                        remote(jm.at[r, :, to], mr.at[l, r, z], fm_s.at[1, r], fm_r.at[1, r], along(axis, to)).start()
+                        remote(jm.at[r, :, to], mr.at[l, r, z], fm_s.at[2], fm_r.at[1, r], along(axis, to)).start()
                 else:
-                    local(src, dst, fl.at[1, r, c]).start()
+                    local(src, dst, fl.at[1, odd]).start()
         mr[l, r, z] = jm[r, :, z]
-        for c in range(3):
-            wait(blocks(3, FWD[c][1]), fa_s.at[r, c])
-        wait(three_lines, fm_s.at[0, r])
+        wait(blocks(3), fa_s.at[odd])
+        wait(three_lines, fm_s.at[odd])
         for p in neighbours:
             pl.semaphore_signal(free.at[r], inc=1, device_id={'grp': p, 'loc': l}, device_id_type=MESH)
 
@@ -299,11 +297,9 @@
             for c in (0, 2):
                 hop_part(r, c, coord[c])
 
-        for c in range(3):
-            wait(idst.at[c, first(3)], meta_r.at[c, 0])
-            wait(idst.at[c, first(3)], meta_s.at[c, 0])
-        wait(three_gates, meta_r.at[0, 1])
-        wait(three_gates, meta_s.at[0, 1])
+        for sem in (meta_r, meta_s):
+            wait(idst.at[:, first(3)], sem.at[0])
+            wait(three_gates, sem.at[1])
         with scope('far_table'):
             def far_table(k, carry_):
                 for c in range(3):
@@ -313,16 +309,14 @@
             lax.fori_loop(1, SIDE, far_table, 0)
 
         for d, k in enumerate(BOTH):
+            with scope('wait_g1'):
+                wait(half_slab, g1_r.at[d, d])
             for c in range(3):
-                src = rmod(coord[c] + SIDE - k)
-                with scope('wait_g1'):
-                    wait(part(c, src, d), g1_r.at[c, d, d])
-                remote(part(c, src, d), part(c, src, d), g2_s.at[c, d], g2_r.at[c, d], along(c, rmod(coord[c] + k))).start()
-        for d, k in enumerate(BOTH):
-            for c in range(3):
-                with scope('wait_g1b'):
-                    wait(part(c, rmod(coord[c] + SIDE - k), 1 - d), g1_r.at[c, d, 1 - d])
-
+                src = part(c, rmod(coord[c] + SIDE - k), d)
+                remote(src, src, g2_s.at[0], g2_r.at[d], along(c, rmod(coord[c] + k))).start()
+        for d in range(2):
+            with scope('wait_g1b'):
+                wait(half_slab, g1_r.at[d, 1 - d])
 
     def before_second_near():
         hop_part(0, 1, y)
@@ -331,10 +325,9 @@
                 hop_part(0, c, rmod(coord[c] + k))
 
     def before_far():
-        for c in range(3):
-            for d in range(2):
-                with scope('wait_g2'):
-                    wait(part(c, rmod(coord[c] + 2), d), g2_r.at[c, d])
+        for d in range(2):
+            with scope('wait_g2'):
+                wait(half_slab, g2_r.at[d])
 
     def after_far():
         for c in range(3):
@@ -366,14 +359,11 @@
         with scope('pass_on'):
             pass_on(r)
         plane_hop(r + 2)
-    for c in range(3):
-        for d in range(2):
-            wait(part(c, 0, d), g2_s.at[c, d])
-            for h in range(2):
-                wait(part(c, 0, d), g1_s.at[c, d, h])
+    wait(gat.at[0], g2_s.at[0])
+    wait(gat.at[first(2)], g1_s.at[0])
     acc[...] = jnp.zeros_like(acc)
-    for cp in weights:
-        cp.wait()
+    wait(wgu, loc_sem.at[3])
+    wait(wdn, loc_sem.at[4])
 
     mine = (iota((LINE, LANES), 1) == l * LINE + iota((LINE, LANES), 0))
     ubuf = gat.at[0, first(CH), pl.ds(D, D)]
@@ -427,42 +417,40 @@
                 to = rmod(coord[axis] + k)
                 src = (rx.at[l, r, to, :, :, :, cs], rx.at[l, r, :, :, to, :, cs], rx.at[l, r, :, to, :, :, cs])[c]
                 if k:
-                    remote(src, dst, ba_s.at[r, c], ba_r.at[r, c], along(axis, to)).start()
+                    remote(src, dst, b_s.at[0], b_r.at[0, r], along(axis, to)).start()
                     if c == 0:
-                        remote(dgb.at[0, r, to], km.at[r, z], bm_s.at[0, r], bm_r.at[0, r], along(axis, to)).start()
+                        remote(dgb.at[0, r, to], km.at[r, z], bm_s.at[0], bm_r.at[0, r], along(axis, to)).start()
                 else:
                     dst[...] = src[...]
         km[r, z] = dgb[0, r, z]
 
     def home_second(r):
+        with scope('wait_ba'):
+            wait(blocks(3, D), b_r.at[0, r])
+        wait(three_lines, bm_r.at[0, r])
         for c, buf in enumerate((ia, ib, ic)):
             axis = AXES[c][0]
-            with scope('wait_ba'):
-                wait(blocks(3, BWD[c][1]), ba_r.at[r, c])
-            if c == 0:
-                wait(three_lines, bm_r.at[0, r])
             dst = buf.at[r, coord[axis]] if c == 1 else buf.at[r, :, coord[axis]]
             cs = pl.ds(D + BWD[c][0], BWD[c][1])
             for k in (*NEAR, 0):
                 to = rmod(coord[axis] + k)
                 src = snd.at[r, :, :, to, :, cs] if c == 2 else snd.at[r, :, to, :, :, cs]
                 if k:
-                    remote(src, dst, bb_s.at[r, c], bb_r.at[r, c], along(axis, to)).start()
+                    remote(src, dst, b_s.at[1], b_r.at[1, r], along(axis, to)).start()
                     if c == 0:
-                        remote(km.at[r, :, to], dgi.at[r, :, y], bm_s.at[1, r], bm_r.at[1, r], along(axis, to)).start()
+                        remote(km.at[r, :, to], dgi.at[r, :, y], bm_s.at[1], bm_r.at[1, r], along(axis, to)).start()
                 else:
-                    local(src, dst, bl.at[0, r, c]).start()
+                    local(src, dst, bl.at[0, r]).start()
         dgi[r, :, y] = km[r, :, y]
 
     def home_third(r):
+        with scope('wait_bb'):
+            wait(blocks(3, D), b_r.at[1, r])
+        wait(blocks(1, D), bl.at[0, r])
+        wait(three_lines, bm_r.at[1, r])
+        for p in range(PLANE):
+            dgj[r, pl.ds(p, 1), :] = dgi[r, p // SIDE, p % SIDE]
         for c, buf in enumerate((ia, ib, ic)):
-            with scope('wait_bb'):
-                wait(blocks(3, BWD[c][1]), bb_r.at[r, c])
-            wait(blocks(1, BWD[c][1]), bl.at[0, r, c])
-            if c == 0:
-                wait(three_lines, bm_r.at[1, r])
-                for p in range(PLANE):
-                    dgj[r, pl.ds(p, 1), :] = dgi[r, p // SIDE, p % SIDE]
             cs = pl.ds(*BWD[c])
             dst = (snd.at[r, :, :, x, :, cs], snd.at[r, :, y, :, :, cs], snd.at[r, z, :, :, :, cs])[c]
             for k in (*NEAR, 0):
@@ -470,10 +458,10 @@
                 src = buf.at[r, :, :, to]
                 if k:
                     if c == 0:
-                        remote(dgj.at[r], dgh.at[r, x], bm_s.at[2, r], bm_r.at[2, r], along(c, to)).start()
-                    remote(src, dst, bc_s.at[r, c], bc_r.at[r, c], along(c, to)).start()
+                        remote(dgj.at[r], dgh.at[r, x], bm_s.at[2], bm_r.at[2, r], along(c, to)).start()
+                    remote(src, dst, b_s.at[2], b_r.at[2, r], along(c, to)).start()
                 else:
-                    local(src, dst, bl.at[1, r, c]).start()
+                    local(src, dst, bl.at[1, r]).start()
         dgh[r, x] = dgj[r]
 
     start, mid, end = range(3)
@@ -489,23 +477,22 @@
                         hop(which)
 
     def round_body(r, carry_):
-        for c in range(3):
-            with scope('wait_fb'):
-                wait(blocks(3, FWD[c][1]), fb_r.at[r, c])
-            wait(blocks(1, FWD[c][1]), fl.at[1, r, c])
+        with scope('wait_fb'):
+            wait(blocks(3), fb_r.at[r])
+        wait(blocks(1), fl.at[1, lax.rem(r, 2)])
         wait(three_lines, fm_r.at[1, r])
-        remote(rx.at[l, r], rx.at[l, r], d2_s.at[r], d2_r.at[r], loc=other).start()
-        remote(mr.at[l, r], mr.at[l, r], dm_s.at[0, r], dm_r.at[0, r], loc=other).start()
+        remote(rx.at[l, r], rx.at[l, r], d2.at[0], d2.at[1], loc=other).start()
+        remote(mr.at[l, r], mr.at[l, r], dm_s.at[0], dm_r.at[0], loc=other).start()
         move(r, start)
 
         def step(kk, carry2):
             @pl.when(kk == 1)
             def _():
-                wait(rx.at[l, r], d2_s.at[r])
-                pl.semaphore_signal(credit.at[r], inc=1, device_id={'grp': g, 'loc': other}, device_id_type=MESH)
+                wait(rx.at[l, r], d2.at[0])
+                pl.semaphore_signal(credit.at[0], inc=1, device_id={'grp': g, 'loc': other}, device_id_type=MESH)
                 with scope('wait_d2'):
-                    wait(rx.at[other, r], d2_r.at[r])
-                wait(mr.at[other, r], dm_r.at[0, r])
+                    wait(rx.at[other, r], d2.at[1])
+                wait(mr.at[other, r], dm_r.at[0])
                 move(r, mid)
 
             with scope('chunk'):
@@ -514,10 +501,10 @@
 
         lax.fori_loop(0, 2, step, 0)
         with scope('credit'):
-            pl.semaphore_wait(credit.at[r], 1)
+            pl.semaphore_wait(credit.at[0], 1)
         rx[other, r, :, :, :, :, first(D)] = result(1)[...].reshape(SIDE, SIDE, SIDE, RS, D)
-        remote(rx.at[other, r, :, :, :, :, first(D)], rx.at[other, r, :, :, :, :, pl.ds(D, D)], c_s.at[r], c_r.at[r], loc=other).start()
-        remote(dgb.at[1, r], dgr.at[r], dm_s.at[1, r], dm_r.at[1, r], loc=other).start()
+        remote(rx.at[other, r, :, :, :, :, first(D)], rx.at[other, r, :, :, :, :, pl.ds(D, D)], c_sem.at[0], c_sem.at[1], loc=other).start()
+        remote(dgb.at[1, r], dgr.at[r], dm_s.at[1], dm_r.at[1], loc=other).start()
 
         @pl.when(r < ROUNDS - 2)
         def _():
@@ -529,7 +516,7 @@
             plane_hop(r + 4)
 
         with scope('wait_c'):
-            wait(rx.at[l, r, :, :, :, :, pl.ds(D, D)], c_r.at[r])
+            wait(rx.at[l, r, :, :, :, :, pl.ds(D, D)], c_sem.at[1])
 
         def add(zy, carry2):
             zz, yy = zy // SIDE, rmod(zy)
@@ -540,7 +527,7 @@
 
         with scope('add'):
             lax.fori_loop(0, PLANE, add, 0)
-        wait(dgr.at[r], dm_r.at[1, r])
+        wait(dgr.at[r], dm_r.at[1])
         dgb[0, r] = dgb[0, r] + dgr[r]
         with scope('home_first'):
             home_first(r)
@@ -550,17 +537,15 @@
     lax.fori_loop(0, ROUNDS, round_body, 0)
 
     with scope('flush'):
-        outs = [local(gat.at[3, first(F), pl.ds(D, D)], dwd_hbm, out_sem.at[0])]
         gat[3, first(F), pl.ds(D, D)] = acc[first(F), :].astype(BF16)
+        local(gat.at[3, first(F), pl.ds(D, D)], dwd_hbm, out_sem.at[0]).start()
         eye = onehot(iota((F, F), 0) == iota((F, F), 1))
         for i, out in enumerate((dwg_hbm, dwu_hbm)):
             for n in range(4):
                 block = acc[pl.ds((i + 1) * F, F), pl.ds(n * WIDE, WIDE)].astype(BF16)
                 stage = gat.at[1 + n // 3, pl.ds(n % 3 * WIDE, WIDE), pl.ds(i * F, F)]
                 stage[...] = dot(block, eye, 0, 0).astype(BF16)
-                outs.append(local(stage, out.at[pl.ds(n * WIDE, WIDE), :], out_sem.at[1 + 4 * i + n]))
-        for cp in outs:
-            cp.start()
+                local(stage, out.at[pl.ds(n * WIDE, WIDE), :], out_sem.at[1]).start()
         dgacc[...] = jnp.zeros_like(dgacc)
         acc[first(TOK), :] = jnp.zeros((TOK, D), F32)
         slotn = slott[...].astype(BF16)
@@ -586,10 +571,9 @@
             dgacc[e] = cur
 
     def arrived(r):
-        for c in range(3):
-            with scope('wait_bc'):
-                wait(blocks(3, BWD[c][1]), bc_r.at[r, c])
-            wait(blocks(1, BWD[c][1]), bl.at[1, r, c])
+        with scope('wait_bc'):
+            wait(blocks(3, D), b_r.at[2, r])
+        wait(blocks(1, D), bl.at[1, r])
 
     def summed(r, ns):
         return acc[first(TOK), ns] + dot(gat[0, :, first(GROUPS * RS)], snd[r, :, :, :, :, ns].reshape(GROUPS * RS, WIDE))
@@ -617,18 +601,16 @@
     with scope('pick'):
         pick(ROUNDS - 1)
     with scope('drain'):
-        for r in range(ROUNDS):
-            for i in range(2):
-                wait(three_lines, bm_s.at[i, r])
-                wait(dgr.at[r], dm_s.at[i, r])
-            wait(three_lines, fm_s.at[1, r])
-            wait(rx.at[0, r, :, :, :, :, first(D)], c_s.at[r])
-            for c in range(3):
-                wait(blocks(3, FWD[c][1]), fb_s.at[r, c])
-                for sem in (ba_s, bb_s):
-                    wait(blocks(3, BWD[c][1]), sem.at[r, c])
-        for cp in outs:
-            cp.wait()
+        wait(snd.at[:, first(3)], fb_s.at[0])
+        wait(mg.at[:, first(3)], fm_s.at[2])
+        for i in range(2):
+            wait(snd.at[:, first(3), :, :, :, first(D)], b_s.at[i])
+            wait(mg.at[:, first(3)], bm_s.at[i])
+        wait(rx.at[0, :, :, :, :, :, first(D)], c_sem.at[0])
+        wait(mr.at[0], dm_s.at[0])
+        wait(dgr, dm_s.at[1])
+        wait(wdn, out_sem.at[0])
+        wait(wgu, out_sem.at[1])
     with scope('dg'):
         gate_gradients(ROUNDS - 1)
         for j in range(TOP_K):
@@ -637,18 +619,13 @@
             dgate_ref[pl.ds(j, 1), :] = over_rows(jnp.where(idj // 2 == home_gid(), val, 0.0))
     arrived(ROUNDS - 1)
     with scope('finish'):
-        outs = []
         for n in range(4):
             ns = pl.ds(n * WIDE, WIDE)
             gat[3, :, ns] = summed(ROUNDS - 1, ns).astype(BF16)
-            outs.append(local(gat.at[3, :, ns], dx_hbm.at[:, ns], out_sem.at[9 + n]))
-            outs[-1].start()
-        for r in range(ROUNDS):
-            wait(three_planes, bm_s.at[2, r])
-            for c in range(3):
-                wait(blocks(3, BWD[c][1]), bc_s.at[r, c])
-        for cp in outs:
-            cp.wait()
+            local(gat.at[3, :, ns], dx_hbm.at[:, ns], out_sem.at[2]).start()
+        wait(dgh.at[:, first(3)], bm_s.at[2])
+        wait(snd.at[:, first(3), :, :, :, first(D)], b_s.at[2])
+        wait(gat.at[3, :, first(D)], out_sem.at[2])
 
 
 def hand_over(*refs):
@@ -672,6 +649,7 @@
         any_ = pl.BlockSpec(memory_space=pl.ANY)
         vmem = pl.BlockSpec(memory_space=pltpu.VMEM)
         dma = pltpu.SemaphoreType.DMA
+        one, two, three, per_round = (dma((n,)) for n in (1, 2, 3, ROUNDS))
         sd = jax.ShapeDtypeStruct
         cube = (ROUNDS, SIDE, SIDE, SIDE, RS)
         lines = (ROUNDS, SIDE, SIDE, 1, LANES)
@@ -704,10 +682,9 @@
                 pltpu.VMEM((ROUNDS, PLANE, LANES), F32),
                 pltpu.VMEM((ROUNDS, SIDE, PLANE, LANES), F32),
                 pltpu.VMEM((2, GROUPS, TOK), F32),
-                dma((3, 4)), dma((13,)), *[dma((3, 2))] * 2, *[dma((3, 2, 2))] * 2, *[dma((3, 2))] * 2,
-                *[dma((ROUNDS, 3))] * 4, dma((2, ROUNDS, 3)), *[dma((2, ROUNDS))] * 2,
-                *[dma((ROUNDS,))] * 4, *[dma((2, ROUNDS))] * 2, *[dma((ROUNDS, 3))] * 6, dma((2, ROUNDS, 3)),
-                *[dma((3, ROUNDS))] * 2, *[pltpu.SemaphoreType.REGULAR((ROUNDS,))] * 2,
+                dma((5,)), three, two, two, one, dma((2, 2)), one, two, two, per_round, one, per_round, dma((2, 2)), three,
+                dma((2, ROUNDS)), *[two] * 4, three, dma((3, ROUNDS)), dma((2, ROUNDS)), three, dma((3, ROUNDS)),
+                pltpu.SemaphoreType.REGULAR((1,)), pltpu.SemaphoreType.REGULAR((ROUNDS,)),
             ],
             compiler_params=pltpu.CompilerParams(collective_id=0, has_side_effects=True, vmem_limit_bytes=67043328),
         )(x_rows, dy_rows, expert_ids.T, gate_vals.T, w_gate[0], w_up[0], w_down[0])

time: 217 us -> 214 us (0.986)
  Pallas kernels: 216 us -> 213 us
    pallas_call x1, Pallas kernels: 213 us -> 209 us  [device_step(): pl.pallas_call(kernel, name='moe_backward', in_specs=[any_] * 7, out_spec...]
where the time goes in v6:
time: 214 us; the launch traced here: 213 us
  Pallas kernels  213 us (100%)
    pallas_call x1, Pallas kernels, device_step(): pl.pallas_call(kernel, name='moe_backward', in_specs=[any_] * 7, out_spec...  209 us

profile of v6, /device:TPU:0, one launch (start us, length us, event | category | flops | bytes accessed | tf_op | source)
XLA Modules:
  0.0 213.5 jit_solution(15969800471005475950)
XLA Ops:
  0.6 209.4 %moe_backward.1 = (bf16[768,1024]{1,0:T(8,128)(2,1)}, f32[8,768]{1,0:T(8,128)}, bf16[1024,384]{1,0:T(8,128)(2,1)}, bf16[1024,384]{1,0:T(8,128)(2,1)}, bf16[384,1...) custom-call(bf16[768,1024]{1,0:T(8,128)(2,1)} %x_hbm.1, ...), custom_call_target="tpu_custom_call" | custom-call | tf_op jit(solution)/shard_map/moe_backward/pallas_call | solution.py:656
  210.0 3.4 %hand_over.1 = (bf16[768,1024]{1,0:T(8,128)(2,1)}, f32[8,768]{1,0:T(8,128)}, bf16[1024,384]{1,0:T(8,128)(2,1)}, bf16[1024,384]{1,0:T(8,128)(2,1)}, bf16[384,1024]{1,0:T(8,128)(2,1)}) custom-call(bf16[768,1024]{1,0:T(8,128)(2,1)} %get-tuple-element.15.refs_0_, f32[8,768]{1,0:T(8,128)} %get-tuple-element.16.refs_1_, ...), custom_call_target="tpu_custom_call" | custom-call | tf_op jit(solution)/shard_map/hand_over/pallas_call | solution.py:691

commit v7 on v6

--- a/solution.py
+++ b/solution.py
@@ -59,9 +59,9 @@
 
 
 def kernel(x_hbm, dy_hbm, idst_hbm, gatt_hbm, wg_hbm, wu_hbm, wd_hbm,
-           dx_hbm, dgate_ref, dwg_hbm, dwu_hbm, dwd_hbm, ja, jb, jc, ia, ib, ic,
+           dx_ref, dgate_ref, dwg_ref, dwu_ref, dwd_ref, ja, jb, jc, ia, ib, ic,
            gat, snd, rx, wgu, wdn, acc, hd, pbuf, slott, idst, gatt, mg, jm, mr, dgb, dgr, km, dgi, dgj, dgh, dgacc,
-           loc_sem, out_sem, meta_s, meta_r, g1_s, g1_r, g2_s, g2_r, fa_s, fa_r, fb_s, fb_r, fl, fm_s, fm_r,
+           loc_sem, meta_s, meta_r, g1_s, g1_r, g2_s, g2_r, fa_s, fa_r, fb_s, fb_r, fl, fm_s, fm_r,
            d2, c_sem, dm_s, dm_r, b_s, b_r, bl, bm_s, bm_r, credit, free):
     g = lax.axis_index('grp')
     l = lax.axis_index('loc')
@@ -276,7 +276,7 @@
         wait(three_lines, fm_r.at[0, r])
         for c, buf in enumerate(hop_bufs):
             axis = AXES[c][1]
-            dst = (rx.at[l, r, z, :, :, :, cols(c)], rx.at[l, r, :, :, x, :, cols(c)], rx.at[l, r, :, y, :, :, cols(c)])[c]
+            dst = (rx.at[r, z, :, :, :, cols(c)], rx.at[r, :, :, x, :, cols(c)], rx.at[r, :, y, :, :, cols(c)])[c]
             for k in (*NEAR, 0):
                 to = rmod(coord[axis] + k)
                 src = buf.at[r, :, :, to] if c == 2 else buf.at[r, :, to]
@@ -371,20 +371,24 @@
     def result(kk, n=first(D)):
         return gat.at[kk, first(CH), n]
 
+    def guest(r):
+        return ROUNDS + lax.rem(r, 2)
+
     def chunk(r, kk):
         lp = jnp.where(kk == 0, l, other)
+        slot = jnp.where(kk == 0, r, guest(r))
 
         def col(c0, w):
-            return rx[lp, r, :, :, :, :, pl.ds(c0, w)].reshape(CH, w)
+            return rx[slot, :, :, :, :, pl.ds(c0, w)].reshape(CH, w)
 
         for m in range(PLANE):
             zz, yy = m // SIDE, m % SIDE
             gcol = over_lanes(jnp.where(mine, mr[lp, r, zz, yy], 0.0))
-            rows = rx[lp, r, zz, yy, :, :, pl.ds(D, D)].reshape(LINE, D)
+            rows = rx[slot, zz, yy, :, :, pl.ds(D, D)].reshape(LINE, D)
             ubuf[pl.ds(m * LINE, LINE), :] = (gcol * rows.astype(F32)).astype(BF16)
         for h in range(2):
             hs = pl.ds(h * WIDE, WIDE)
-            ab = dot(rx[lp, r, pl.ds(2 * h, 2), :, :, :, first(D)].reshape(WIDE, D), wgu[...])
+            ab = dot(rx[slot, pl.ds(2 * h, 2), :, :, :, first(D)].reshape(WIDE, D), wgu[...])
             dh = dot(ubuf[hs, :], wdn[...], 1, 1)
             a = ab[:, :F]
             b = ab[:, F:]
@@ -415,7 +419,7 @@
             dst = snd.at[r, coord[axis], :, :, :, pl.ds(D + BWD[c][0], BWD[c][1])]
             for k in (*NEAR, 0):
                 to = rmod(coord[axis] + k)
-                src = (rx.at[l, r, to, :, :, :, cs], rx.at[l, r, :, :, to, :, cs], rx.at[l, r, :, to, :, :, cs])[c]
+                src = (rx.at[r, to, :, :, :, cs], rx.at[r, :, :, to, :, cs], rx.at[r, :, to, :, :, cs])[c]
                 if k:
                     remote(src, dst, b_s.at[0], b_r.at[0, r], along(axis, to)).start()
                     if c == 0:
@@ -481,17 +485,17 @@
             wait(blocks(3), fb_r.at[r])
         wait(blocks(1), fl.at[1, lax.rem(r, 2)])
         wait(three_lines, fm_r.at[1, r])
-        remote(rx.at[l, r], rx.at[l, r], d2.at[0], d2.at[1], loc=other).start()
+        remote(rx.at[r], rx.at[guest(r)], d2.at[0], d2.at[1], loc=other).start()
         remote(mr.at[l, r], mr.at[l, r], dm_s.at[0], dm_r.at[0], loc=other).start()
         move(r, start)
 
         def step(kk, carry2):
             @pl.when(kk == 1)
             def _():
-                wait(rx.at[l, r], d2.at[0])
+                wait(rx.at[r], d2.at[0])
                 pl.semaphore_signal(credit.at[0], inc=1, device_id={'grp': g, 'loc': other}, device_id_type=MESH)
                 with scope('wait_d2'):
-                    wait(rx.at[other, r], d2.at[1])
+                    wait(rx.at[r], d2.at[1])
                 wait(mr.at[other, r], dm_r.at[0])
                 move(r, mid)
 
@@ -502,8 +506,14 @@
         lax.fori_loop(0, 2, step, 0)
         with scope('credit'):
             pl.semaphore_wait(credit.at[0], 1)
-        rx[other, r, :, :, :, :, first(D)] = result(1)[...].reshape(SIDE, SIDE, SIDE, RS, D)
-        remote(rx.at[other, r, :, :, :, :, first(D)], rx.at[other, r, :, :, :, :, pl.ds(D, D)], c_sem.at[0], c_sem.at[1], loc=other).start()
+
+        @pl.when(r > 0)
+        def _():
+            wait(rx.at[r, :, :, :, :, first(D)], c_sem.at[0])
+
+        mine_there = rx.at[guest(r), :, :, :, :, first(D)]
+        mine_there[...] = result(1)[...].reshape(SIDE, SIDE, SIDE, RS, D)
+        remote(mine_there, rx.at[r, :, :, :, :, pl.ds(D, D)], c_sem.at[0], c_sem.at[1], loc=other).start()
         remote(dgb.at[1, r], dgr.at[r], dm_s.at[1], dm_r.at[1], loc=other).start()
 
         @pl.when(r < ROUNDS - 2)
@@ -516,13 +526,13 @@
             plane_hop(r + 4)
 
         with scope('wait_c'):
-            wait(rx.at[l, r, :, :, :, :, pl.ds(D, D)], c_sem.at[1])
+            wait(rx.at[r, :, :, :, :, pl.ds(D, D)], c_sem.at[1])
 
         def add(zy, carry2):
             zz, yy = zy // SIDE, rmod(zy)
             p0 = gat[0, pl.ds(zy * LINE, LINE), first(D)].astype(F32).reshape(SIDE, RS, D)
-            p1 = rx[l, r, zz, yy, :, :, pl.ds(D, D)].astype(F32)
-            rx[l, r, zz, yy, :, :, first(D)] = (p0 + p1).astype(BF16)
+            p1 = rx[r, zz, yy, :, :, pl.ds(D, D)].astype(F32)
+            rx[r, zz, yy, :, :, first(D)] = (p0 + p1).astype(BF16)
             return carry2
 
         with scope('add'):
@@ -537,15 +547,12 @@
     lax.fori_loop(0, ROUNDS, round_body, 0)
 
     with scope('flush'):
-        gat[3, first(F), pl.ds(D, D)] = acc[first(F), :].astype(BF16)
-        local(gat.at[3, first(F), pl.ds(D, D)], dwd_hbm, out_sem.at[0]).start()
+        dwd_ref[...] = acc[first(F), :].astype(BF16)
         eye = onehot(iota((F, F), 0) == iota((F, F), 1))
-        for i, out in enumerate((dwg_hbm, dwu_hbm)):
+        for i, out in enumerate((dwg_ref, dwu_ref)):
             for n in range(4):
-                block = acc[pl.ds((i + 1) * F, F), pl.ds(n * WIDE, WIDE)].astype(BF16)
-                stage = gat.at[1 + n // 3, pl.ds(n % 3 * WIDE, WIDE), pl.ds(i * F, F)]
-                stage[...] = dot(block, eye, 0, 0).astype(BF16)
-                local(stage, out.at[pl.ds(n * WIDE, WIDE), :], out_sem.at[1]).start()
+                ns = pl.ds(n * WIDE, WIDE)
+                out[ns, :] = dot(acc[pl.ds((i + 1) * F, F), ns].astype(BF16), eye, 0, 0).astype(BF16)
         dgacc[...] = jnp.zeros_like(dgacc)
         acc[first(TOK), :] = jnp.zeros((TOK, D), F32)
         slotn = slott[...].astype(BF16)
@@ -606,11 +613,9 @@
         for i in range(2):
             wait(snd.at[:, first(3), :, :, :, first(D)], b_s.at[i])
             wait(mg.at[:, first(3)], bm_s.at[i])
-        wait(rx.at[0, :, :, :, :, :, first(D)], c_sem.at[0])
+        wait(rx.at[0, :, :, :, :, first(D)], c_sem.at[0])
         wait(mr.at[0], dm_s.at[0])
         wait(dgr, dm_s.at[1])
-        wait(wdn, out_sem.at[0])
-        wait(wgu, out_sem.at[1])
     with scope('dg'):
         gate_gradients(ROUNDS - 1)
         for j in range(TOP_K):
@@ -621,24 +626,17 @@
     with scope('finish'):
         for n in range(4):
             ns = pl.ds(n * WIDE, WIDE)
-            gat[3, :, ns] = summed(ROUNDS - 1, ns).astype(BF16)
-            local(gat.at[3, :, ns], dx_hbm.at[:, ns], out_sem.at[2]).start()
+            dx_ref[:, ns] = summed(ROUNDS - 1, ns).astype(BF16)
         wait(dgh.at[:, first(3)], bm_s.at[2])
         wait(snd.at[:, first(3), :, :, :, first(D)], b_s.at[2])
-        wait(gat.at[3, :, first(D)], out_sem.at[2])
 
 
 def hand_over(*refs):
-    n = len(refs) // 4
-    ins, outs, bufs, sems = refs[:n], refs[n:2 * n], refs[2 * n:3 * n], refs[3 * n:]
-    loads = [pltpu.make_async_copy(a, b, sem.at[0]) for a, b, sem in zip(ins, bufs, sems)]
-    stores = [pltpu.make_async_copy(b, o, sem.at[1]) for b, o, sem in zip(bufs, outs, sems)]
-    for cp in loads:
+    n = len(refs) // 3
+    copies = [pltpu.make_async_copy(a, b, sem) for a, b, sem in zip(refs[:n], refs[n:2 * n], refs[2 * n:])]
+    for cp in copies:
         cp.start()
-    for load, store in zip(loads, stores):
-        load.wait()
-        store.start()
-    for cp in stores:
+    for cp in copies:
         cp.wait()
 
 
@@ -651,19 +649,19 @@
         dma = pltpu.SemaphoreType.DMA
         one, two, three, per_round = (dma((n,)) for n in (1, 2, 3, ROUNDS))
         sd = jax.ShapeDtypeStruct
+        results = [sd((TOK, D), BF16), sd((TOP_K, TOK), F32), *[sd((D, F), BF16)] * 2, sd((F, D), BF16)]
         cube = (ROUNDS, SIDE, SIDE, SIDE, RS)
         lines = (ROUNDS, SIDE, SIDE, 1, LANES)
         out = pl.pallas_call(
             kernel,
             name='moe_backward',
             in_specs=[any_] * 7,
-            out_specs=[any_, vmem] + [any_] * 9,
-            out_shape=[sd((TOK, D), BF16), sd((TOP_K, TOK), F32), *[sd((D, F), BF16)] * 2, sd((F, D), BF16),
-                       *[sd((*cube, w), BF16) for _, w in FWD + BWD]],
+            out_specs=[vmem] * 5 + [any_] * 6,
+            out_shape=[*[pltpu.VMEM(o.shape, o.dtype) for o in results], *[sd((*cube, w), BF16) for _, w in FWD + BWD]],
             scratch_shapes=[
                 pltpu.VMEM((SIDE, TOK, 2 * D), BF16),
                 pltpu.VMEM((*cube, 2 * D), BF16),
-                pltpu.VMEM((2, *cube, 2 * D), BF16),
+                pltpu.VMEM((ROUNDS + 2, SIDE, SIDE, SIDE, RS, 2 * D), BF16),
                 pltpu.VMEM((D, 2 * F), BF16),
                 pltpu.VMEM((F, D), BF16),
                 pltpu.VMEM((3 * F, D), F32),
@@ -682,20 +680,21 @@
                 pltpu.VMEM((ROUNDS, PLANE, LANES), F32),
                 pltpu.VMEM((ROUNDS, SIDE, PLANE, LANES), F32),
                 pltpu.VMEM((2, GROUPS, TOK), F32),
-                dma((5,)), three, two, two, one, dma((2, 2)), one, two, two, per_round, one, per_round, dma((2, 2)), three,
+                dma((5,)), two, two, one, dma((2, 2)), one, two, two, per_round, one, per_round, dma((2, 2)), three,
                 dma((2, ROUNDS)), *[two] * 4, three, dma((3, ROUNDS)), dma((2, ROUNDS)), three, dma((3, ROUNDS)),
                 pltpu.SemaphoreType.REGULAR((1,)), pltpu.SemaphoreType.REGULAR((ROUNDS,)),
             ],
-            compiler_params=pltpu.CompilerParams(collective_id=0, has_side_effects=True, vmem_limit_bytes=67043328),
+            compiler_params=pltpu.CompilerParams(collective_id=0, has_side_effects=True, vmem_limit_bytes=60 << 20),
         )(x_rows, dy_rows, expert_ids.T, gate_vals.T, w_gate[0], w_up[0], w_down[0])
         dx, d_gates, dwg, dwu, dwd = pl.pallas_call(
             hand_over,
             name='hand_over',
-            in_specs=[any_] * 5,
+            in_specs=[vmem] * 5,
             out_specs=[any_] * 5,
-            out_shape=[sd(o.shape, o.dtype) for o in out[:5]],
-            scratch_shapes=[pltpu.VMEM(o.shape, o.dtype) for o in out[:5]] + [dma((2,))] * 5,
-        )(*out[:5])
+            out_shape=results,
+            scratch_shapes=[pltpu.SemaphoreType.DMA] * 5,
+            compiler_params=pltpu.CompilerParams(vmem_limit_bytes=1 << 20),
+        )(*[pltpu.with_memory_space_constraint(o, pltpu.VMEM) for o in out[:5]])
         return dx, d_gates.T, dwg[None], dwu[None], dwd[None]
 
     return jax.shard_map(device_step, mesh=mesh, in_specs=(spec,) * 7, out_specs=(spec,) * 5, check_vma=False)

time: 214 us -> 210 us (0.981)
  Pallas kernels: 213 us -> 210 us
where the time goes in v7:
time: 210 us
  Pallas kernels  210 us (100%)
    pallas_call x1, Pallas kernels, device_step(): pl.pallas_call(kernel, name='moe_backward', in_specs=[any_] * 7, out_spec...  208 us

profile of v7, /device:TPU:0, one launch (start us, length us, event | category | flops | bytes accessed | tf_op | source)
XLA Modules:
  0.0 210.3 jit_solution(2248861355847119435)
XLA Ops:
  0.6 207.7 %moe_backward.1 = (bf16[768,1024]{1,0:T(8,128)(2,1)S(1)}, f32[8,768]{1,0:T(8,128)S(1)}, bf16[1024,384]{1,0:T(8,128)(2,1)S(1)}, bf16[1024,384]{1,0:T(8,128)(2,1)S...) custom-call(bf16[768,1024]{1,0:T(8,128)(2,1)} %x_hbm.1, ...), custom_call_target="tpu_custom_call" | custom-call | tf_op jit(solution)/shard_map/moe_backward/pallas_call | solution.py:655
  208.4 2.0 hand_over.1

commit v8 on v7

--- a/solution.py
+++ b/solution.py
@@ -65,7 +65,9 @@
            d2, c_sem, dm_s, dm_r, b_s, b_r, bl, bm_s, bm_r, credit, free):
     g = lax.axis_index('grp')
     l = lax.axis_index('loc')
-    z, y, x = g // PLANE, (g // SIDE) % SIDE, g % SIDE
+    cz, cy, cx = g // PLANE, (g // SIDE) % SIDE, g % SIDE
+    x, y, z = cx + l * (cz - cx), cy + l * (cx - cy), cz + l * (cy - cz)
+    step_x, step_y, step_z = 1 + l * (PLANE - 1), SIDE + l * (1 - SIDE), PLANE + l * (SIDE - PLANE)
     coord = (x, y, z)
     other = 1 - l
 
@@ -73,7 +75,7 @@
         return lax.rem(v, SIDE)
 
     def gid(zz, yy, xx):
-        return zz * PLANE + yy * SIDE + xx
+        return zz * step_z + yy * step_y + xx * step_x
 
     def along(axis, k):
         return gid(*(k if a == axis else coord[a] for a in (2, 1, 0)))
@@ -192,7 +194,7 @@
 
     def home_gid():
         v = iota((GROUPS, 1), 0)
-        return lax.rem(v, PLANE) * SIDE + v // PLANE
+        return gid(lax.rem(v, PLANE) // SIDE, rmod(v), v // PLANE)
 
     with scope('home_table'):
         carry = jnp.zeros((GROUPS, 1), F32)
@@ -292,10 +294,17 @@
         for p in neighbours:
             pl.semaphore_signal(free.at[r], inc=1, device_id={'grp': p, 'loc': l}, device_id_type=MESH)
 
+    def own_part(r, early):
+        for c, core in ((2, 0), (0, 1)):
+            @pl.when(l == (core if early else 1 - core))
+            def _():
+                hop_part(r, c, coord[c])
+        if not early:
+            hop_part(r, 1, y)
+
     def before_near():
         for r in range(2):
-            for c in (0, 2):
-                hop_part(r, c, coord[c])
+            own_part(r, early=True)
 
         for sem in (meta_r, meta_s):
             wait(idst.at[:, first(3)], sem.at[0])
@@ -319,7 +328,7 @@
                 wait(half_slab, g1_r.at[d, 1 - d])
 
     def before_second_near():
-        hop_part(0, 1, y)
+        own_part(0, early=False)
         for c in range(3):
             for k in BOTH:
                 hop_part(0, c, rmod(coord[c] + k))
@@ -333,7 +342,7 @@
         for c in range(3):
             hop_part(0, c, rmod(coord[c] + 2))
         hop_rest(0)
-        hop_part(1, 1, y)
+        own_part(1, early=False)
         for k in NEAR:
             for c in range(3):
                 hop_part(1, c, rmod(coord[c] + k))
@@ -556,8 +565,8 @@
         dgacc[...] = jnp.zeros_like(dgacc)
         acc[first(TOK), :] = jnp.zeros((TOK, D), F32)
         slotn = slott[...].astype(BF16)
-        glane = iota((GROUPS, GROUPS * RS), 1) // RS
-        spread = onehot(home_gid() == glane)
+        at = iota((1, GROUPS * RS), 1) // RS
+        spread = onehot(home_gid() == gid(at // PLANE, rmod(at // SIDE), rmod(at)))
     def pick(r):
         want = (lax.rem(iota((1, GROUPS * RS), 1), RS) + r * RS).astype(F32)
         for n in range(2):

time: 210 us -> 210 us (level)
  no operation moved by 1% of the time
where the time goes in v8:
time: 210 us
  Pallas kernels  209 us (100%)
    pallas_call x1, Pallas kernels, device_step(): pl.pallas_call(kernel, name='moe_backward', in_specs=[any_] * 7, out_spec...  207 us

profile of v8, /device:TPU:0, one launch (start us, length us, event | category | flops | bytes accessed | tf_op | source)
XLA Modules:
  0.0 209.7 jit_solution(6241319077960980695)
XLA Ops:
  0.6 207.1 %moe_backward.1 = (bf16[768,1024]{1,0:T(8,128)(2,1)S(1)}, f32[8,768]{1,0:T(8,128)S(1)}, bf16[1024,384]{1,0:T(8,128)(2,1)S(1)}, bf16[1024,384]{1,0:T(8,128)(2,1)S...) custom-call(bf16[768,1024]{1,0:T(8,128)(2,1)} %x_hbm.1, ...), custom_call_target="tpu_custom_call" | custom-call | tf_op jit(solution)/shard_map/moe_backward/pallas_call | solution.py:664
  207.7 2.0 hand_over.1

commit v9 on v8

--- a/solution.py
+++ b/solution.py
@@ -453,13 +453,13 @@
                     if c == 0:
                         remote(km.at[r, :, to], dgi.at[r, :, y], bm_s.at[1], bm_r.at[1, r], along(axis, to)).start()
                 else:
-                    local(src, dst, bl.at[0, r]).start()
+                    local(src, dst, bl.at[0, lax.rem(r, 3)]).start()
         dgi[r, :, y] = km[r, :, y]
 
     def home_third(r):
         with scope('wait_bb'):
             wait(blocks(3, D), b_r.at[1, r])
-        wait(blocks(1, D), bl.at[0, r])
+        wait(blocks(1, D), bl.at[0, lax.rem(r, 3)])
         wait(three_lines, bm_r.at[1, r])
         for p in range(PLANE):
             dgj[r, pl.ds(p, 1), :] = dgi[r, p // SIDE, p % SIDE]
@@ -474,7 +474,7 @@
                         remote(dgj.at[r], dgh.at[r, x], bm_s.at[2], bm_r.at[2, r], along(c, to)).start()
                     remote(src, dst, b_s.at[2], b_r.at[2, r], along(c, to)).start()
                 else:
-                    local(src, dst, bl.at[1, r]).start()
+                    local(src, dst, bl.at[1, lax.rem(r, 3)]).start()
         dgh[r, x] = dgj[r]
 
     start, mid, end = range(3)
@@ -589,7 +589,7 @@
     def arrived(r):
         with scope('wait_bc'):
             wait(blocks(3, D), b_r.at[2, r])
-        wait(blocks(1, D), bl.at[1, r])
+        wait(blocks(1, D), bl.at[1, lax.rem(r, 3)])
 
     def summed(r, ns):
         return acc[first(TOK), ns] + dot(gat[0, :, first(GROUPS * RS)], snd[r, :, :, :, :, ns].reshape(GROUPS * RS, WIDE))
@@ -690,7 +690,7 @@
                 pltpu.VMEM((ROUNDS, SIDE, PLANE, LANES), F32),
                 pltpu.VMEM((2, GROUPS, TOK), F32),
                 dma((5,)), two, two, one, dma((2, 2)), one, two, two, per_round, one, per_round, dma((2, 2)), three,
-                dma((2, ROUNDS)), *[two] * 4, three, dma((3, ROUNDS)), dma((2, ROUNDS)), three, dma((3, ROUNDS)),
+                dma((2, ROUNDS)), *[two] * 4, three, dma((3, ROUNDS)), dma((2, 3)), three, dma((3, ROUNDS)),
                 pltpu.SemaphoreType.REGULAR((1,)), pltpu.SemaphoreType.REGULAR((ROUNDS,)),
             ],
             compiler_params=pltpu.CompilerParams(collective_id=0, has_side_effects=True, vmem_limit_bytes=60 << 20),

time: 210 us -> 210 us (level)
  no operation moved by 1% of the time
where the time goes in v9:
time: 210 us
  Pallas kernels  209 us (100%)
    pallas_call x1, Pallas kernels, device_step(): pl.pallas_call(kernel, name='moe_backward', in_specs=[any_] * 7, out_spec...  207 us

profile of v9, /device:TPU:0, one launch (start us, length us, event | category | flops | bytes accessed | tf_op | source)
XLA Modules:
  0.0 209.6 jit_solution(2877599337441715123)
XLA Ops:
  0.6 207.0 %moe_backward.1 = (bf16[768,1024]{1,0:T(8,128)(2,1)S(1)}, f32[8,768]{1,0:T(8,128)S(1)}, bf16[1024,384]{1,0:T(8,128)(2,1)S(1)}, bf16[1024,384]{1,0:T(8,128)(2,1)S...) custom-call(bf16[768,1024]{1,0:T(8,128)(2,1)} %x_hbm.1, ...), custom_call_target="tpu_custom_call" | custom-call | tf_op jit(solution)/shard_map/moe_backward/pallas_call | solution.py:664
  207.7 2.0 hand_over.1
